TPU v7x, 1024 devices: a whole 4x8x16 slice. The times are simulated.
1024 devices in a mesh: dp: 64 (over y_lo, z), tp: 16 (over x, y_hi, core).
Axes of the slice: x: 4, y: 8 (y_hi: 2, y_lo: 4; y = y_hi * 4 + y_lo), z: 16, core: 2. Of those that a mesh axis runs over, the one named last changes fastest.
Arguments:
- queries: bfloat16 [16384, 4096], P('dp', 'tp'), may hold values from -6 to 6
- keys: bfloat16 [16384, 512], P(('dp', 'tp')), may hold values from -6 to 6
- values: bfloat16 [16384, 512], P(('dp', 'tp')), may hold values from -6 to 6
- out_weight: bfloat16 [4096, 8192], P('tp', 'dp'), may hold values from -0.09375 to 0.09375
- residual: bfloat16 [16384, 8192], P(('dp', 'tp')), may hold values from -40 to 40
- norm_gain: float32 [8192], replicated, may hold values from 0.5 to 1.5
Outputs:
- hidden_out: bfloat16 [16384, 8192], P(('dp', 'tp'))
- normed: bfloat16 [16384, 8192], P(('dp', 'tp'))
All inputs are finite; a program needn't handle non-finite values.
Results may differ from a plain program's by a relative error of at most 0.012.
Values may be sent and summed in bfloat16 or wider, within the bound.
A program may use at most 32 MiB of HBM per device.

v0:
```python
import math

import jax
import jax.numpy as jnp
from jax import lax
from jax.sharding import Mesh
from jax.sharding import PartitionSpec as P

KVH = 4
HDIM = 128
LEN = 32
DP = ("dp_0", "dp_1")
DP_TP = ("dp_0", "dp_1", "tp")


def in_one_piece(arrays, axis, dim, along):
    ends, at = ([], 0)
    for a in arrays[:-1]:
        at += a.shape[along]
        ends.append(at)
    both = jnp.concatenate(arrays, axis=along)
    return tuple(jnp.split(lax.all_gather(both, axis, axis=dim, tiled=True), ends, axis=along))


def in_order(pieces, dim):
    pieces = jnp.moveaxis(pieces, 0, dim)
    dims = pieces.shape
    return pieces.reshape(*dims[:dim], dims[dim] * dims[dim + 1], *dims[dim + 2 :])


def stacked_from(value, axes, sequence):
    pieces = value[None]
    for k in sequence:
        pieces = lax.all_gather(pieces, axes[k], axis=0, tiled=True)
    held = [lax.axis_size(axes[k]) for k in reversed(sequence)]
    pieces = pieces.reshape(*held, *value.shape)
    turned = sorted(range(len(sequence)), key=lambda place: sequence[len(sequence) - 1 - place])
    return pieces.transpose(*turned, *range(len(sequence), pieces.ndim)).reshape(-1, *value.shape)


def gather_axes(value, axes, sequence, dim):
    return in_order(stacked_from(value, axes, sequence), dim)


def attention(queries, key_head, value_head):
    rows = queries.shape[0]
    sequences = rows // LEN
    local_heads = queries.shape[1] // HDIM
    query_heads = queries.reshape(sequences, LEN, local_heads, HDIM)
    key_rows = key_head.reshape(sequences, LEN, HDIM)
    value_rows = value_head.reshape(sequences, LEN, HDIM)
    scores = jnp.einsum(
        "slhd,smd->shlm", query_heads, key_rows, preferred_element_type=jnp.float32
    ) / math.sqrt(HDIM)
    causal = jnp.arange(LEN)[:, None] >= jnp.arange(LEN)[None, :]
    scores = jnp.where(causal, scores, -1e30)
    highest = jnp.max(scores, axis=-1, keepdims=True)
    powers = jnp.exp(scores - highest)
    weights = (powers / jnp.sum(powers, axis=-1, keepdims=True)).astype(jnp.bfloat16)
    attended = jnp.einsum("shlm,smd->slhd", weights, value_rows, preferred_element_type=jnp.float32)
    return attended.astype(jnp.bfloat16).reshape(rows, local_heads * HDIM)


def local(queries, keys, values, out_weight, residual, norm_gain):
    tp_size = lax.axis_size("tp")
    position = lax.axis_index("tp")
    gathered_keys, gathered_values = in_one_piece((keys, values), "tp", 0, 1)
    head = position * KVH // tp_size
    key_head = lax.dynamic_slice_in_dim(gathered_keys, head * HDIM, HDIM, 1)
    value_head = lax.dynamic_slice_in_dim(gathered_values, head * HDIM, HDIM, 1)
    attended = attention(queries, key_head, value_head)
    whole_weight = gather_axes(out_weight, DP, (0, 1), 1)
    projected = lax.psum_scatter(
        jnp.dot(attended, whole_weight, preferred_element_type=jnp.float32).astype(jnp.bfloat16),
        "tp",
        scatter_dimension=0,
        tiled=True,
    ).astype(jnp.float32)
    updated = residual.astype(jnp.float32) + projected
    hidden_out = updated.astype(jnp.bfloat16)
    meansq = jnp.mean(updated * updated, axis=-1, keepdims=True)
    normed = (updated * lax.rsqrt(meansq + 1e-05) * norm_gain).astype(jnp.bfloat16)
    return (hidden_out, normed)


def solution(mesh):
    finer = Mesh(mesh.devices.reshape(4, 16, mesh.shape["tp"]), ("dp_0", "dp_1", "tp"))
    in_specs = (P(DP, "tp"), P(DP_TP, None), P(DP_TP, None), P("tp", DP), P(DP_TP, None), P())
    out_specs = (P(DP_TP, None), P(DP_TP, None))
    return jax.shard_map(local, mesh=finer, in_specs=in_specs, out_specs=out_specs, check_vma=False)
```

profile of v0, /device:TPU:1, one launch (start us, length us, event | category | flops | bytes accessed | tf_op | source)
XLA Modules:
  0.0 261.7 jit_solution(12991915781458646047)
XLA Ops:
  7.2 0.0 all-gather.3.cloned.1.call-start
  7.2 14.3 %all-gather = bf16[1024,128]{1,0:T(8,128)(2,1)} all-gather(bf16[256,128]{1,0:T(8,128)(2,1)} %param.9), channel_id=2, replica_groups=mesh['dp_0'=4,'dp_1'=16,'tp'=16] {'dp_0'}, dimensions={0}, use_global_device_ids=true | all-gather | bytes 327680 | tf_op jit(solution)/shard_map/all_gather | solution.py:34
  21.5 0.0 all-gather.3.cloned.1.call-update
  21.5 0.0 reduce-scatter.2.cloned.1.call-start
  21.6 0.9 reshape.38
  22.6 0.7 pad_maximum_fusion
  23.3 41.2 %all_gather.9 = bf16[256,1024]{1,0:T(8,128)(2,1)S(1)} all-gather(bf16[16,1024]{1,0:T(8,128)(2,1)S(1)} %pad_maximum_fusion), channel_id=1, replica_groups=mesh['dp_0'=4,'dp_1'=16,'tp'=16] {'tp'}, dimensions={0}, use_global_device_ids=true | all-gather | bytes 557056 | tf_op jit(solution)/shard_map/all_gather | solution.py:22
  64.6 0.4 fusion.17
  65.0 0.3 fusion.3
  65.3 0.3 fusion.5
  65.5 0.1 copy.21
  65.7 37.7 %all-gather.3.cloned.1.call-done = bf16[64,256,128]{2,1,0:T(8,128)(2,1)} async-done(((bf16[4,256,128]{2,1,0:T(8,128)(2,1)}), bf16[64,256,128]{2,1,0:T(8,128)(2,1)}) %all-gather.3.cloned.1.call-update) | async-done | bytes 4194320 | tf_op jit(solution)/shard_map/all_gather | solution.py:34
  103.3 4.7 %copy.22 = bf16[4,16,256,128]{3,2,1,0:T(8,128)(2,1)} copy(bf16[4,16,256,128]{3,2,0,1:T(8,128)(2,1)} %bitcast.40) | data formatting | bytes 8388608 | tf_op jit(solution)/shard_map/transpose | solution.py:38
  108.0 6.4 %copy.23 = bf16[256,64,128]{0,2,1:T(8,128)(2,1)} copy(bf16[256,64,128]{2,0,1:T(8,128)(2,1)} %bitcast.39) | data formatting | bytes 8388608 | tf_op jit(solution)/shard_map/transpose | solution.py:26
  114.4 5.4 %convolution_convert_fusion = bf16[256,8192]{1,0:T(8,128)(2,1)} fusion(bf16[256,8192]{0,1:T(8,128)(2,1)} %bitcast.38, bf16[32,8,2,128]{3,2,1,0:T(2,128)(2,1)S(1)} %bitcast.42), kind=kOutput, calls=%fused_computation.1 | convolution fusion | flops 1075838976 | bytes 8519680 | tf_op jit(solution)/shard_map/dot_general | solution.py:74
  119.8 0.0 copy-start
  119.8 0.0 copy-start.1
  119.8 0.0 reduce-scatter.2.cloned.1.call-update
  119.9 132.0 %reduce-scatter.2.cloned.1.call-done = bf16[16,8192]{1,0:T(8,128)(2,1)} async-done(((bf16[256,8192]{1,0:T(8,128)(2,1)}), bf16[16,8192]{1,0:T(8,128)(2,1)}) %reduce-scatter.2.cloned.1.call-update) | async-done | bytes 262160 | tf_op jit(solution)/shard_map/reduce_scatter | solution.py:73
  251.9 0.0 copy-done
  251.9 1.1 multiply_reduce_fusion
  253.0 0.0 copy-done.1
  253.0 1.8 multiply_convert_fusion
  (4 shorter events, 0.1 us)
Async XLA Ops:
  7.2 96.2 %all-gather.3.cloned.1.call-start = ((), (), s32[]{:S(2)}) async-start(), calls=%async_computation.1 | async-start | bytes 4456448 | tf_op jit(solution)/shard_map/all_gather | solution.py:34
  21.5 230.3 %reduce-scatter.2.cloned.1.call-start = ((), (), s32[]{:S(2)}) async-start(), calls=%async_computation.2 | async-start | bytes 4456448 | tf_op jit(solution)/shard_map/reduce_scatter | solution.py:73
  119.8 132.0 %copy-start = (bf16[16,8192]{1,0:T(8,128)(2,1)S(1)}, bf16[16,8192]{1,0:T(8,128)(2,1)}, u32[]{:S(2)}) copy-start(bf16[16,8192]{1,0:T(8,128)(2,1)} %param.10) | copy-start | bytes 786436
  119.8 133.2 %copy-start.1 = (f32[8192]{0:T(1024)S(1)}, f32[8192]{0:T(1024)}, u32[]{:S(2)}) copy-start(f32[8192]{0:T(1024)} %param.11) | copy-start | bytes 98308
Sparse Core Ops, SparseCore 0:
  21.6 81.6 all-gather.2
  120.0 131.8 reduce-scatter.1
where the time goes:
time: 262 us
  waiting for transfers between devices  170 us (65%)
  blocking collectives  55.5 us (21%)
  between operations  14.1 us (5%)
  local copies, waits for them, and re-layouts  12.2 us (5%)
  matrix products  6.39 us (2%)
  other arithmetic  3.72 us (1%)
    reduce_scatter x1, waiting for transfers between devices, local(): lax.psum_scatter(jnp.dot(attended, whole_weight, preferred_element_type=j...  132 us
    all_gather x1, blocking collectives, in_one_piece(): lax.all_gather(both, axis, axis=dim, tiled=True)  41.2 us
    all_gather x1, waiting for transfers between devices, stacked_from(): pieces = lax.all_gather(pieces, axes[k], axis=0, tiled=True)  37.7 us
    all_gather x1, blocking collectives, stacked_from(): pieces = lax.all_gather(pieces, axes[k], axis=0, tiled=True)  14.3 us
    transpose x1, local copies, waits for them, and re-layouts, in_order(): pieces = jnp.moveaxis(pieces, 0, dim)  6.39 us
    dot_general x1, matrix products, local(): jnp.dot(attended, whole_weight, preferred_element_type=jnp.float32)  5.45 us
  transfers between devices with their start and end apart: 2, of which 2 were waited for; matrix products, arithmetic and copies ran while one was open for 1% of the time, Pallas kernels for 0%

commit v1 on v0

v1 whole, which is shorter than its diff:
```python
import functools
import math

import jax
import jax.numpy as jnp
from jax import lax
from jax.experimental import pallas as pl
from jax.experimental.pallas import tpu as pltpu
from jax.sharding import Mesh
from jax.sharding import PartitionSpec as P

MESH = pl.DeviceIdType.MESH
F32, BF16 = jnp.float32, jnp.bfloat16

ORDER = (0, 1, -1, 3, -3, 2, -2, 4, -4, 6, -6, 5, -5, 7, -7, 8)
SLOT = {d: i for i, d in enumerate(ORDER)}
PIECES = 4
NT = (((1,), (1,)), ((), ()))


def kernel(
    q, k, v, w, res, gain, hid, nrm,
    qall, kvl, kvr, kvp, wv, wcross, wall, bias, att, psend, xr, ssend, rbuf, u, resv, gv, hidv, nrmv,
    lsem, ssem, qsem, qdsem, ksem, kxsem, kdsem, wsem, wcsem, wdsem, xsem, asem,
):
    yl, z, x, yh, c = (lax.axis_index(a) for a in ("yl", "z", "x", "yh", "c"))
    y = yh * 4 + yl
    sends = []

    def dev(dy=0, dz=0, dx=0, flip=False):
        yt = lax.rem(y + (dy + 8), 8)
        return (
            lax.rem(yt, 4),
            lax.rem(z + (dz + 16), 16),
            lax.rem(x + dx, 4),
            lax.div(yt, 4),
            1 - c if flip else c,
        )

    def remote(src, dst, send_sem, recv_sem, to):
        return pltpu.make_async_remote_copy(
            src_ref=src, dst_ref=dst, send_sem=send_sem, recv_sem=recv_sem, device_id=to, device_id_type=MESH
        )

    def send(src, dst, recv_sem, to):
        copy = remote(src, dst, ssem.at[len(sends)], recv_sem, to)
        copy.start()
        sends.append(copy)

    def received(dst, recv_sem):
        remote(dst, dst, ssem.at[0], recv_sem, dev(flip=True)).wait_recv()

    def halfway(gs, h):
        first = lax.div(yl + gs, 4)
        return 1 - first if h else first

    def keeper(gs):
        return jnp.where(lax.rem(yh + halfway(gs, 0), 2) == c, 0, 1)

    local = [
        pltpu.make_async_copy(w, wv, lsem.at[0]),
        pltpu.make_async_copy(k, kvl.at[0], lsem.at[1]),
        pltpu.make_async_copy(v, kvl.at[1], lsem.at[2]),
        pltpu.make_async_copy(q.at[:, c], qall.at[0, 0, 0], lsem.at[3]),
        pltpu.make_async_copy(res, resv, lsem.at[4]),
        pltpu.make_async_copy(gain, gv, lsem.at[5]),
    ]
    for copy in local:
        copy.start()
    peers = [dev(flip=True), dev(dy=1), dev(dy=-1), dev(dy=4)]
    peers += [dev(dz=d) for d in (1, -1, 2, -2, 3, -3)]
    peers += [dev(dx=d) for d in (1, 2, 3)]
    barrier = pltpu.get_barrier_semaphore()
    for peer in peers:
        pl.semaphore_signal(barrier, inc=1, device_id=peer, device_id_type=MESH)

    row = lax.broadcasted_iota(jnp.int32, (128, 128), 0)
    col = lax.broadcasted_iota(jnp.int32, (128, 128), 1)
    half = jnp.where(col < 64, c, 1 - c)
    place = half * 16 + lax.rem(col, 16)
    same = lax.div(row, 32) == lax.div(lax.rem(col, 64), 16)
    bias[...] = jnp.where(same & (place <= lax.rem(row, 32)), 0.0, -1e30)

    local[0].wait()
    turned = wv[...].astype(F32).T.astype(BF16)
    top, bottom = turned[:64], turned[64:]
    wall[0, 0, 0] = jnp.where(yh == 0, top, bottom)
    wcross[...] = jnp.where(yh == 0, bottom, top)
    local[1].wait()
    local[2].wait()
    kvr[0, 0, x] = kvl[:, :, pl.ds(pl.multiple_of(x * 128, 128), 128)]
    local[3].wait()

    pl.semaphore_wait(barrier, len(peers))

    def wsend(wk, source, hop):
        dst = SLOT[source - hop if source - hop != -8 else 8]
        send(wall.at[SLOT[source], wk, 0], wall.at[dst, wk, 0], wsem.at[dst, wk], dev(dz=hop))

    def worigin(wk):
        for hop in (3, -3, 1, -1):
            wsend(wk, 0, hop)

    def wgot(d, wk):
        received(wall.at[SLOT[d], wk, 0], wsem.at[SLOT[d], wk])

    def wrelay(wk, d):
        wgot(d, wk)
        sign = 1 if d < 0 else -1
        if abs(d) == 3:
            for hop in (3 * sign, sign, -sign):
                wsend(wk, d, hop)
        else:
            if (d < 0) == (wk == 0):
                wsend(wk, d, 2 * sign)
            for hop in (sign, -sign):
                wsend(wk, d, hop)

    def wpass(p, wk):
        send(
            wall.at[pl.ds(4 * p, 4), wk, 0], wall.at[pl.ds(4 * p, 4), wk, 1], wdsem.at[p, wk], dev(flip=True)
        )

    def wpassed(p, wk):
        received(wall.at[pl.ds(4 * p, 4), wk, 1], wdsem.at[p, wk])

    def place_of(r):
        return (r, 0) if r >= 0 else (r + 4, 1)

    def qsend(r, s, hop):
        gs, h = place_of(r)
        gt, ht = place_of(r - hop if r - hop != 4 else -4)
        send(qall.at[gs, h, s], qall.at[gt, ht, s], qsem.at[gt, ht, s], dev(dy=hop))

    def qgot(r, s):
        gs, h = place_of(r)
        received(qall.at[gs, h, s], qsem.at[gs, h, s])

    def qrelay(r, s):
        qgot(r, s)
        if abs(r) < 3 or s == (0 if r < 0 else 1):
            qsend(r, s, 1 if r < 0 else -1)

    def ksend(r, hop):
        gs, h = place_of(r)
        gt, ht = place_of(r - hop if r - hop != 4 else -4)
        if (gt, ht) == (0, 1):
            part = 0 if hop > 0 else 1
            rows = pl.ds(2 * part, 2)
            send(kvr.at[gs, h, rows], kvr.at[gt, ht, rows], ksem.at[gt, ht, part], dev(dy=hop))
        else:
            send(kvr.at[gs, h], kvr.at[gt, ht], ksem.at[gt, ht, 0], dev(dy=hop))

    def kgot(r):
        gs, h = place_of(r)
        if r == -4:
            for part in range(2):
                received(kvr.at[gs, h, pl.ds(2 * part, 2)], ksem.at[gs, h, part])
        else:
            received(kvr.at[gs, h], ksem.at[gs, h, 0])

    def krelay(r):
        kgot(r)
        ksend(r, 1 if r < 0 else -1)

    def kpass(gs):
        send(kvr.at[gs, 1 - keeper(gs)], kvp.at[gs], kdsem.at[gs], dev(flip=True))

    def kpassed(gs):
        received(kvp.at[gs], kdsem.at[gs])

    def attend(gs, h):
        kept = kvr[gs, keeper(gs)]
        passed = kvp[gs]
        keys = jnp.concatenate([kept[:, 0].reshape(64, 128), passed[:, 0].reshape(64, 128)], axis=0)
        values = jnp.concatenate([kept[:, 1].reshape(64, 128), passed[:, 1].reshape(64, 128)], axis=0)
        for s in range(2):
            for j in range(2):
                lanes = slice(j * 128, j * 128 + 128)
                queries = qall[gs, h, s, :, :, lanes].reshape(128, 128)
                scores = lax.dot_general(queries, keys, NT, preferred_element_type=F32)
                scores = scores * (1.0 / math.sqrt(128.0)) + bias[...]
                powers = jnp.exp(scores - jnp.max(scores, axis=-1, keepdims=True))
                weights = powers * (1.0 / jnp.sum(powers, axis=-1, keepdims=True))
                heads = jnp.dot(weights.astype(BF16), values, preferred_element_type=F32)
                att[gs, h, s, :, lanes] = heads.astype(BF16)

    def piece(gs, p):
        total = None
        for h in range(2):
            wk = halfway(gs, h)
            for s in range(2):
                rows = wall[pl.ds(4 * p, 4), wk, s].reshape(256, 256)
                term = lax.dot_general(att[gs, h, s], rows, NT, preferred_element_type=F32)
                total = term if total is None else total + term
        psend[gs, p] = total.astype(BF16).reshape(4, 32, 256)
        for d in (2, 1, 3):
            send(psend.at[gs, p, lax.rem(x + d, 4)], xr.at[gs, p, d - 1], xsem.at[gs, p, d - 1], dev(dx=d))

    pending = []

    def reduced(gs, p):
        total = psend[gs, p, x].astype(F32)
        for d in range(3):
            received(xr.at[gs, p, d], xsem.at[gs, p, d])
            total = total + xr[gs, p, d].astype(F32)
        ssend[gs, p] = total.astype(BF16).reshape(2, 16, 256)
        home = (lax.rem(yl + gs, 4), z, x, c)
        send(ssend.at[gs, p, 1 - c], rbuf.at[y, p], asem.at[y, p], home + (1 - c,))
        if gs:
            send(ssend.at[gs, p, c], rbuf.at[y, p], asem.at[y, p], home + (c,))
        else:
            copy = remote(ssend.at[0, p, c], rbuf.at[y, p], ssem.at[len(sends)], asem.at[y, p], home + (c,))
            sends.append(None)
            pending.append(copy)

            @pl.when(yh != c)
            def _():
                copy.start()

            @pl.when(yh == c)
            def _():
                rbuf[y, p] = ssend[0, p, c]

    squares = [jnp.zeros((16, 128), F32)]

    def finish(p):
        for source in range(8):

            @pl.when((y != source) | (yh != c))
            def _(source=source):
                received(rbuf.at[source, p], asem.at[source, p])

        low = lax.broadcasted_iota(jnp.int32, (16, 128), 1) < 64
        for part in range(4):
            for t in range(2):
                lanes = slice(t * 128, t * 128 + 128)
                a = rbuf[part, p, :, lanes].astype(F32)
                b = rbuf[4 + part, p, :, lanes].astype(F32)
                pair = (
                    jnp.where(low, a, pltpu.roll(b, 64, 1)),
                    jnp.where(low, pltpu.roll(a, 64, 1), b),
                )
                for i in range(2):
                    block = part * 16 + lax.rem(z + (ORDER[4 * p + 2 * t + i] + 16), 16)
                    at = pl.ds(pl.multiple_of(block * 128, 128), 128)
                    updated = resv[:, at].astype(F32) + pair[i]
                    u[:, at] = updated
                    hidv[:, at] = updated.astype(BF16)
                    squares[0] = squares[0] + updated * updated

    worigin(0)
    send(wcross, wall.at[0, 1, 0], wcsem.at[0], dev(dy=4))
    for d in (2, 1, 3):
        head = pl.ds(pl.multiple_of(lax.rem(x + d, 4) * 128, 128), 128)
        send(kvl.at[:, :, head], kvr.at[0, 0, x], kxsem.at[d - 1], dev(dx=d))
    send(q.at[:, 1 - c], qall.at[0, 0, 1], qdsem.at[0], dev(flip=True))
    qsend(0, 0, 1)
    qsend(0, 0, -1)
    received(qall.at[0, 0, 1], qdsem.at[0])
    qsend(0, 1, 1)
    qsend(0, 1, -1)
    qrelay(-1, 0)
    qrelay(1, 0)
    wrelay(0, -3)
    wrelay(0, 3)
    for d in range(1, 4):
        received(kvr.at[0, 0, lax.rem(x + (4 - d), 4)], kxsem.at[d - 1])
    ksend(0, 1)
    ksend(0, -1)
    qrelay(-1, 1)
    qrelay(1, 1)
    received(wall.at[0, 1, 0], wcsem.at[0])
    worigin(1)
    krelay(-1)
    krelay(1)
    qrelay(-2, 0)
    qrelay(2, 0)
    wrelay(0, -6)
    wrelay(0, 6)
    qrelay(-2, 1)
    qrelay(2, 1)
    wgot(1, 0)
    wgot(-1, 0)
    wpass(0, 0)
    krelay(-2)
    krelay(2)
    kpass(2)
    wrelay(1, -3)
    wrelay(1, 3)
    wgot(1, 1)
    wgot(-1, 1)
    wpass(0, 1)
    qrelay(-3, 0)
    qrelay(3, 0)
    wgot(2, 0)
    wgot(-2, 0)
    wgot(4, 0)
    wpass(1, 0)
    qrelay(-3, 1)
    qrelay(3, 1)
    kpassed(2)
    attend(2, 0)
    attend(2, 1)
    krelay(-3)
    krelay(3)
    kpass(1)
    kpass(3)
    wrelay(1, -6)
    wrelay(1, 6)
    wpassed(0, 0)
    wpassed(0, 1)
    piece(2, 0)
    wgot(2, 1)
    wgot(-2, 1)
    wgot(4, 1)
    wpass(1, 1)
    wgot(-4, 0)
    wgot(5, 0)
    wpass(2, 0)
    kpassed(1)
    attend(1, 0)
    attend(1, 1)
    kpassed(3)
    attend(3, 0)
    attend(3, 1)
    wgot(-4, 1)
    wgot(5, 1)
    wpass(2, 1)
    kgot(-4)
    kpass(0)
    qgot(-4, 0)
    qgot(-4, 1)
    wgot(-5, 0)
    wgot(7, 0)
    wgot(-7, 0)
    wgot(8, 0)
    wpass(3, 0)
    piece(1, 0)
    piece(3, 0)
    wgot(-5, 1)
    wgot(7, 1)
    wgot(-7, 1)
    wgot(8, 1)
    wpass(3, 1)
    kpassed(0)
    attend(0, 0)
    attend(0, 1)
    piece(0, 0)
    for p in range(1, PIECES):
        wpassed(p, 0)
        wpassed(p, 1)
        for gs in (2, 1, 3, 0):
            piece(gs, p)
        for gs in (2, 1, 3, 0):
            reduced(gs, p - 1)
    for gs in (2, 1, 3, 0):
        reduced(gs, PIECES - 1)
    local[4].wait()
    local[5].wait()
    for p in range(PIECES):
        finish(p)
    scale = lax.rsqrt(jnp.sum(squares[0], axis=-1, keepdims=True) * (1.0 / 8192.0) + 1e-05)
    out = pltpu.make_async_copy(hidv, hid, lsem.at[6])
    out.start()
    for block in range(64):
        lanes = slice(block * 128, block * 128 + 128)
        nrmv[:, lanes] = (u[:, lanes] * scale * gv[block : block + 1, :]).astype(BF16)
    last = pltpu.make_async_copy(nrmv, nrm, lsem.at[7])
    last.start()
    for copy in sends:
        if copy is not None:
            copy.wait_send()
    for copy in pending:

        @pl.when(yh != c)
        def _(copy=copy):
            copy.wait_send()

    out.wait()
    last.wait()


def local(queries, keys, values, out_weight, residual, norm_gain):
    any_space = pl.BlockSpec(memory_space=pl.ANY)
    vmem = pltpu.VMEM
    dma = pltpu.SemaphoreType.DMA
    return pl.pallas_call(
        kernel,
        out_shape=(jax.ShapeDtypeStruct((16, 8192), BF16),) * 2,
        in_specs=[any_space] * 6,
        out_specs=(any_space,) * 2,
        scratch_shapes=[
            vmem((4, 2, 2, 4, 32, 256), BF16),
            vmem((2, 16, 512), BF16),
            vmem((4, 2, 4, 2, 16, 128), BF16),
            vmem((4, 4, 2, 16, 128), BF16),
            vmem((256, 128), BF16),
            vmem((64, 256), BF16),
            vmem((16, 2, 2, 64, 256), BF16),
            vmem((128, 128), F32),
            vmem((4, 2, 2, 128, 256), BF16),
            vmem((4, PIECES, 4, 32, 256), BF16),
            vmem((4, PIECES, 3, 32, 256), BF16),
            vmem((4, PIECES, 2, 16, 256), BF16),
            vmem((8, PIECES, 16, 256), BF16),
            vmem((16, 8192), F32),
            vmem((16, 8192), BF16),
            vmem((64, 128), F32),
            vmem((16, 8192), BF16),
            vmem((16, 8192), BF16),
            dma((8,)),
            dma((200,)),
            dma((4, 2, 2)),
            dma((1,)),
            dma((4, 2, 2)),
            dma((3,)),
            dma((4,)),
            dma((16, 2)),
            dma((1,)),
            dma((PIECES, 2)),
            dma((4, PIECES, 3)),
            dma((8, PIECES)),
        ],
        compiler_params=pltpu.CompilerParams(collective_id=0, has_side_effects=True),
        name="layer",
    )(
        queries.reshape(4, 2, 32, 256),
        keys,
        values,
        out_weight,
        residual,
        norm_gain.reshape(64, 128),
    )


def solution(mesh):
    finer = Mesh(mesh.devices.reshape(4, 16, 4, 2, 2), ("yl", "z", "x", "yh", "c"))
    rows, heads = ("yl", "z"), ("x", "yh", "c")
    both = rows + heads
    in_specs = (P(rows, heads), P(both, None), P(both, None), P(heads, rows), P(both, None), P())
    out_specs = (P(both, None), P(both, None))
    return jax.shard_map(local, mesh=finer, in_specs=in_specs, out_specs=out_specs, check_vma=False)
```

time: 262 us -> 74.5 us (0.28)
  waiting for transfers between devices: 170 us -> 0 us
  Pallas kernels: 0 us -> 71.2 us
  blocking collectives: 55.5 us -> 0 us
  between operations: 14.1 us -> 0.65 us
  local copies, waits for them, and re-layouts: 12.2 us -> 2.42 us
  matrix products: 6.39 us -> 0 us
  other arithmetic: 3.72 us -> 0 us
    reduce_scatter x1 -> x0, waiting for transfers between devices: 132 us -> none  [local(): lax.psum_scatter(jnp.dot(attended, whole_weight, preferred_element_type=j...]
    pallas_call x0 -> x1, Pallas kernels: none -> 71.2 us  [local(): pl.pallas_call(kernel, out_shape=(jax.ShapeDtypeStruct((16, 8192), BF16),...]
    all_gather x2 -> x0, blocking collectives: 55.5 us -> none  [the longest x1 41.2 us: in_one_piece(): lax.all_gather(both, axis, axis=dim, tiled=True)]
    all_gather x1 -> x0, waiting for transfers between devices: 37.7 us -> none  [stacked_from(): pieces = lax.all_gather(pieces, axes[k], axis=0, tiled=True)]
    transpose x2 -> x0, local copies, waits for them, and re-layouts: 11 us -> none  [the longest x1 6.39 us: in_order(): pieces = jnp.moveaxis(pieces, 0, dim)]
    dot_general x3 -> x0, matrix products: 6.02 us -> none  [the longest x1 5.45 us: local(): jnp.dot(attended, whole_weight, preferred_element_type=jnp.float32)]
  transfers between devices with their start and end apart: 2 -> 0, of which waited for: 2 -> 0; matrix products, arithmetic and copies ran while one was open for 1% -> 0% of each run, Pallas kernels for 0% -> 0%
where the time goes in v1:
time: 74.5 us; the launch traced here: 74.3 us
  Pallas kernels  71.2 us (96%)
  local copies, waits for them, and re-layouts  2.42 us (3%)
    pallas_call x1, Pallas kernels, local(): pl.pallas_call(kernel, out_shape=(jax.ShapeDtypeStruct((16, 8192), BF16),...  71.2 us
    unnamed x4, local copies, waits for them, and re-layouts  2.42 us

profile of v1, /device:TPU:1, one launch (start us, length us, event | category | flops | bytes accessed | tf_op | source)
XLA Modules:
  0.0 74.3 jit_solution(3440897575216542047)
XLA Ops:
  0.6 71.2 %layer.1 = (bf16[16,8192]{1,0:T(8,128)(2,1)}, bf16[16,8192]{1,0:T(8,128)(2,1)}) custom-call(bf16[4,2,32,256]{3,2,1,0:T(8,128)(2,1)} %bitcast.2, bf16[16,512]{1,0:T(8,128)(2,1)} %k.1, bf16[16,512]{1,0:T(8,128)(2,1)} %v.1, bf16[256,128]{1,0:T(8,128)(2,1)} %w.1, bf16[16,8192]{1,0:T(8,128)(2,1)} %res.1, f32[64,128]{1,0:T(8,128)} %bitcast.3), custom_call_target="tpu_custom_call" | custom-call | tf_op jit(solution)/shard_map/layer/pallas_call | solution.py:388
  71.9 0.0 copy-start
  71.9 1.7 %copy.10 = bf16[16,8192]{1,0:T(8,128)(2,1)} copy(bf16[16,8192]{1,0:T(8,128)(2,1)} %get-tuple-element.4) | data formatting | bytes 524288
  73.6 0.0 copy-done
  73.6 0.7 copy.11
Async XLA Ops:
  71.9 1.7 %copy-start = (bf16[16,8192]{1,0:T(8,128)(2,1)S(1)}, bf16[16,8192]{1,0:T(8,128)(2,1)}, u32[]{:S(2)}) copy-start(bf16[16,8192]{1,0:T(8,128)(2,1)} %get-tuple-element.5) | copy-start | bytes 786436

commit v2 on v0

v2 whole, which is shorter than its diff:
```python
import math

import jax
import jax.numpy as jnp
from jax import lax
from jax.experimental import pallas as pl
from jax.experimental.pallas import tpu as pltpu
from jax.sharding import Mesh
from jax.sharding import PartitionSpec as P

MESH = pl.DeviceIdType.MESH
F32, BF16 = jnp.float32, jnp.bfloat16
NT = (((1,), (1,)), ((), ()))

QC, WC = 0, 1
VMEM = 60 * 1024 * 1024
PIECES = 4
GROUPS = (2, 1, 3, 0)

ORDER = (0, 1, -1, 3, -3, 2, -2, 4, -4, 6, -6, 5, -5, 7, -7, 8)
SLOT = {d: i for i, d in enumerate(ORDER)}

SPREAD = (
    {0: (3, -3, 1, -1), 3: (6, 4, 2), -3: (-6, -4, -2), 6: (8, 7, 5), -6: (-7, -5)},
    {0: (3, -3, 1, -1), 3: (6, 4, 2), -3: (-6, -4, -2), 6: (7, 5), -6: (8, -7, -5)},
)
RELAYS = [(wave, core, d) for wave in range(2) for core in range(2) for d in SPREAD[wave] if d]


def seat(d):
    return -d if d != 8 else 8


LEAVES = [
    [
        (d, wave, core)
        for d in ORDER[4 * p : 4 * p + 4]
        for wave in range(2)
        for core in range(2)
        if d and (wave, core, seat(d)) not in RELAYS
    ]
    for p in range(PIECES)
]

PLAN_Q = (
    ("q_begin",), ("q_own",),
    ("q_relay", -1, 0), ("q_relay", 1, 0), ("k_own",), ("q_relay", -1, 1), ("q_relay", 1, 1),
    ("q_relay", -2, 0), ("q_relay", 2, 0), ("k_relay", -1), ("k_relay", 1),
    ("q_relay", -2, 1), ("q_relay", 2, 1), ("k_relay", -2), ("k_relay", 2),
    ("q_relay", -3, 0), ("q_relay", 3, 0), ("attend", 2),
    ("q_relay", -3, 1), ("q_relay", 3, 1), ("k_relay", -3), ("k_relay", 3),
    ("attend", 1), ("attend", 3),
    ("q_last",), ("k_last",), ("attend", 0),
    ("w_passed", 0), ("piece", 0),
    ("w_passed", 1), ("piece", 1),
    ("reduced", 0, 2), ("reduced", 0, 1), ("reduced", 0, 3), ("reduced", 0, 0),
    ("reduced", 1, 2), ("reduced", 1, 1), ("reduced", 1, 3), ("reduced", 1, 0),
)

PLAN_W = (
    ("w_begin",), ("w_other",),
    ("w_relay", 0, WC, 3), ("w_relay", 0, WC, -3), ("w_relay", 0, QC, 3), ("w_relay", 0, QC, -3),
    ("w_crossed", WC), ("w_crossed", QC),
    ("w_relay", 0, WC, 6), ("w_relay", 0, WC, -6), ("w_relay", 0, QC, 6), ("w_relay", 0, QC, -6),
    ("w_relay", 1, WC, 3), ("w_relay", 1, WC, -3), ("w_relay", 1, QC, 3), ("w_relay", 1, QC, -3),
    ("w_got", 0), ("w_pass", 0),
    ("w_relay", 1, WC, 6), ("w_relay", 1, WC, -6), ("w_got", 1), ("w_pass", 1),
    ("w_relay", 1, QC, 6), ("w_relay", 1, QC, -6),
    ("a_got", 2), ("a_got", 1), ("a_got", 3), ("a_got", 0),
    ("w_got", 2), ("piece", 2),
    ("w_got", 3), ("piece", 3),
    ("reduced", 2, 2), ("reduced", 2, 1), ("reduced", 2, 3), ("reduced", 2, 0),
    ("reduced", 3, 2), ("reduced", 3, 1), ("reduced", 3, 3), ("reduced", 3, 0),
)


def kernel(
    q, k, v, w, sums,
    qall, kvl, kvr, wv, wt, wcross, wall, bias, att, psend, xr, ssend, rbuf, size,
    lsem, ssem, rsem, wpsem, atsem, xsem, asem, go,
):
    yl, z, x, yh, c = (lax.axis_index(a) for a in ("yl", "z", "x", "yh", "c"))
    y = yh * 4 + yl

    def dev(dy=0, dz=0, dx=0, core=None):
        yt = lax.rem(y + (dy + 8), 8)
        return (lax.rem(yt, 4), lax.rem(z + (dz + 16), 16), lax.rem(x + dx, 4), lax.div(yt, 4), c if core is None else core)

    def remote(src, dst, send_sem, recv_sem, to):
        return pltpu.make_async_remote_copy(
            src_ref=src, dst_ref=dst, send_sem=send_sem, recv_sem=recv_sem, device_id=to, device_id_type=MESH
        )

    sent = [0]

    def send(src, dst, recv_sem, to):
        remote(src, dst, ssem.at[0], recv_sem, to).start()
        sent[0] += math.prod(src.shape) * 2

    def received(dst, recv_sem):
        remote(dst, dst, ssem.at[0], recv_sem, dev(core=1 - c)).wait_recv()

    def sized(bytes_):
        assert bytes_ % 8192 == 0
        return size.at[pl.ds(0, bytes_ // 8192)]

    def half_of(r):
        return lax.div(lax.rem(y + (r + 8), 8), 4)

    w_load = pltpu.make_async_copy(w, wv, lsem.at[0])
    q_load = pltpu.make_async_copy(q, qall.at[0, yh, c], lsem.at[1])
    kv_load = [pltpu.make_async_copy(k, kvl.at[0], lsem.at[2]), pltpu.make_async_copy(v, kvl.at[1], lsem.at[2])]
    barrier = pltpu.get_barrier_semaphore()
    around_q = [dict(dy=1), dict(dy=-1), dict(dx=1), dict(dx=2), dict(dx=3)]
    hops = sorted({t - s for spread in SPREAD for s, ts in spread.items() for t in ts})
    around_w = [dict(dy=4)] + [dict(dz=d) for d in sorted({d for h in hops for d in (h, -h)})]

    @pl.when(c == QC)
    def _():
        for peer in around_q:
            pl.semaphore_signal(barrier, inc=1, device_id=dev(**peer), device_id_type=MESH)

    @pl.when(c == WC)
    def _():
        pl.semaphore_signal(barrier, inc=1, device_id=dev(core=QC), device_id_type=MESH)
        for peer in around_w:
            pl.semaphore_signal(barrier, inc=1, device_id=dev(**peer), device_id_type=MESH)

    w_load.start()
    for copy in kv_load:
        copy.start()
    q_load.start()

    w_load.wait()
    wt[...] = wv[...].astype(F32).T.astype(BF16).reshape(2, 64, 256)

    def lanes_of(half, core):
        return pl.ds(pl.multiple_of((half * 2 + core) * 256, 256), 256)

    def head_of(i):
        return pl.ds(pl.multiple_of(i * 128, 128), 128)

    def unit(d, wave, core):
        return wall.at[SLOT[d], :, lanes_of(1 - yh if wave else yh, core)]

    def w_sem(d, wave, core):
        if d == 0:
            return rsem.at[core if wave else 2]
        if (wave, core, seat(d)) in RELAYS:
            return rsem.at[3 + PIECES + RELAYS.index((wave, core, seat(d)))]
        return rsem.at[3 + SLOT[d] // 4]

    def w_spread(wave, core, d):
        for t in SPREAD[wave].get(d, ()):
            send(unit(seat(d), wave, core), unit(seat(t), wave, core), w_sem(seat(t), wave, core), dev(dz=t - d))

    def w_origin(core):
        send(wcross.at[core], wall.at[0, :, lanes_of(yh, core)], w_sem(0, 1, core), dev(dy=4))
        w_spread(0, core, 0)

    def w_other():
        received(sized(65536), rsem.at[2])
        w_origin(QC)

    def w_crossed(core):
        received(unit(0, 1, core), w_sem(0, 1, core))
        w_spread(1, core, 0)

    def w_relay(wave, core, d):
        received(unit(seat(d), wave, core), w_sem(seat(d), wave, core))
        w_spread(wave, core, d)

    def w_got(p):
        received(sized(len(LEAVES[p]) * 32768), rsem.at[3 + p])

    def w_pass(p):
        rows = pl.ds(4 * p, 4)
        send(wall.at[rows], wall.at[rows], wpsem.at[p], dev(core=QC))

    def w_passed(p):
        received(wall.at[pl.ds(4 * p, 4)], wpsem.at[p])

    def q_send(r, s, hop):
        t = (r - hop) % 8
        sem = rsem.at[0 if t == 4 else 1 + 2 * t + s]
        send(qall.at[r % 4, half_of(r), s], qall.at[t % 4, half_of(r), s], sem, dev(dy=hop))

    def q_relay(r, s):
        received(qall.at[r % 4, half_of(r), s], rsem.at[1 + 2 * (r % 8) + s])
        if abs(r) < 3 or s == (0 if r < 0 else 1):
            q_send(r, s, 1 if r < 0 else -1)

    def q_last():
        received(qall.at[0, half_of(4)], rsem.at[0])

    def k_send(r, hop):
        t = (r - hop) % 8
        some = pl.ds(0 if hop > 0 else 2, 2) if t == 4 else pl.ds(0, 4)
        send(kvr.at[r % 4, half_of(r), some], kvr.at[t % 4, half_of(r), some], rsem.at[17 + t], dev(dy=hop))

    def k_relay(r):
        received(kvr.at[r % 4, half_of(r)], rsem.at[17 + r % 8])
        k_send(r, 1 if r < 0 else -1)

    def k_last():
        received(kvr.at[0, half_of(4)], rsem.at[21])

    def k_spread():
        for copy in kv_load:
            copy.wait()
        for d in (2, 1, 3):
            head = head_of(lax.rem(x + d, 4))
            send(kvl.at[:, :, head], kvr.at[0, yh, x, :, c], rsem.at[17], dev(dx=d, core=QC))

    def k_own():
        received(sized(7 * 8192), rsem.at[17])
        k_send(0, 1)
        k_send(0, -1)

    def q_own():
        received(qall.at[0, yh, WC], rsem.at[1 + WC])
        q_send(0, WC, 1)
        q_send(0, WC, -1)

    def q_begin():
        pl.semaphore_wait(barrier, len(around_q) + 1)
        pl.semaphore_signal(go, inc=1, device_id=dev(core=WC), device_id_type=MESH)
        send(wt.at[yh], unit(0, 0, QC), rsem.at[2], dev(core=WC))
        send(wt.at[1 - yh], wcross.at[QC], rsem.at[2], dev(core=WC))
        k_spread()
        kvr[0, yh, x, :, QC] = kvl[:, :, head_of(x)]
        q_load.wait()
        q_send(0, QC, 1)
        q_send(0, QC, -1)
        row = lax.broadcasted_iota(jnp.int32, (128, 128), 0)
        col = lax.broadcasted_iota(jnp.int32, (128, 128), 1)
        bias[...] = jnp.where((lax.div(row, 32) == lax.div(col, 32)) & (col <= row), 0.0, -1e30)

    def w_greet():
        pl.semaphore_wait(barrier, len(around_w))
        w_origin(WC)

    def w_give():
        pl.semaphore_wait(go, 1)
        q_load.wait()
        send(qall.at[0, yh, WC], qall.at[0, yh, WC], rsem.at[1 + WC], dev(core=QC))
        k_spread()
        send(kvl.at[:, :, head_of(x)], kvr.at[0, yh, x, :, WC], rsem.at[17], dev(core=QC))

    def w_begin():
        wall[0, :, lanes_of(yh, WC)] = wt[yh]
        wcross[WC] = wt[1 - yh]
        before = sent[0]

        @pl.when(z < 8)
        def _():
            w_give()
            w_greet()

        sent[0] = before

        @pl.when(z >= 8)
        def _():
            w_greet()
            w_give()

    def attend(gs):
        for t in range(2):
            pair = kvr[gs, t]
            keys, values = pair[:, 0].reshape(128, 128), pair[:, 1].reshape(128, 128)
            values = jnp.concatenate([values, jnp.ones((128, 128), BF16)], axis=1)
            for h in range(2):
                queries = jnp.concatenate(
                    [
                        qall[gs, h, s, :, j * 128 : j * 128 + 128].reshape(4, 2, 32, 128)[:, t].reshape(128, 128)
                        for s in range(2)
                        for j in range(2)
                    ],
                    axis=0,
                )
                scores = lax.dot_general(queries, keys, NT, preferred_element_type=F32)
                scores = scores * (1.0 / math.sqrt(128.0)) + jnp.concatenate([bias[...]] * 4, axis=0)
                powers = jnp.exp(scores - jnp.max(scores, axis=-1, keepdims=True)).astype(BF16)
                sums = jnp.dot(powers, values, preferred_element_type=F32)
                heads = (sums[:, :128] / sums[:, 128:]).astype(BF16)
                for i in range(4):
                    att[gs, t, :, h * 512 + i * 128 : h * 512 + i * 128 + 128] = heads[i * 128 : i * 128 + 128]
        send(att.at[gs], att.at[gs], atsem.at[gs], dev(core=WC))

    def a_got(gs):
        received(att.at[gs], atsem.at[gs])

    def piece(p):
        rows = wall[4 * p : 4 * p + 4].reshape(256, 1024)
        total = lax.dot_general(att[...].reshape(1024, 1024), rows, NT, preferred_element_type=F32)
        psend[p % 2] = total.astype(BF16).reshape(4, 2, 4, 32, 256)
        for gs in GROUPS:
            for d in (2, 1, 3):
                there = lax.rem(x + d, 4)
                send(psend.at[p % 2, gs, :, there], xr.at[p % 2, gs, d - 1], xsem.at[p % 2, gs], dev(dx=d))

    def reduced(p, gs):
        received(xr.at[p % 2, gs], xsem.at[p % 2, gs])
        total = psend[p % 2, gs, :, x].astype(F32)
        for d in range(3):
            total = total + xr[p % 2, gs, d].astype(F32)
        ssend[p % 2, gs] = total.astype(BF16).reshape(2, 2, 16, 256)
        for other in (1, 0):
            half = 1 - yh if other else yh
            there = half * 4 + lax.rem(yl + gs, 4)
            place = lax.rem(y + 8 - there, 8)
            for core in (1 - c, c):
                home = (lax.rem(yl + gs, 4), z, x, half, core)
                if gs or other:
                    send(ssend.at[p % 2, gs, half, core], rbuf.at[p, place], asem.at[p], home)
                elif core is c:
                    rbuf[p, 0] = ssend[p % 2, 0, yh, c]
                else:
                    send(ssend.at[p % 2, 0, yh, core], rbuf.at[p, 0], asem.at[4 + p % 2], home)

    steps = dict(
        q_begin=q_begin, w_begin=w_begin, q_own=q_own, q_relay=q_relay, q_last=q_last, k_own=k_own, k_relay=k_relay,
        k_last=k_last, attend=attend, w_origin=w_origin, w_other=w_other, w_crossed=w_crossed, w_relay=w_relay,
        w_got=w_got, w_pass=w_pass, w_passed=w_passed, a_got=a_got, piece=piece, reduced=reduced,
    )

    def follow(plan):
        sent[0] = 0
        for name, *numbers in plan:
            with jax.named_scope("_".join(map(str, (name, *numbers)))):
                steps[name](*numbers)

    def arrive(mine):
        with jax.named_scope("arrive"):
            outs = []
            for p in range(PIECES):
                received(rbuf.at[p, pl.ds(1, 7)], asem.at[p])
                if p // 2 != mine:
                    received(rbuf.at[p, 0], asem.at[4 + p % 2])
                outs.append(pltpu.make_async_copy(rbuf.at[p], sums.at[p], lsem.at[3 + p]))
                outs[-1].start()
            stand_in = sized(sent[0])
            remote(stand_in, stand_in, ssem.at[0], ssem.at[0], dev(core=1 - c)).wait_send()
            for copy in outs:
                copy.wait()

    @pl.when(c == QC)
    def _():
        follow(PLAN_Q)
        arrive(0)

    @pl.when(c == WC)
    def _():
        follow(PLAN_W)
        arrive(1)


def last_kernel(sums, res, gain, hid, nrm, rbuf, resv, gv, u, hidv, nrmv, sem):
    yl, z, yh = (lax.axis_index(a) for a in ("yl", "z", "yh"))
    y = yh * 4 + yl
    loads = [
        pltpu.make_async_copy(res, resv, sem.at[0]),
        pltpu.make_async_copy(gain, gv, sem.at[0]),
    ]
    loads += [pltpu.make_async_copy(sums.at[p], rbuf.at[p], sem.at[1 + p]) for p in range(PIECES)]
    for copy in loads:
        copy.start()
    for copy in loads[:2]:
        copy.wait()
    squares = jnp.zeros((16, 128), F32)
    low = lax.broadcasted_iota(jnp.int32, (16, 128), 1) < 64
    for p in range(PIECES):
        loads[2 + p].wait()
        for r in range(4):
            here = lax.div(lax.rem(y + r, 8), 4)
            first, second = r + 4 * here, r + 4 - 4 * here
            for t in range(2):
                lanes = slice(t * 128, t * 128 + 128)
                a = rbuf[p, first, :, lanes].astype(F32)
                b = rbuf[p, second, :, lanes].astype(F32)
                pair = (jnp.where(low, a, pltpu.roll(b, 64, 1)), jnp.where(low, pltpu.roll(a, 64, 1), b))
                for i in range(2):
                    block = lax.rem(yl + r, 4) * 16 + lax.rem(z + (ORDER[4 * p + 2 * t + i] + 16), 16)
                    at = pl.ds(pl.multiple_of(block * 128, 128), 128)
                    updated = resv[:, at].astype(F32) + pair[i]
                    u[:, at] = updated
                    hidv[:, at] = updated.astype(BF16)
                    squares = squares + updated * updated
    stores = [pltpu.make_async_copy(hidv, hid, sem.at[5])]
    stores[0].start()
    scale = lax.rsqrt(jnp.sum(squares, axis=-1, keepdims=True) * (1.0 / 8192.0) + 1e-05)
    for part in range(2):
        for block in range(32 * part, 32 * part + 32):
            lanes = slice(block * 128, block * 128 + 128)
            nrmv[:, lanes] = (u[:, lanes] * scale * gv[block : block + 1, :]).astype(BF16)
        lanes = pl.ds(4096 * part, 4096)
        stores.append(pltpu.make_async_copy(nrmv.at[:, lanes], nrm.at[:, lanes], sem.at[6 + part]))
        stores[-1].start()
    for copy in stores:
        copy.wait()


def local(queries, keys, values, out_weight, residual, norm_gain):
    in_hbm = pl.BlockSpec(memory_space=pltpu.HBM)
    vmem = pltpu.VMEM
    dma = pltpu.SemaphoreType.DMA
    sums = pl.pallas_call(
        kernel,
        out_shape=jax.ShapeDtypeStruct((PIECES, 8, 16, 256), BF16),
        in_specs=[in_hbm] * 4,
        out_specs=in_hbm,
        scratch_shapes=[
            vmem((4, 2, 2, 256, 256), BF16),
            vmem((2, 16, 512), BF16),
            vmem((4, 2, 4, 2, 2, 16, 128), BF16),
            vmem((256, 128), BF16),
            vmem((2, 64, 256), BF16),
            vmem((2, 64, 256), BF16),
            vmem((16, 64, 1024), BF16),
            vmem((128, 128), F32),
            vmem((4, 2, 128, 1024), BF16),
            vmem((2, 4, 2, 4, 32, 256), BF16),
            vmem((2, 4, 3, 2, 32, 256), BF16),
            vmem((2, 4, 2, 2, 16, 256), BF16),
            vmem((PIECES, 8, 16, 256), BF16),
            vmem((800, 16, 256), BF16),
            dma((3 + PIECES,)),
            dma((1,)),
            dma((max(25, 3 + PIECES + len(RELAYS)),)),
            dma((2,)),
            dma((4,)),
            dma((2, 4)),
            dma((6,)),
            pltpu.SemaphoreType.REGULAR,
        ],
        compiler_params=pltpu.CompilerParams(collective_id=0, has_side_effects=True, vmem_limit_bytes=VMEM),
        name="layer",
    )(queries, keys, values, out_weight)
    return pl.pallas_call(
        last_kernel,
        out_shape=(jax.ShapeDtypeStruct((16, 8192), BF16),) * 2,
        in_specs=[in_hbm] * 3,
        out_specs=(in_hbm,) * 2,
        scratch_shapes=[
            vmem((PIECES, 8, 16, 256), BF16),
            vmem((16, 8192), BF16),
            vmem((64, 128), F32),
            vmem((16, 8192), F32),
            vmem((16, 8192), BF16),
            vmem((16, 8192), BF16),
            dma((8,)),
        ],
        compiler_params=pltpu.CompilerParams(vmem_limit_bytes=VMEM),
        name="final",
    )(sums, residual, norm_gain.reshape(64, 128))


def solution(mesh):
    finer = Mesh(mesh.devices.reshape(4, 16, 4, 2, 2), ("yl", "z", "x", "yh", "c"))
    rows, heads = ("yl", "z"), ("x", "yh", "c")
    both = rows + heads
    in_specs = (P(rows, heads), P(both, None), P(both, None), P(heads, rows), P(both, None), P())
    out_specs = (P(both, None), P(both, None))
    return jax.shard_map(local, mesh=finer, in_specs=in_specs, out_specs=out_specs, check_vma=False)
```

time: 262 us -> 62.7 us (0.24)
  waiting for transfers between devices: 170 us -> 0 us
  Pallas kernels: 0 us -> 61.9 us
  blocking collectives: 55.5 us -> 0 us
  between operations: 14.1 us -> 0.64 us
  local copies, waits for them, and re-layouts: 12.2 us -> 0 us
  matrix products: 6.39 us -> 0 us
  other arithmetic: 3.72 us -> 0 us
    reduce_scatter x1 -> x0, waiting for transfers between devices: 132 us -> none  [local(): lax.psum_scatter(jnp.dot(attended, whole_weight, preferred_element_type=j...]
    pallas_call x0 -> x2, Pallas kernels: none -> 61.9 us  [the longest x1 59.6 us: local(): pl.pallas_call(kernel, out_shape=jax.ShapeDtypeStruct((PIECES, 8, 16, 256...]
    all_gather x2 -> x0, blocking collectives: 55.5 us -> none  [the longest x1 41.2 us: in_one_piece(): lax.all_gather(both, axis, axis=dim, tiled=True)]
    all_gather x1 -> x0, waiting for transfers between devices: 37.7 us -> none  [stacked_from(): pieces = lax.all_gather(pieces, axes[k], axis=0, tiled=True)]
    transpose x2 -> x0, local copies, waits for them, and re-layouts: 11 us -> none  [the longest x1 6.39 us: in_order(): pieces = jnp.moveaxis(pieces, 0, dim)]
    dot_general x3 -> x0, matrix products: 6.02 us -> none  [the longest x1 5.45 us: local(): jnp.dot(attended, whole_weight, preferred_element_type=jnp.float32)]
  transfers between devices with their start and end apart: 2 -> 0, of which waited for: 2 -> 0; matrix products, arithmetic and copies ran while one was open for 1% -> 0% of each run, Pallas kernels for 0% -> 0%
where the time goes in v2:
time: 62.7 us; the launch traced here: 62.5 us
  Pallas kernels  61.9 us (99%)
  between operations  0.64 us (1%)
    pallas_call x1, Pallas kernels, local(): pl.pallas_call(kernel, out_shape=jax.ShapeDtypeStruct((PIECES, 8, 16, 256...  59.6 us
    pallas_call x1, Pallas kernels, local(): pl.pallas_call(last_kernel, out_shape=(jax.ShapeDtypeStruct((16, 8192), B...  2.25 us

profile of v2, /device:TPU:1, one launch (start us, length us, event | category | flops | bytes accessed | tf_op | source)
XLA Modules:
  0.0 62.5 jit_solution(11822878520136894251)
XLA Ops:
  0.6 59.6 %layer.1.sums = bf16[4,8,16,256]{3,2,1,0:T(8,128)(2,1)} custom-call(bf16[256,256]{1,0:T(8,128)(2,1)} %q.1, bf16[16,512]{1,0:T(8,128)(2,1)} %k.1, bf16[16,512]{1,0:T(8,128)(2,1)} %v.1, bf16[256,128]{1,0:T(8,128)(2,1)} %w.1), custom_call_target="tpu_custom_call" | custom-call | tf_op jit(solution)/shard_map/layer/pallas_call | solution.py:407
  60.2 2.3 %final.1 = (bf16[16,8192]{1,0:T(8,128)(2,1)}, bf16[16,8192]{1,0:T(8,128)(2,1)}) custom-call(bf16[4,8,16,256]{3,2,1,0:T(8,128)(2,1)} %layer.1.sums, bf16[16,8192]{1,0:T(8,128)(2,1)} %res.1, f32[64,128]{1,0:T(8,128)} %bitcast.1), custom_call_target="tpu_custom_call" | custom-call | tf_op jit(solution)/shard_map/final/pallas_call | solution.py:439

commit v3 on v2

v3 whole, which is shorter than its diff:
```python
import math

import jax
import jax.numpy as jnp
from jax import lax
from jax.experimental import pallas as pl
from jax.experimental.pallas import tpu as pltpu
from jax.sharding import Mesh
from jax.sharding import PartitionSpec as P

MESH = pl.DeviceIdType.MESH
F32, BF16 = jnp.float32, jnp.bfloat16
NT = (((1,), (1,)), ((), ()))

QC, WC = 0, 1
VMEM = 60 * 1024 * 1024
PIECES = 4

ORDER = (
    (0, 2, 3, 1, 4, 13, 5, 12, 7, 11, 6, 10, 15, 14, 9, 8),
    (1, 0, 2, 4, 3, 5, 6, 7, 13, 12, 15, 14, 11, 10, 9, 8),
    (2, 1, 3, 0, 5, 6, 4, 7, 15, 14, 8, 13, 9, 10, 11, 12),
    (3, 1, 0, 2, 5, 4, 6, 7, 8, 15, 12, 9, 10, 11, 14, 13),
    (4, 3, 2, 0, 1, 7, 6, 9, 15, 10, 14, 13, 12, 5, 8, 11),
    (5, 6, 1, 7, 2, 0, 4, 10, 9, 15, 8, 11, 3, 13, 12, 14),
    (6, 4, 3, 10, 2, 7, 1, 8, 11, 9, 12, 14, 13, 15, 5, 0),
    (7, 6, 9, 4, 3, 1, 2, 10, 5, 11, 8, 12, 15, 14, 0, 13),
    (8, 7, 9, 6, 10, 5, 3, 12, 14, 11, 0, 4, 1, 15, 2, 13),
    (9, 8, 10, 11, 6, 12, 7, 5, 14, 4, 3, 2, 1, 15, 0, 13),
    (10, 9, 8, 11, 7, 12, 13, 14, 0, 1, 4, 3, 5, 6, 2, 15),
    (11, 10, 8, 12, 13, 9, 14, 0, 15, 5, 1, 7, 4, 6, 2, 3),
    (12, 11, 13, 10, 9, 8, 0, 15, 14, 7, 4, 5, 1, 6, 3, 2),
    (13, 0, 14, 15, 8, 1, 2, 7, 6, 5, 9, 3, 11, 10, 4, 12),
    (14, 13, 15, 2, 1, 8, 6, 0, 9, 7, 11, 10, 12, 4, 3, 5),
    (15, 14, 13, 9, 12, 2, 11, 1, 10, 0, 8, 6, 7, 5, 3, 4),
)

FIRST = (
    (1, 2, 3, 5),
    (0, 2, 3, 4, 5),
    (0, 1, 3, 4, 6),
    (0, 2, 4, 6),
    (1, 2, 3, 5, 6, 7),
    (2, 3, 4, 6, 7),
    (2, 4, 5, 7),
    (2, 3, 5, 6),
    (3, 4, 5, 6, 7, 9, 10, 11, 12, 13),
    (4, 5, 6, 7, 8, 10, 11, 12),
    (0, 5, 6, 7, 8, 9, 11, 12, 13),
    (0, 6, 7, 9, 10, 12, 13),
    (0, 9, 10, 11, 13, 14, 15),
    (0, 3, 8, 10, 11, 12, 14, 15),
    (0, 1, 2, 3, 4, 8, 9, 10, 11, 13, 15),
    (0, 1, 2, 4, 11, 12, 13, 14),
)

ROUTES = (
    (
        (0, 0, 0, 0, 1, 5, 2, 3), (0, 0, 1, 0, 1, 5, 2, 3), (0, 1, 0, 0, 1, 3, 5, 2), (0, 1, 1, 0, 1, 3, 5, 2),
        (0, 0, 0, 2, 1), (0, 0, 1, 2, 1), (0, 0, 0, 3, 1), (0, 0, 1, 3, 1), (0, 0, 0, 1), (0, 0, 1, 1), (3, 13),
        (1, 0, 0, 0, 13), (1, 0, 1, 0, 13), (1, 1, 0, 0, 13), (1, 1, 1, 0, 13), (1, 0, 0, 1, 13), (1, 0, 1, 1, 13),
        (0, 1, 0, 2, 1), (3, 14), (1, 0, 0, 2, 14), (1, 0, 1, 2, 14), (1, 0, 0, 1, 14), (1, 0, 1, 1, 14),
        (1, 1, 0, 2, 14), (0, 1, 1, 2, 1, 14), (3, 15), (0, 1, 0, 3, 1), (0, 1, 1, 3, 1), (0, 0, 1, 13, 15, 1),
        (0, 1, 0, 1, 14, 13), (0, 0, 1, 12, 15, 3, 1), (0, 1, 1, 1, 14, 13), (2, 0), (0, 0, 1, 11, 15, 1),
        (0, 0, 0, 13, 15, 1), (0, 0, 0, 12, 15, 3, 1), (0, 0, 1, 10, 1, 15), (0, 0, 0, 11, 15, 1),
        (0, 0, 0, 10, 1, 15), (0, 1, 1, 13, 1, 15), (0, 1, 1, 12, 15, 3, 1), (0, 1, 0, 13, 1, 15),
        (0, 1, 1, 11, 15, 1), (0, 1, 0, 12, 15, 3, 1), (2, 1), (0, 1, 1, 10, 1, 15), (0, 0, 1, 8, 15, 1),
        (0, 0, 0, 8, 15, 1), (0, 1, 0, 11, 15, 1), (0, 1, 0, 10, 1, 15), (2, 2), (0, 1, 1, 8, 1, 15), (2, 3),
        (0, 1, 0, 8, 1, 15), (2, 4),
    ),
    (
        (0, 0, 0, 1, 5, 2), (0, 0, 1, 1, 5, 2), (0, 1, 0, 1, 5, 2), (0, 1, 1, 1, 5, 2), (0, 0, 0, 4, 0, 2, 3),
        (0, 0, 1, 4, 0, 2, 3), (0, 0, 0, 5, 0), (3, 14), (0, 0, 1, 5, 0), (0, 0, 1, 6, 0, 14), (0, 0, 0, 6, 0, 14),
        (0, 1, 0, 4, 2, 0, 3), (0, 1, 1, 4, 2, 0, 3), (2, 0), (0, 0, 1, 13, 4, 2), (0, 1, 0, 5, 0), (0, 1, 1, 5, 0),
        (0, 0, 1, 11, 2, 3), (0, 0, 0, 13, 4, 2), (0, 1, 1, 6, 0, 14), (0, 1, 0, 6, 0, 14), (0, 0, 0, 11, 2, 3),
        (0, 1, 1, 13, 4, 2), (2, 1), (0, 1, 0, 13, 4, 2), (0, 1, 1, 11, 3, 2), (2, 2), (0, 1, 0, 11, 3, 2), (2, 3),
        (2, 4),
    ),
    (
        (0, 0, 0, 2, 0, 4), (0, 0, 1, 2, 0, 4), (0, 0, 0, 1, 6, 3, 0), (0, 0, 1, 1, 6, 3, 0), (0, 1, 0, 2, 4, 0),
        (0, 1, 1, 2, 4, 0), (0, 0, 0, 5, 3, 1), (0, 0, 1, 5, 3, 1), (0, 0, 1, 6, 1, 4), (0, 1, 0, 1, 6, 0, 3),
        (0, 0, 0, 6, 1, 4), (0, 1, 1, 1, 6, 0, 3), (0, 0, 1, 7, 0, 1), (0, 0, 0, 7, 0, 1), (0, 1, 0, 5, 3, 1), (2, 0),
        (0, 0, 1, 15, 1, 3, 0, 4), (0, 1, 1, 5, 3, 1), (0, 0, 1, 14, 4, 0, 1), (0, 0, 0, 15, 1, 3, 0, 4),
        (0, 1, 1, 6, 4, 1), (0, 0, 0, 14, 4, 0, 1), (0, 1, 0, 6, 4, 1), (0, 1, 1, 7, 1, 0), (0, 1, 0, 7, 1, 0),
        (0, 1, 1, 15, 0, 4, 3, 1), (2, 1), (0, 1, 1, 14, 1, 0, 4), (0, 1, 0, 15, 0, 4, 3, 1), (0, 1, 0, 14, 1, 0, 4),
        (2, 2), (2, 3), (2, 4),
    ),
    (
        (0, 0, 0, 3, 4, 6, 2, 0), (0, 0, 1, 3, 4, 6, 2, 0), (0, 0, 0, 0, 4), (0, 1, 0, 3, 4, 2, 0, 6),
        (0, 1, 1, 3, 4, 2, 0, 6), (0, 0, 1, 0, 4), (3, 13), (3, 14), (0, 1, 0, 0, 4), (0, 0, 1, 8, 6, 2),
        (0, 1, 1, 0, 4), (2, 0), (0, 0, 0, 8, 6, 2), (0, 0, 1, 12, 2, 14, 13, 4), (0, 1, 1, 8, 2, 6), (2, 1),
        (0, 1, 0, 8, 2, 6), (0, 0, 0, 12, 2, 14, 13, 4), (0, 1, 1, 12, 2, 14, 13, 4), (0, 1, 0, 12, 2, 14, 13, 4),
        (2, 2), (2, 3), (2, 4),
    ),
    (
        (0, 0, 0, 4, 6, 1), (0, 0, 1, 4, 6, 1), (0, 0, 0, 2, 7, 6, 5, 3), (0, 0, 1, 2, 7, 6, 5, 3),
        (0, 1, 0, 4, 1, 6), (0, 1, 1, 4, 1, 6), (3, 14), (3, 15), (0, 1, 0, 2, 5, 3, 6, 7), (0, 1, 1, 2, 5, 3, 6, 7),
        (0, 0, 1, 9, 3, 5, 2, 6), (0, 0, 0, 9, 3, 5, 2, 6), (0, 0, 1, 15, 5, 7), (2, 0), (0, 0, 1, 14, 7, 6, 3),
        (0, 0, 0, 15, 5, 7), (0, 0, 0, 14, 7, 6, 3), (0, 1, 1, 9, 5, 6, 2, 3), (0, 0, 1, 13, 6, 3, 5),
        (0, 1, 1, 15, 7, 5), (0, 1, 0, 9, 5, 6, 2, 3), (2, 1), (0, 0, 0, 13, 6, 3, 5), (0, 1, 1, 14, 6, 7, 3),
        (0, 0, 0, 5, 15, 14, 6), (0, 1, 0, 15, 7, 5), (0, 1, 1, 13, 3, 5, 6), (0, 1, 0, 14, 6, 7, 3),
        (0, 1, 0, 13, 3, 5, 6), (2, 2), (0, 0, 1, 5, 15, 14, 6), (0, 1, 0, 5, 15, 14, 6), (0, 1, 1, 5, 15, 14, 6),
        (2, 3), (2, 4),
    ),
    (
        (0, 0, 0, 5, 2), (0, 0, 1, 5, 2), (0, 0, 0, 1, 4, 7), (0, 0, 1, 1, 4, 7), (0, 0, 1, 7, 4, 3, 6),
        (0, 1, 0, 5, 2), (0, 1, 1, 5, 2), (0, 0, 0, 7, 4, 3, 6), (3, 8), (1, 0, 0, 5, 8), (1, 0, 1, 5, 8),
        (1, 1, 0, 5, 8), (1, 1, 1, 5, 8), (3, 10), (1, 0, 0, 1, 10), (1, 0, 1, 1, 10), (0, 1, 1, 7, 3, 4, 6),
        (0, 1, 0, 1, 4, 7, 10), (0, 1, 1, 1, 4, 7, 10), (0, 1, 0, 7, 3, 4, 6), (2, 0), (0, 0, 1, 10, 3, 4, 2),
        (0, 0, 0, 10, 3, 4, 2), (0, 1, 1, 10, 4, 2, 3), (0, 1, 0, 10, 4, 2, 3), (2, 1), (2, 2), (2, 3), (2, 4),
    ),
    (
        (0, 0, 1, 6, 5, 2, 7), (0, 0, 0, 6, 5, 2, 7), (0, 0, 0, 3, 7), (0, 0, 0, 4, 7, 5), (0, 0, 1, 4, 7, 5),
        (0, 0, 1, 3, 7), (0, 1, 1, 6, 5, 2, 7), (0, 1, 0, 6, 5, 2, 7), (3, 9), (1, 0, 0, 4, 9), (1, 0, 1, 4, 9),
        (3, 8), (1, 0, 0, 3, 8), (1, 0, 1, 3, 8), (0, 0, 1, 10, 7, 5), (0, 0, 1, 11, 5, 4, 8), (0, 0, 0, 10, 7, 5),
        (0, 1, 0, 3, 7, 8), (0, 1, 0, 4, 5, 7, 9), (0, 1, 1, 4, 5, 7, 9), (0, 0, 0, 11, 5, 4, 8), (0, 1, 1, 3, 7, 8),
        (0, 1, 1, 10, 7, 5), (0, 1, 0, 10, 7, 5), (2, 0), (0, 0, 1, 8, 5, 4, 7), (0, 1, 1, 11, 8, 4, 5),
        (0, 0, 0, 8, 5, 4, 7), (0, 1, 1, 8, 4, 5, 7), (0, 0, 1, 13, 9, 8, 7), (0, 1, 0, 8, 4, 5, 7), (2, 1),
        (0, 1, 0, 11, 8, 4, 5), (0, 0, 0, 13, 9, 8, 7), (0, 1, 1, 13, 9, 8, 7), (2, 2), (0, 1, 0, 13, 9, 8, 7),
        (2, 3), (2, 4),
    ),
    (
        (0, 0, 1, 7, 5, 2), (0, 0, 0, 7, 5, 2), (0, 0, 1, 6, 3), (0, 0, 0, 6, 3), (3, 9), (1, 0, 1, 6, 9),
        (1, 0, 0, 6, 9), (0, 1, 1, 7, 5, 2), (3, 8), (1, 0, 1, 7, 8), (1, 0, 0, 7, 8), (1, 0, 1, 6, 8),
        (1, 0, 0, 6, 8), (1, 1, 1, 7, 8), (3, 10), (1, 0, 1, 7, 10), (1, 0, 0, 7, 10), (1, 1, 1, 7, 10),
        (0, 1, 0, 7, 8, 5, 10, 2), (0, 1, 1, 6, 8, 3, 9), (0, 1, 0, 6, 8, 3, 9), (2, 0), (2, 1),
        (0, 0, 1, 15, 9, 10, 8, 6), (0, 0, 0, 15, 9, 10, 8, 6), (0, 1, 1, 15, 9, 6, 10, 8), (2, 2),
        (0, 1, 0, 15, 9, 6, 10, 8), (2, 3), (2, 4),
    ),
    (
        (0, 0, 1, 8, 9, 12, 10, 3, 11), (0, 0, 0, 8, 9, 12, 10, 3, 11), (0, 1, 1, 8, 9, 11, 3, 12, 10),
        (0, 1, 0, 8, 9, 11, 3, 12, 10), (0, 0, 0, 3, 10, 13, 5, 9), (0, 0, 1, 3, 10, 13, 5, 9), (2, 0),
        (0, 0, 0, 5, 11, 4, 9, 7), (0, 0, 1, 5, 11, 4, 9, 7), (0, 1, 0, 5, 7, 11, 9, 4), (0, 1, 1, 5, 7, 11, 9, 4),
        (0, 1, 0, 3, 13, 9, 5, 10), (0, 1, 1, 3, 13, 9, 5, 10), (2, 1), (0, 0, 0, 0, 6, 7, 9), (0, 0, 1, 0, 6, 7, 9),
        (0, 1, 0, 0, 9, 7, 6), (0, 1, 1, 0, 9, 7, 6), (2, 2), (2, 3), (2, 4),
    ),
    (
        (0, 0, 1, 9, 7, 8, 10, 4, 12), (0, 0, 0, 9, 7, 8, 10, 4, 12), (0, 1, 1, 9, 4, 7, 8, 12, 10),
        (0, 1, 0, 9, 4, 7, 8, 12, 10), (0, 0, 1, 12, 7, 6, 5, 8), (0, 0, 0, 12, 7, 6, 5, 8), (0, 0, 0, 4, 8, 10, 12),
        (0, 0, 1, 4, 8, 10, 12), (2, 0), (0, 1, 1, 12, 5, 8, 6, 7), (0, 1, 0, 12, 5, 8, 6, 7),
        (0, 1, 0, 4, 12, 10, 8), (2, 1), (0, 1, 1, 4, 12, 10, 8), (0, 0, 0, 2, 11, 10, 8, 12),
        (0, 0, 1, 2, 11, 10, 8, 12), (0, 1, 0, 2, 11, 8, 12, 10), (0, 1, 1, 2, 11, 8, 12, 10), (2, 2), (2, 3), (2, 4),
    ),
    (
        (0, 0, 1, 10, 12, 9, 6, 0, 11, 8), (0, 0, 0, 10, 12, 9, 6, 0, 11, 8), (0, 1, 1, 10, 6, 11, 8, 0, 12, 9),
        (0, 1, 0, 10, 6, 11, 8, 0, 12, 9), (0, 0, 1, 7, 13, 9), (0, 0, 1, 14, 9, 12, 11, 5), (0, 0, 0, 7, 13, 9),
        (0, 1, 1, 7, 13, 9), (2, 0), (0, 1, 0, 7, 13, 9), (0, 0, 0, 14, 9, 12, 11, 5), (0, 1, 1, 14, 9, 12, 11, 5),
        (0, 1, 0, 14, 9, 12, 11, 5), (0, 0, 0, 1, 12, 8, 9, 11), (2, 1), (0, 0, 1, 1, 12, 8, 9, 11),
        (0, 1, 0, 1, 9, 12, 8, 11), (0, 1, 1, 1, 9, 12, 8, 11), (2, 2), (2, 3), (2, 4),
    ),
    (
        (0, 0, 1, 11, 6, 9, 0, 10, 12, 7), (0, 0, 0, 11, 6, 9, 0, 10, 12, 7), (0, 1, 1, 11, 6, 12, 9, 10, 7, 0),
        (0, 1, 0, 11, 6, 12, 9, 10, 7, 0), (2, 0), (0, 0, 0, 5, 13, 12, 10), (0, 0, 1, 5, 13, 12, 10),
        (0, 1, 0, 5, 13, 10, 12), (2, 1), (0, 1, 1, 5, 13, 10, 12), (2, 2), (2, 3), (2, 4),
    ),
    (
        (0, 0, 1, 12, 10, 0, 11, 9), (0, 0, 0, 12, 10, 0, 11, 9), (0, 1, 1, 12, 10, 9, 0, 11), (0, 0, 1, 9, 11, 15),
        (0, 1, 0, 12, 10, 9, 0, 11), (0, 0, 0, 9, 11, 15), (0, 0, 1, 8, 14, 0, 13), (0, 0, 0, 8, 14, 0, 13),
        (0, 1, 1, 9, 11, 15), (2, 0), (0, 1, 0, 9, 11, 15), (0, 1, 1, 8, 0, 14, 13), (0, 0, 0, 0, 14, 10, 15, 11),
        (0, 1, 0, 8, 0, 14, 13), (0, 0, 1, 0, 14, 10, 15, 11), (0, 1, 0, 0, 11, 15, 10, 14),
        (0, 1, 1, 0, 11, 15, 10, 14), (0, 0, 0, 4, 13, 11, 15, 14), (0, 0, 1, 4, 13, 11, 15, 14), (2, 1),
        (0, 1, 0, 4, 11, 14, 13, 15), (0, 1, 1, 4, 11, 14, 13, 15), (2, 2), (2, 3), (2, 4),
    ),
    (
        (0, 0, 1, 13, 11, 12, 0, 14, 10), (0, 0, 0, 13, 11, 12, 0, 14, 10), (0, 1, 1, 13, 0, 12, 11, 14, 10),
        (0, 1, 0, 13, 0, 12, 11, 14, 10), (0, 0, 0, 0, 12, 8), (0, 0, 1, 0, 12, 8), (0, 1, 0, 0, 12, 8),
        (0, 1, 1, 0, 12, 8), (0, 0, 1, 7, 12, 14, 15, 11), (2, 0), (0, 0, 0, 7, 12, 14, 15, 11),
        (0, 1, 1, 7, 11, 12, 15, 14), (0, 0, 1, 6, 12), (0, 0, 0, 3, 11, 14, 12, 15), (0, 1, 0, 7, 11, 12, 15, 14),
        (2, 1), (0, 0, 0, 6, 12), (0, 0, 1, 3, 11, 14, 12, 15), (0, 1, 1, 6, 12), (0, 1, 0, 3, 15, 14, 11, 12),
        (0, 1, 0, 6, 12), (0, 1, 1, 3, 15, 14, 11, 12), (2, 2), (2, 3), (2, 4),
    ),
    (
        (0, 0, 1, 14, 8, 10, 15, 13, 2), (0, 0, 0, 14, 8, 10, 15, 13, 2), (0, 1, 1, 14, 10, 8, 15, 2, 13),
        (0, 1, 0, 14, 10, 8, 15, 2, 13), (0, 0, 0, 2, 9, 13, 15), (0, 0, 1, 2, 9, 13, 15), (0, 0, 0, 1, 15),
        (0, 0, 1, 1, 15), (0, 1, 0, 2, 15, 9, 13), (0, 1, 1, 2, 15, 9, 13), (2, 0), (0, 0, 1, 6, 13, 10, 15, 11),
        (0, 1, 0, 1, 15), (0, 1, 1, 1, 15), (0, 0, 0, 6, 13, 10, 15, 11), (0, 1, 1, 6, 10, 13, 11, 15),
        (0, 1, 0, 6, 10, 13, 11, 15), (2, 1), (2, 2), (2, 3), (2, 4),
    ),
    (
        (0, 0, 1, 15, 12, 11, 14, 2, 13), (0, 0, 0, 15, 12, 11, 14, 2, 13), (0, 1, 1, 15, 2, 14, 11, 13, 12),
        (0, 1, 0, 15, 2, 14, 11, 13, 12), (0, 0, 1, 9, 14, 0, 13, 1), (0, 0, 0, 9, 14, 0, 13, 1),
        (0, 0, 1, 11, 14, 13), (0, 0, 1, 10, 14, 13), (0, 0, 0, 11, 14, 13), (0, 0, 0, 10, 14, 13),
        (0, 1, 1, 9, 1, 0, 14, 13), (0, 1, 1, 11, 13, 14), (0, 1, 0, 9, 1, 0, 14, 13), (2, 0), (0, 1, 1, 10, 13, 14),
        (0, 1, 0, 11, 13, 14), (2, 1), (0, 1, 0, 10, 13, 14), (2, 2), (2, 3), (2, 4),
    ),
)

SLOT = [{source: i for i, source in enumerate(order)} for order in ORDER]
RELAYS = [[tuple(step[1:4]) for step in route if step[0] == 0 and step[3] != z] for z, route in enumerate(ROUTES)]
BOUNDS = (0, 4, 8, 12, 14, 16)
PART = [sum(slot >= bound for bound in BOUNDS[1:]) for slot in range(16)]
RSEMS = 10 + max(map(len, RELAYS))


def leaves(z, p):
    return [
        (wave, core, source)
        for source in ORDER[z][BOUNDS[p] : BOUNDS[p + 1]]
        for wave in range(2)
        for core in range(2)
        if source != z and (wave, core, source) not in RELAYS[z]
    ]


RING = (
    ("q_begin",), ("q_own",),
    ("q_relay", -1, 0, 0), ("q_relay", 1, 0, 0), ("q_relay", -1, 0, 1), ("q_relay", 1, 0, 1),
    ("k_own",),
    ("q_relay", -2, 0, 0), ("q_relay", 2, 0, 0), ("q_relay", -1, 1, 0), ("q_relay", 1, 1, 0),
    ("q_relay", -2, 0, 1), ("q_relay", 2, 0, 1), ("q_relay", -1, 1, 1), ("q_relay", 1, 1, 1),
    ("k_relay", -1), ("k_relay", 1),
    ("q_relay", -3, 0, 0), ("q_relay", 3, 0, 0), ("q_relay", -2, 1, 0), ("q_relay", 2, 1, 0),
    ("q_relay", -3, 0, 1), ("q_relay", 3, 0, 1), ("q_relay", -2, 1, 1), ("q_relay", 2, 1, 1),
    ("k_relay", -2), ("k_relay", 2),
    ("q_relay", -3, 1, 0), ("q_relay", 3, 1, 0), ("q_relay", -3, 1, 1), ("q_relay", 3, 1, 1),
    ("k_relay", -3), ("k_relay", 3),
)

LATE_RING = (
    ("q_begin",), ("q_own_first",),
    ("q_relay", -1, 1, 0), ("q_relay", 1, 1, 0), ("q_relay", -1, 1, 1), ("q_relay", 1, 1, 1),
    ("q_relay", -2, 1, 0), ("q_relay", 2, 1, 0), ("q_relay", -2, 1, 1), ("q_relay", 2, 1, 1),
    ("q_relay", -3, 1, 0), ("q_relay", 3, 1, 0), ("q_relay", -3, 1, 1), ("q_relay", 3, 1, 1),
    ("q_own_last",), ("k_own",),
    ("q_relay", -1, 0, 0), ("q_relay", 1, 0, 0), ("q_relay", -1, 0, 1), ("q_relay", 1, 0, 1),
    ("k_relay", -1), ("k_relay", 1),
    ("q_relay", -2, 0, 0), ("q_relay", 2, 0, 0), ("q_relay", -2, 0, 1), ("q_relay", 2, 0, 1),
    ("k_relay", -2), ("k_relay", 2),
    ("q_relay", -3, 0, 0), ("q_relay", 3, 0, 0), ("q_relay", -3, 0, 1), ("q_relay", 3, 0, 1),
    ("k_relay", -3), ("k_relay", 3),
)

PLAN_Q = (
    ("ring",),
    ("attend", 2), ("attend", 1), ("attend", 3),
    ("w_passed", 0), ("piece", 0, 1), ("w_passed", 1), ("piece", 1, 1),
    ("q_last",), ("k_last",), ("attend", 0),
    ("piece", 0, 0), ("piece", 1, 0),
    ("reduced", 0, 2), ("reduced", 0, 1), ("reduced", 0, 3), ("reduced", 1, 2), ("reduced", 1, 1), ("reduced", 1, 3),
    ("reduced", 0, 0), ("reduced", 1, 0),
)

PLAN_W = (
    ("w_begin",), ("w_route", 0),
    ("a_got", 2), ("a_got", 1), ("a_got", 3), ("a_got", 0),
    ("w_piece", 2, 0, 4), ("w_route", 1), ("w_piece", 3, 0, 2), ("w_route", 2), ("w_piece", 3, 2, 2),
    ("reduced", 2, 0), ("reduced", 2, 1), ("reduced", 2, 3), ("reduced", 2, 2),
    ("reduced", 3, 0), ("reduced", 3, 1), ("reduced", 3, 3), ("reduced", 3, 2),
)


def by_place(z, do, low=0, high=16):
    if high - low == 1:
        do(low)
        return
    middle = (low + high) // 2
    pl.when(z < middle)(lambda: by_place(z, do, low, middle))
    pl.when(z >= middle)(lambda: by_place(z, do, middle, high))


def kernel(
    q, k, v, w, sums,
    qall, kvl, kvr, wv, wt, wcross, wall, bias, att, psend, xr, ssend, rbuf, size,
    lsem, ssem, rsem, wpsem, atsem, xsem, asem, go, late,
):
    yl, z, x, yh, c = (lax.axis_index(a) for a in ("yl", "z", "x", "yh", "c"))
    y = yh * 4 + yl

    def dev(dy=0, dz=0, dx=0, to_z=None, role=None):
        yt = lax.rem(y + (dy + 8), 8)
        zt = lax.rem(z + (dz + 16), 16) if to_z is None else to_z
        xt = lax.rem(x + dx, 4)
        core = role if to_z else jnp.where(xt + yt + zt == 0, 1 - role, role)
        return (lax.rem(yt, 4), zt, xt, lax.div(yt, 4), core)

    origin = x + y + z == 0
    for_q = jnp.where(origin, 1 - QC, QC) == c
    one_more = jnp.where(origin, 0, 1)

    def remote(src, dst, send_sem, recv_sem, to):
        return pltpu.make_async_remote_copy(
            src_ref=src, dst_ref=dst, send_sem=send_sem, recv_sem=recv_sem, device_id=to, device_id_type=MESH
        )

    sent = [0]

    def send(src, dst, recv_sem, to):
        remote(src, dst, ssem.at[0], recv_sem, to).start()
        sent[0] += math.prod(src.shape) * 2

    def received(dst, recv_sem):
        remote(dst, dst, ssem.at[0], recv_sem, (yl, z, x, yh, 1 - c)).wait_recv()

    def sized(bytes_):
        assert bytes_ % 8192 == 0 and bytes_ // 8192 <= size.shape[0]
        return size.at[pl.ds(0, bytes_ // 8192)]

    def half_of(r):
        return lax.div(lax.rem(y + (r + 8), 8), 4)

    w_load = pltpu.make_async_copy(w, wv, lsem.at[0])
    q_load = pltpu.make_async_copy(q, qall.at[0, yh, c], lsem.at[1])
    kv_load = [pltpu.make_async_copy(k, kvl.at[0], lsem.at[2]), pltpu.make_async_copy(v, kvl.at[1], lsem.at[2])]
    barrier = pltpu.get_barrier_semaphore()
    around_q = [dict(dy=1), dict(dy=-1), dict(dx=1), dict(dx=2), dict(dx=3)]

    w_load.start()
    for copy in kv_load:
        copy.start()
    q_load.start()

    @pl.when(for_q)
    def _():
        for peer in around_q:
            pl.semaphore_signal(barrier, inc=1, device_id=dev(role=QC, **peer), device_id_type=MESH)

    @pl.when(~for_q)
    def _():
        pl.semaphore_signal(barrier, inc=1, device_id=dev(dy=4, role=WC), device_id_type=MESH)

        @pl.when(~origin)
        def _():
            pl.semaphore_signal(barrier, inc=1, device_id=dev(role=QC), device_id_type=MESH)

        def greet(place):
            for other in range(16):
                if place in FIRST[other]:
                    pl.semaphore_signal(barrier, inc=1, device_id=dev(to_z=other, role=WC), device_id_type=MESH)

        by_place(z, greet)

    w_load.wait()
    wt[...] = wv[...].astype(F32).T.astype(BF16).reshape(2, 64, 256)
    for copy in kv_load:
        copy.wait()

    def lanes_of(half, core):
        return pl.ds(pl.multiple_of((half * 2 + core) * 256, 256), 256)

    def head_of(i):
        return pl.ds(pl.multiple_of(i * 128, 128), 128)

    def unit(slot, wave, core):
        return wall.at[slot, :, lanes_of(1 - yh if wave else yh, core)]

    def w_sem(place, wave, core, source):
        if (wave, core, source) in RELAYS[place]:
            return rsem.at[10 + RELAYS[place].index((wave, core, source))]
        return rsem.at[5 + PART[SLOT[place][source]]]

    def w_sends(place, wave, core, source, targets):
        for t in targets:
            here, there = SLOT[place][source], SLOT[t][source]
            to = dev(to_z=t, role=WC)
            send(unit(here, wave, core), unit(there, wave, core), w_sem(t, wave, core, source), to)

    def w_cross(core):
        send(wcross.at[core], wall.at[0, :, lanes_of(yh, core)], rsem.at[2 + core], dev(dy=4, role=WC))

    waited = []

    def w_step(place, kind, *step):
        if kind == 3:
            pl.semaphore_wait(late.at[step[0] - 8], 1)
            return
        if kind == 2:
            p = step[0]
            if leaves(place, p):
                received(sized(len(leaves(place, p)) * 32768), rsem.at[5 + p])
            if p < 2:
                rows = pl.ds(4 * p, 4)
                send(wall.at[rows], wall.at[rows], wpsem.at[p], dev(role=QC))
            return
        wave, core, source, *targets = step
        if kind == 0:
            if source != place:
                received(unit(SLOT[place][source], wave, core), w_sem(place, wave, core, source))
            elif wave:
                received(unit(0, 1, core), rsem.at[2 + core])
            else:
                if (core == QC or place == 0) and place not in waited:
                    received(sized(65536), rsem.at[4])
                    waited.append(place)
                w_cross(core)
        w_sends(place, wave, core, source, targets)

    def w_route(part):
        totals = []

        def go_on(place):
            route = ROUTES[place]
            first = 1 + max(i for i, step in enumerate(route) if step[0] != 2 or step[1] == 2)
            cuts = (0, first, max(first, 1 + route.index((2, 3))), len(route))
            start = sent[0]
            for step in route[cuts[part] : cuts[part + 1]]:
                with jax.named_scope("_".join(map(str, ("at", place, *step)))):
                    w_step(place, *step)
            totals.append(sent[0] - start)
            sent[0] = start

        by_place(z, go_on)
        w_totals.append(totals)

    w_totals = []

    def w_passed(p):
        received(wall.at[pl.ds(4 * p, 4)], wpsem.at[p])

    def q_part(r, s, u):
        return qall.at[r % 4, half_of(r), s, pl.ds(128 * u, 128)]

    def q_sem(t, s, u):
        return rsem.at[0 if t == 4 else 8 + 4 * (t if t < 4 else t - 1) + 2 * s + u]

    def q_send(r, s, u, hop):
        t = (r - hop) % 8
        rows = pl.ds(128 * u, 128)
        dst = qall.at[t % 4, half_of(r), s, rows]
        send(q_part(r, s, u), dst, q_sem(t, s, u), dev(dy=hop, role=QC))

    def q_relay(r, s, u):
        received(q_part(r, s, u), q_sem(r % 8, s, u))
        if abs(r) < 3 or s == (0 if r < 0 else 1):
            q_send(r, s, u, 1 if r < 0 else -1)

    def q_last():
        received(qall.at[0, half_of(4)], rsem.at[0])

    def k_send(r, hop):
        t = (r - hop) % 8
        some = pl.ds(0 if hop > 0 else 2, 2) if t == 4 else pl.ds(0, 4)
        src, dst = kvr.at[r % 4, half_of(r), some], kvr.at[t % 4, half_of(r), some]
        send(src, dst, rsem.at[t if t else 8], dev(dy=hop, role=QC))

    def k_relay(r):
        received(kvr.at[r % 4, half_of(r)], rsem.at[r % 8])
        k_send(r, 1 if r < 0 else -1)

    def k_last():
        received(kvr.at[0, half_of(4)], rsem.at[4])

    def k_spread():
        for d in (2, 1, 3):
            head = head_of(lax.rem(x + d, 4))
            send(kvl.at[:, :, head], kvr.at[0, yh, x, :, c], rsem.at[8], dev(dx=d, role=QC))

    def k_own():
        received(sized(7 * 8192), rsem.at[8])
        k_send(0, 1)
        k_send(0, -1)

    def ring():
        before = sent[0]
        for late, plan in ((False, RING), (True, LATE_RING)):
            sent[0] = before

            def go_round(plan=plan):
                for step in plan:
                    do(*step)

            pl.when((x + z == 0) if late else (x + z > 0))(go_round)

    def q_own_first():
        once(~origin, None, q_own)

    def q_own_last():
        before = sent[0]
        pl.when(origin)(q_own)
        sent[0] = before

    def w_hand():
        send(wt.at[yh], unit(0, 0, c), rsem.at[4], dev(role=WC))
        send(wt.at[1 - yh], wcross.at[c], rsem.at[4], dev(role=WC))

    def once(first, second, do):
        before = sent[0]
        pl.when(second if first is None else first)(do)
        if first is None:
            sent[0] = before

    def q_own():
        received(qall.at[0, yh, 1 - c], rsem.at[9])
        for u in range(2):
            for hop in (1, -1):
                q_send(0, 1 - c, u, hop)
        before = sent[0]
        pl.when(origin)(w_hand)
        sent[0] = before

    def q_begin():
        pl.semaphore_wait(barrier, len(around_q) + one_more)

        def meet():
            pl.semaphore_signal(go, inc=1, device_id=dev(role=WC), device_id_type=MESH)
            w_hand()

        once(~origin, None, meet)

        @pl.when(origin)
        def _():
            pl.semaphore_signal(barrier, inc=1, device_id=dev(role=WC), device_id_type=MESH)

        k_spread()
        kvr[0, yh, x, :, c] = kvl[:, :, head_of(x)]
        q_load.wait()
        for u in range(2):
            for hop in (1, -1):
                q_send(0, c, u, hop)
        row = lax.broadcasted_iota(jnp.int32, (128, 128), 0)
        col = lax.broadcasted_iota(jnp.int32, (128, 128), 1)
        bias[...] = jnp.where((lax.div(row, 32) == lax.div(col, 32)) & (col <= row), 0.0, -1e30)

    def w_begin():
        wall[0, :, lanes_of(yh, c)] = wt[yh]
        wcross[c] = wt[1 - yh]
        q_load.wait()

        def give():
            send(qall.at[0, yh, c], qall.at[0, yh, c], rsem.at[9], dev(role=QC))
            k_spread()
            send(kvl.at[:, :, head_of(x)], kvr.at[0, yh, x, :, c], rsem.at[8], dev(role=QC))

        def meet():
            pl.semaphore_wait(go, 1)
            give()

        once(~origin, None, meet)

        def greeted(place):
            pl.semaphore_wait(barrier, 2 + len(FIRST[place]) - one_more)
            for other in range(8):
                if (3, place) in ROUTES[other]:
                    to = dev(to_z=other, role=WC)
                    pl.semaphore_signal(late.at[place - 8], inc=1, device_id=to, device_id_type=MESH)

        by_place(z, greeted)
        once(None, origin, give)

    def attend(gs):
        for t in range(2):
            pair = kvr[gs, t]
            keys, values = pair[:, 0].reshape(128, 128), pair[:, 1].reshape(128, 128)
            values = jnp.concatenate([values, jnp.ones((128, 128), BF16)], axis=1)
            for h in range(2):
                queries = jnp.concatenate(
                    [
                        qall[gs, h, s, :, j * 128 : j * 128 + 128].reshape(4, 2, 32, 128)[:, t].reshape(128, 128)
                        for s in range(2)
                        for j in range(2)
                    ],
                    axis=0,
                )
                scores = lax.dot_general(queries, keys, NT, preferred_element_type=F32)
                scores = scores * (1.0 / math.sqrt(128.0)) + jnp.concatenate([bias[...]] * 4, axis=0)
                powers = jnp.exp(scores - jnp.max(scores, axis=-1, keepdims=True)).astype(BF16)
                total = jnp.dot(powers, values, preferred_element_type=F32)
                heads = (total[:, :128] / total[:, 128:]).astype(BF16)
                for i in range(4):
                    att[gs, t, :, h * 512 + i * 128 : h * 512 + i * 128 + 128] = heads[i * 128 : i * 128 + 128]
        send(att.at[gs], att.at[gs], atsem.at[gs], dev(role=WC))

    def a_got(gs):
        received(att.at[gs], atsem.at[gs])

    def spread(p, gs, lanes):
        for d in (2, 1, 3):
            src = psend.at[p % 2, gs, :, lax.rem(x + d, 4), :, lanes]
            dst = xr.at[p % 2, gs, d - 1, :, :, lanes]
            send(src, dst, xsem.at[p % 2, gs], dev(dx=d, role=QC if p < 2 else WC))

    def piece(p, most):
        groups = slice(1, 4) if most else slice(0, 1)
        n = 3 if most else 1
        rows = wall[4 * p : 4 * p + 4].reshape(256, 1024)
        total = lax.dot_general(att[groups].reshape(n * 256, 1024), rows, NT, preferred_element_type=F32)
        psend[p, groups] = total.astype(BF16).reshape(n, 2, 4, 32, 256)
        for gs in (2, 1, 3) if most else (0,):
            spread(p, gs, pl.ds(0, 256))

    def w_piece(p, slot, n):
        slots = slice(4 * p + slot, 4 * p + slot + n)
        rows = wall[slots].reshape(64 * n, 1024)
        total = lax.dot_general(att[...].reshape(1024, 1024), rows, NT, preferred_element_type=F32)
        lanes = slice(64 * slot, 64 * (slot + n))
        psend[p - 2, :, :, :, :, lanes] = total.astype(BF16).reshape(4, 2, 4, 32, 64 * n)
        for gs in (0, 1, 3, 2):
            spread(p, gs, pl.ds(64 * slot, 64 * n))

    def reduced(p, gs):
        received(xr.at[p % 2, gs], xsem.at[p % 2, gs])
        total = psend[p % 2, gs, :, x].astype(F32)
        for d in range(3):
            total = total + xr[p % 2, gs, d].astype(F32)
        ssend[p % 2, gs] = total.astype(BF16).reshape(2, 2, 16, 256)
        for other in (1, 0):
            half = 1 - yh if other else yh
            there = half * 4 + lax.rem(yl + gs, 4)
            place = lax.rem(y + 8 - there, 8)
            for core in (1 - c, c):
                home = (lax.rem(yl + gs, 4), z, x, half, core)
                if gs or other:
                    send(ssend.at[p % 2, gs, half, core], rbuf.at[p, place], asem.at[p], home)
                elif core is c:
                    rbuf[p, 0] = ssend[p % 2, 0, yh, c]
                else:
                    send(ssend.at[p % 2, 0, yh, core], rbuf.at[p, 0], asem.at[4 + p % 2], home)

    steps = dict(
        q_begin=q_begin, w_begin=w_begin, q_own=q_own, q_relay=q_relay, q_last=q_last, k_own=k_own, k_relay=k_relay,
        k_last=k_last, attend=attend, w_route=w_route, w_passed=w_passed, a_got=a_got, piece=piece, w_piece=w_piece, reduced=reduced,
        ring=ring, q_own_first=q_own_first, q_own_last=q_own_last,
    )

    def do(name, *numbers):
        with jax.named_scope("_".join(map(str, (name, *numbers)))):
            steps[name](*numbers)

    def follow(plan):
        sent[0] = 0
        for step in plan:
            do(*step)

    def drain(bytes_):
        stand_in = sized(bytes_)
        remote(stand_in, stand_in, ssem.at[0], ssem.at[0], (yl, z, x, yh, 1 - c)).wait_send()

    def arrive(mine):
        with jax.named_scope("arrive"):
            outs = []
            for p in range(PIECES):
                received(rbuf.at[p, pl.ds(1, 7)], asem.at[p])
                if p // 2 != mine:
                    received(rbuf.at[p, 0], asem.at[4 + p % 2])
                outs.append(pltpu.make_async_copy(rbuf.at[p], sums.at[p], lsem.at[3 + p]))
                outs[-1].start()
            if mine:
                by_place(z, lambda place: drain(sent[0] + sum(totals[place] for totals in w_totals)))
            else:
                drain(sent[0])
            for copy in outs:
                copy.wait()

    @pl.when(for_q)
    def _():
        follow(PLAN_Q)
        arrive(0)

    @pl.when(~for_q)
    def _():
        follow(PLAN_W)
        arrive(1)


def last_kernel(sums, res, gain, hid, nrm, rbuf, resv, gv, u, hidv, nrmv, sem):
    yl, z, yh = (lax.axis_index(a) for a in ("yl", "z", "yh"))
    y = yh * 4 + yl
    loads = [
        pltpu.make_async_copy(res, resv, sem.at[0]),
        pltpu.make_async_copy(gain, gv, sem.at[0]),
    ]
    loads += [pltpu.make_async_copy(sums.at[p], rbuf.at[p], sem.at[1 + p]) for p in range(PIECES)]
    for copy in loads:
        copy.start()

    def source_of(slot):
        low, high = (
            sum(ORDER[8 * part + i][slot] << (4 * i) for i in range(8)) for part in range(2)
        )
        low, high = (n - (1 << 32) if n >> 31 else n for n in (low, high))
        word = jnp.where(z < 8, jnp.int32(low), jnp.int32(high))
        return lax.shift_right_logical(word, 4 * lax.rem(z, 8)) & 15

    for copy in loads[:2]:
        copy.wait()
    squares = jnp.zeros((16, 128), F32)
    low = lax.broadcasted_iota(jnp.int32, (16, 128), 1) < 64
    for p in range(PIECES):
        sources = [source_of(4 * p + i) for i in range(4)]
        loads[2 + p].wait()
        for r in range(4):
            here = lax.div(lax.rem(y + r, 8), 4)
            first, second = r + 4 * here, r + 4 - 4 * here
            for t in range(2):
                lanes = slice(t * 128, t * 128 + 128)
                a = rbuf[p, first, :, lanes].astype(F32)
                b = rbuf[p, second, :, lanes].astype(F32)
                pair = (jnp.where(low, a, pltpu.roll(b, 64, 1)), jnp.where(low, pltpu.roll(a, 64, 1), b))
                for i in range(2):
                    block = lax.rem(yl + r, 4) * 16 + sources[2 * t + i]
                    at = pl.ds(pl.multiple_of(block * 128, 128), 128)
                    updated = resv[:, at].astype(F32) + pair[i]
                    u[:, at] = updated
                    hidv[:, at] = updated.astype(BF16)
                    squares = squares + updated * updated
    stores = [pltpu.make_async_copy(hidv, hid, sem.at[5])]
    stores[0].start()
    scale = lax.rsqrt(jnp.sum(squares, axis=-1, keepdims=True) * (1.0 / 8192.0) + 1e-05)
    for part in range(2):
        for block in range(32 * part, 32 * part + 32):
            lanes = slice(block * 128, block * 128 + 128)
            nrmv[:, lanes] = (u[:, lanes] * scale * gv[block : block + 1, :]).astype(BF16)
        lanes = pl.ds(4096 * part, 4096)
        stores.append(pltpu.make_async_copy(nrmv.at[:, lanes], nrm.at[:, lanes], sem.at[6 + part]))
        stores[-1].start()
    for copy in stores:
        copy.wait()


def local(queries, keys, values, out_weight, residual, norm_gain):
    in_hbm = pl.BlockSpec(memory_space=pltpu.HBM)
    vmem = pltpu.VMEM
    dma = pltpu.SemaphoreType.DMA
    sums = pl.pallas_call(
        kernel,
        out_shape=jax.ShapeDtypeStruct((PIECES, 8, 16, 256), BF16),
        in_specs=[in_hbm] * 4,
        out_specs=in_hbm,
        scratch_shapes=[
            vmem((4, 2, 2, 256, 256), BF16),
            vmem((2, 16, 512), BF16),
            vmem((4, 2, 4, 2, 2, 16, 128), BF16),
            vmem((256, 128), BF16),
            vmem((2, 64, 256), BF16),
            vmem((2, 64, 256), BF16),
            vmem((16, 64, 1024), BF16),
            vmem((128, 128), F32),
            vmem((4, 2, 128, 1024), BF16),
            vmem((2, 4, 2, 4, 32, 256), BF16),
            vmem((2, 4, 3, 2, 32, 256), BF16),
            vmem((2, 4, 2, 2, 16, 256), BF16),
            vmem((PIECES, 8, 16, 256), BF16),
            vmem((1200, 16, 256), BF16),
            dma((3 + PIECES,)),
            dma((1,)),
            dma((max(40, RSEMS),)),
            dma((2,)),
            dma((4,)),
            dma((2, 4)),
            dma((6,)),
            pltpu.SemaphoreType.REGULAR,
            pltpu.SemaphoreType.REGULAR((8,)),
        ],
        compiler_params=pltpu.CompilerParams(collective_id=0, has_side_effects=True, vmem_limit_bytes=VMEM),
        name="layer",
    )(queries, keys, values, out_weight)
    return pl.pallas_call(
        last_kernel,
        out_shape=(jax.ShapeDtypeStruct((16, 8192), BF16),) * 2,
        in_specs=[in_hbm] * 3,
        out_specs=(in_hbm,) * 2,
        scratch_shapes=[
            vmem((PIECES, 8, 16, 256), BF16),
            vmem((16, 8192), BF16),
            vmem((64, 128), F32),
            vmem((16, 8192), F32),
            vmem((16, 8192), BF16),
            vmem((16, 8192), BF16),
            dma((8,)),
        ],
        compiler_params=pltpu.CompilerParams(vmem_limit_bytes=VMEM),
        name="final",
    )(sums, residual, norm_gain.reshape(64, 128))


def solution(mesh):
    finer = Mesh(mesh.devices.reshape(4, 16, 4, 2, 2), ("yl", "z", "x", "yh", "c"))
    rows, heads = ("yl", "z"), ("x", "yh", "c")
    both = rows + heads
    in_specs = (P(rows, heads), P(both, None), P(both, None), P(heads, rows), P(both, None), P())
    out_specs = (P(both, None), P(both, None))
    return jax.shard_map(local, mesh=finer, in_specs=in_specs, out_specs=out_specs, check_vma=False)
```

time: 62.7 us -> 59.5 us (0.949)
  the two profiles are of different devices: /device:TPU:1 before, /device:TPU:3 now
where the time goes in v3:
time: 59.5 us; the launch traced here: 59.3 us
  Pallas kernels  58.5 us (98%)
  between operations  0.82 us (1%)
    pallas_call x1, Pallas kernels, local(): pl.pallas_call(kernel, out_shape=jax.ShapeDtypeStruct((PIECES, 8, 16, 256...  56.2 us
    pallas_call x1, Pallas kernels, local(): pl.pallas_call(last_kernel, out_shape=(jax.ShapeDtypeStruct((16, 8192), B...  2.25 us

profile of v3, /device:TPU:3, one launch (start us, length us, event | category | flops | bytes accessed | tf_op | source)
XLA Modules:
  0.0 59.3 jit_solution(14779806625499737460)
XLA Ops:
  0.6 56.2 %layer.1.sums = bf16[4,8,16,256]{3,2,1,0:T(8,128)(2,1)} custom-call(bf16[256,256]{1,0:T(8,128)(2,1)} %q.1, bf16[16,512]{1,0:T(8,128)(2,1)} %k.1, bf16[16,512]{1,0:T(8,128)(2,1)} %v.1, bf16[256,128]{1,0:T(8,128)(2,1)} %w.1), custom_call_target="tpu_custom_call" | custom-call | tf_op jit(solution)/shard_map/layer/pallas_call | solution.py:713
  56.8 2.3 %final.1 = (bf16[16,8192]{1,0:T(8,128)(2,1)}, bf16[16,8192]{1,0:T(8,128)(2,1)}) custom-call(bf16[4,8,16,256]{3,2,1,0:T(8,128)(2,1)} %layer.1.sums, bf16[16,8192]{1,0:T(8,128)(2,1)} %res.1, f32[64,128]{1,0:T(8,128)} %bitcast.1), custom_call_target="tpu_custom_call" | custom-call | tf_op jit(solution)/shard_map/final/pallas_call | solution.py:746

commit v4 on v3

--- a/solution.py
+++ b/solution.py
@@ -17,22 +17,22 @@
 PIECES = 4
 
 ORDER = (
-    (0, 2, 3, 1, 4, 13, 5, 12, 7, 11, 6, 10, 15, 14, 9, 8),
-    (1, 0, 2, 4, 3, 5, 6, 7, 13, 12, 15, 14, 11, 10, 9, 8),
-    (2, 1, 3, 0, 5, 6, 4, 7, 15, 14, 8, 13, 9, 10, 11, 12),
-    (3, 1, 0, 2, 5, 4, 6, 7, 8, 15, 12, 9, 10, 11, 14, 13),
-    (4, 3, 2, 0, 1, 7, 6, 9, 15, 10, 14, 13, 12, 5, 8, 11),
-    (5, 6, 1, 7, 2, 0, 4, 10, 9, 15, 8, 11, 3, 13, 12, 14),
-    (6, 4, 3, 10, 2, 7, 1, 8, 11, 9, 12, 14, 13, 15, 5, 0),
-    (7, 6, 9, 4, 3, 1, 2, 10, 5, 11, 8, 12, 15, 14, 0, 13),
-    (8, 7, 9, 6, 10, 5, 3, 12, 14, 11, 0, 4, 1, 15, 2, 13),
-    (9, 8, 10, 11, 6, 12, 7, 5, 14, 4, 3, 2, 1, 15, 0, 13),
-    (10, 9, 8, 11, 7, 12, 13, 14, 0, 1, 4, 3, 5, 6, 2, 15),
-    (11, 10, 8, 12, 13, 9, 14, 0, 15, 5, 1, 7, 4, 6, 2, 3),
-    (12, 11, 13, 10, 9, 8, 0, 15, 14, 7, 4, 5, 1, 6, 3, 2),
-    (13, 0, 14, 15, 8, 1, 2, 7, 6, 5, 9, 3, 11, 10, 4, 12),
-    (14, 13, 15, 2, 1, 8, 6, 0, 9, 7, 11, 10, 12, 4, 3, 5),
-    (15, 14, 13, 9, 12, 2, 11, 1, 10, 0, 8, 6, 7, 5, 3, 4),
+    (0, 2, 3, 1, 4, 13, 5, 12, 6, 11, 7, 15, 10, 14, 8, 9),
+    (1, 0, 4, 2, 3, 5, 6, 7, 13, 15, 12, 14, 11, 10, 9, 8),
+    (2, 1, 3, 5, 0, 6, 4, 7, 15, 14, 13, 8, 9, 11, 10, 12),
+    (3, 1, 0, 2, 5, 7, 4, 6, 8, 15, 9, 12, 10, 14, 11, 13),
+    (4, 3, 2, 7, 0, 1, 6, 9, 15, 10, 14, 13, 11, 12, 5, 8),
+    (5, 6, 7, 1, 2, 4, 0, 10, 9, 11, 15, 3, 13, 8, 12, 14),
+    (6, 4, 3, 10, 7, 2, 1, 11, 9, 8, 12, 14, 13, 15, 5, 0),
+    (7, 6, 9, 4, 3, 1, 2, 10, 5, 11, 12, 15, 8, 14, 0, 13),
+    (8, 7, 9, 6, 10, 5, 3, 12, 11, 14, 4, 0, 2, 15, 13, 1),
+    (9, 10, 8, 11, 6, 12, 7, 4, 14, 2, 5, 3, 15, 0, 1, 13),
+    (10, 9, 11, 8, 7, 12, 13, 14, 4, 0, 1, 3, 2, 5, 6, 15),
+    (11, 10, 12, 8, 13, 9, 15, 14, 0, 7, 5, 4, 2, 6, 1, 3),
+    (12, 11, 13, 10, 9, 8, 15, 0, 14, 4, 7, 6, 5, 2, 1, 3),
+    (13, 14, 15, 8, 0, 7, 2, 1, 6, 9, 4, 11, 10, 3, 5, 12),
+    (14, 13, 15, 2, 1, 8, 6, 7, 9, 11, 0, 4, 10, 12, 5, 3),
+    (15, 14, 13, 9, 12, 2, 11, 1, 10, 7, 8, 6, 0, 5, 4, 3),
 )
 
 FIRST = (
@@ -56,96 +56,96 @@
 
 ROUTES = (
     (
-        (0, 0, 0, 0, 1, 5, 2, 3), (0, 0, 1, 0, 1, 5, 2, 3), (0, 1, 0, 0, 1, 3, 5, 2), (0, 1, 1, 0, 1, 3, 5, 2),
-        (0, 0, 0, 2, 1), (0, 0, 1, 2, 1), (0, 0, 0, 3, 1), (0, 0, 1, 3, 1), (0, 0, 0, 1), (0, 0, 1, 1), (3, 13),
-        (1, 0, 0, 0, 13), (1, 0, 1, 0, 13), (1, 1, 0, 0, 13), (1, 1, 1, 0, 13), (1, 0, 0, 1, 13), (1, 0, 1, 1, 13),
-        (0, 1, 0, 2, 1), (3, 14), (1, 0, 0, 2, 14), (1, 0, 1, 2, 14), (1, 0, 0, 1, 14), (1, 0, 1, 1, 14),
-        (1, 1, 0, 2, 14), (0, 1, 1, 2, 1, 14), (3, 15), (0, 1, 0, 3, 1), (0, 1, 1, 3, 1), (0, 0, 1, 13, 15, 1),
-        (0, 1, 0, 1, 14, 13), (0, 0, 1, 12, 15, 3, 1), (0, 1, 1, 1, 14, 13), (2, 0), (0, 0, 1, 11, 15, 1),
-        (0, 0, 0, 13, 15, 1), (0, 0, 0, 12, 15, 3, 1), (0, 0, 1, 10, 1, 15), (0, 0, 0, 11, 15, 1),
-        (0, 0, 0, 10, 1, 15), (0, 1, 1, 13, 1, 15), (0, 1, 1, 12, 15, 3, 1), (0, 1, 0, 13, 1, 15),
-        (0, 1, 1, 11, 15, 1), (0, 1, 0, 12, 15, 3, 1), (2, 1), (0, 1, 1, 10, 1, 15), (0, 0, 1, 8, 15, 1),
-        (0, 0, 0, 8, 15, 1), (0, 1, 0, 11, 15, 1), (0, 1, 0, 10, 1, 15), (2, 2), (0, 1, 1, 8, 1, 15), (2, 3),
-        (0, 1, 0, 8, 1, 15), (2, 4),
+        (0, 0, 0, 0, 1, 5, 2, 3), (0, 0, 1, 0, 1, 5, 2, 3), (0, 0, 0, 2, 1), (0, 0, 1, 2, 1),
+        (0, 1, 0, 0, 1, 3, 5, 2), (0, 1, 1, 0, 1, 3, 5, 2), (0, 0, 0, 3, 1), (0, 0, 1, 3, 1), (0, 0, 0, 1),
+        (0, 0, 1, 1), (0, 1, 0, 2, 1), (3, 15), (3, 14), (1, 0, 0, 2, 14), (1, 0, 1, 2, 14), (1, 0, 0, 1, 14),
+        (1, 0, 1, 1, 14), (1, 1, 0, 2, 14), (3, 13), (1, 0, 0, 0, 13), (1, 0, 1, 0, 13), (1, 1, 0, 0, 13),
+        (1, 1, 1, 0, 13), (1, 0, 0, 1, 13), (1, 0, 1, 1, 13), (0, 1, 1, 2, 1, 14), (0, 1, 0, 3, 1), (0, 1, 1, 3, 1),
+        (0, 0, 1, 13, 15, 1), (0, 1, 0, 1, 14, 13), (0, 0, 1, 12, 15, 3, 1), (0, 0, 0, 13, 15, 1),
+        (0, 1, 1, 1, 14, 13), (0, 0, 0, 12, 15, 3, 1), (0, 0, 1, 11, 15, 1), (0, 0, 0, 11, 15, 1), (2, 0),
+        (0, 0, 1, 10, 1, 15), (0, 0, 0, 10, 1, 15), (0, 1, 1, 13, 1, 15), (0, 1, 1, 12, 15, 3, 1),
+        (0, 1, 0, 13, 1, 15), (0, 1, 0, 12, 15, 3, 1), (0, 1, 1, 11, 15, 1), (2, 1), (0, 1, 0, 11, 15, 1),
+        (0, 0, 0, 8, 15, 1), (0, 1, 1, 10, 1, 15), (0, 0, 1, 8, 15, 1), (0, 1, 0, 10, 1, 15), (2, 2),
+        (0, 1, 0, 8, 1, 15), (2, 3), (0, 1, 1, 8, 1, 15), (2, 4),
     ),
     (
         (0, 0, 0, 1, 5, 2), (0, 0, 1, 1, 5, 2), (0, 1, 0, 1, 5, 2), (0, 1, 1, 1, 5, 2), (0, 0, 0, 4, 0, 2, 3),
-        (0, 0, 1, 4, 0, 2, 3), (0, 0, 0, 5, 0), (3, 14), (0, 0, 1, 5, 0), (0, 0, 1, 6, 0, 14), (0, 0, 0, 6, 0, 14),
-        (0, 1, 0, 4, 2, 0, 3), (0, 1, 1, 4, 2, 0, 3), (2, 0), (0, 0, 1, 13, 4, 2), (0, 1, 0, 5, 0), (0, 1, 1, 5, 0),
-        (0, 0, 1, 11, 2, 3), (0, 0, 0, 13, 4, 2), (0, 1, 1, 6, 0, 14), (0, 1, 0, 6, 0, 14), (0, 0, 0, 11, 2, 3),
-        (0, 1, 1, 13, 4, 2), (2, 1), (0, 1, 0, 13, 4, 2), (0, 1, 1, 11, 3, 2), (2, 2), (0, 1, 0, 11, 3, 2), (2, 3),
+        (0, 0, 1, 4, 0, 2, 3), (0, 0, 0, 5, 0), (0, 0, 1, 5, 0), (3, 14), (0, 0, 1, 6, 0, 14), (0, 0, 0, 6, 0, 14),
+        (0, 1, 0, 4, 2, 0, 3), (0, 1, 1, 4, 2, 0, 3), (0, 1, 0, 5, 0), (2, 0), (0, 0, 1, 13, 4, 2), (0, 1, 1, 5, 0),
+        (0, 0, 0, 13, 4, 2), (0, 1, 1, 6, 0, 14), (0, 0, 1, 11, 2, 3), (0, 1, 0, 6, 0, 14), (0, 0, 0, 11, 2, 3),
+        (0, 1, 1, 13, 4, 2), (2, 1), (0, 1, 0, 13, 4, 2), (0, 1, 1, 11, 3, 2), (0, 1, 0, 11, 3, 2), (2, 2), (2, 3),
         (2, 4),
     ),
     (
         (0, 0, 0, 2, 0, 4), (0, 0, 1, 2, 0, 4), (0, 0, 0, 1, 6, 3, 0), (0, 0, 1, 1, 6, 3, 0), (0, 1, 0, 2, 4, 0),
-        (0, 1, 1, 2, 4, 0), (0, 0, 0, 5, 3, 1), (0, 0, 1, 5, 3, 1), (0, 0, 1, 6, 1, 4), (0, 1, 0, 1, 6, 0, 3),
-        (0, 0, 0, 6, 1, 4), (0, 1, 1, 1, 6, 0, 3), (0, 0, 1, 7, 0, 1), (0, 0, 0, 7, 0, 1), (0, 1, 0, 5, 3, 1), (2, 0),
-        (0, 0, 1, 15, 1, 3, 0, 4), (0, 1, 1, 5, 3, 1), (0, 0, 1, 14, 4, 0, 1), (0, 0, 0, 15, 1, 3, 0, 4),
-        (0, 1, 1, 6, 4, 1), (0, 0, 0, 14, 4, 0, 1), (0, 1, 0, 6, 4, 1), (0, 1, 1, 7, 1, 0), (0, 1, 0, 7, 1, 0),
-        (0, 1, 1, 15, 0, 4, 3, 1), (2, 1), (0, 1, 1, 14, 1, 0, 4), (0, 1, 0, 15, 0, 4, 3, 1), (0, 1, 0, 14, 1, 0, 4),
+        (0, 1, 1, 2, 4, 0), (0, 0, 0, 5, 3, 1), (0, 0, 1, 5, 3, 1), (0, 0, 1, 6, 1, 4), (0, 0, 0, 6, 1, 4),
+        (0, 1, 0, 1, 6, 0, 3), (0, 1, 1, 1, 6, 0, 3), (0, 0, 1, 7, 0, 1), (0, 0, 0, 7, 0, 1), (0, 1, 0, 5, 3, 1),
+        (0, 1, 1, 5, 3, 1), (0, 0, 1, 15, 1, 3, 0, 4), (2, 0), (0, 0, 0, 15, 1, 3, 0, 4), (0, 0, 1, 14, 4, 0, 1),
+        (0, 1, 1, 6, 4, 1), (0, 1, 0, 6, 4, 1), (0, 0, 0, 14, 4, 0, 1), (0, 1, 1, 7, 1, 0), (0, 1, 0, 7, 1, 0),
+        (0, 1, 1, 15, 0, 4, 3, 1), (2, 1), (0, 1, 0, 15, 0, 4, 3, 1), (0, 1, 1, 14, 1, 0, 4), (0, 1, 0, 14, 1, 0, 4),
         (2, 2), (2, 3), (2, 4),
     ),
     (
-        (0, 0, 0, 3, 4, 6, 2, 0), (0, 0, 1, 3, 4, 6, 2, 0), (0, 0, 0, 0, 4), (0, 1, 0, 3, 4, 2, 0, 6),
-        (0, 1, 1, 3, 4, 2, 0, 6), (0, 0, 1, 0, 4), (3, 13), (3, 14), (0, 1, 0, 0, 4), (0, 0, 1, 8, 6, 2),
-        (0, 1, 1, 0, 4), (2, 0), (0, 0, 0, 8, 6, 2), (0, 0, 1, 12, 2, 14, 13, 4), (0, 1, 1, 8, 2, 6), (2, 1),
-        (0, 1, 0, 8, 2, 6), (0, 0, 0, 12, 2, 14, 13, 4), (0, 1, 1, 12, 2, 14, 13, 4), (0, 1, 0, 12, 2, 14, 13, 4),
-        (2, 2), (2, 3), (2, 4),
+        (0, 0, 0, 3, 4, 6, 2, 0), (0, 0, 1, 3, 4, 6, 2, 0), (0, 1, 0, 3, 4, 2, 0, 6), (0, 1, 1, 3, 4, 2, 0, 6),
+        (0, 0, 0, 0, 4), (0, 0, 1, 0, 4), (0, 1, 0, 0, 4), (3, 14), (3, 13), (0, 0, 0, 8, 6, 2), (0, 1, 1, 0, 4),
+        (0, 0, 1, 8, 6, 2), (2, 0), (0, 0, 1, 12, 2, 14, 13, 4), (0, 1, 0, 8, 2, 6), (0, 0, 0, 12, 2, 14, 13, 4),
+        (0, 1, 1, 8, 2, 6), (2, 1), (0, 1, 1, 12, 2, 14, 13, 4), (0, 1, 0, 12, 2, 14, 13, 4), (2, 2), (2, 3), (2, 4),
     ),
     (
         (0, 0, 0, 4, 6, 1), (0, 0, 1, 4, 6, 1), (0, 0, 0, 2, 7, 6, 5, 3), (0, 0, 1, 2, 7, 6, 5, 3),
-        (0, 1, 0, 4, 1, 6), (0, 1, 1, 4, 1, 6), (3, 14), (3, 15), (0, 1, 0, 2, 5, 3, 6, 7), (0, 1, 1, 2, 5, 3, 6, 7),
-        (0, 0, 1, 9, 3, 5, 2, 6), (0, 0, 0, 9, 3, 5, 2, 6), (0, 0, 1, 15, 5, 7), (2, 0), (0, 0, 1, 14, 7, 6, 3),
-        (0, 0, 0, 15, 5, 7), (0, 0, 0, 14, 7, 6, 3), (0, 1, 1, 9, 5, 6, 2, 3), (0, 0, 1, 13, 6, 3, 5),
-        (0, 1, 1, 15, 7, 5), (0, 1, 0, 9, 5, 6, 2, 3), (2, 1), (0, 0, 0, 13, 6, 3, 5), (0, 1, 1, 14, 6, 7, 3),
-        (0, 0, 0, 5, 15, 14, 6), (0, 1, 0, 15, 7, 5), (0, 1, 1, 13, 3, 5, 6), (0, 1, 0, 14, 6, 7, 3),
-        (0, 1, 0, 13, 3, 5, 6), (2, 2), (0, 0, 1, 5, 15, 14, 6), (0, 1, 0, 5, 15, 14, 6), (0, 1, 1, 5, 15, 14, 6),
-        (2, 3), (2, 4),
-    ),
-    (
-        (0, 0, 0, 5, 2), (0, 0, 1, 5, 2), (0, 0, 0, 1, 4, 7), (0, 0, 1, 1, 4, 7), (0, 0, 1, 7, 4, 3, 6),
-        (0, 1, 0, 5, 2), (0, 1, 1, 5, 2), (0, 0, 0, 7, 4, 3, 6), (3, 8), (1, 0, 0, 5, 8), (1, 0, 1, 5, 8),
-        (1, 1, 0, 5, 8), (1, 1, 1, 5, 8), (3, 10), (1, 0, 0, 1, 10), (1, 0, 1, 1, 10), (0, 1, 1, 7, 3, 4, 6),
-        (0, 1, 0, 1, 4, 7, 10), (0, 1, 1, 1, 4, 7, 10), (0, 1, 0, 7, 3, 4, 6), (2, 0), (0, 0, 1, 10, 3, 4, 2),
-        (0, 0, 0, 10, 3, 4, 2), (0, 1, 1, 10, 4, 2, 3), (0, 1, 0, 10, 4, 2, 3), (2, 1), (2, 2), (2, 3), (2, 4),
+        (0, 1, 0, 4, 1, 6), (0, 1, 1, 4, 1, 6), (0, 1, 0, 2, 5, 3, 6, 7), (0, 1, 1, 2, 5, 3, 6, 7), (3, 15), (3, 14),
+        (0, 0, 1, 9, 3, 5, 2, 6), (0, 0, 0, 9, 3, 5, 2, 6), (0, 0, 1, 15, 5, 7), (0, 0, 0, 15, 5, 7),
+        (0, 1, 1, 9, 5, 6, 2, 3), (2, 0), (0, 0, 1, 14, 7, 6, 3), (0, 1, 0, 9, 5, 6, 2, 3), (0, 0, 0, 14, 7, 6, 3),
+        (2, 1), (0, 0, 1, 13, 6, 3, 5), (0, 0, 0, 13, 6, 3, 5), (0, 1, 1, 15, 7, 5), (0, 1, 0, 15, 7, 5),
+        (0, 1, 1, 14, 6, 7, 3), (0, 0, 0, 5, 15, 14, 6), (0, 1, 0, 14, 6, 7, 3), (0, 1, 1, 13, 3, 5, 6),
+        (0, 1, 0, 13, 3, 5, 6), (0, 0, 1, 5, 15, 14, 6), (2, 2), (0, 1, 0, 5, 15, 14, 6), (2, 3),
+        (0, 1, 1, 5, 15, 14, 6), (2, 4),
+    ),
+    (
+        (0, 0, 0, 5, 2), (0, 0, 1, 5, 2), (0, 0, 0, 1, 4, 7), (0, 1, 0, 5, 2), (0, 1, 1, 5, 2), (0, 0, 1, 7, 4, 3, 6),
+        (0, 0, 1, 1, 4, 7), (0, 0, 0, 7, 4, 3, 6), (3, 8), (1, 0, 0, 5, 8), (1, 0, 1, 5, 8), (1, 1, 0, 5, 8),
+        (1, 1, 1, 5, 8), (3, 10), (1, 0, 0, 1, 10), (1, 0, 1, 1, 10), (0, 1, 1, 7, 3, 4, 6), (0, 1, 0, 1, 4, 7, 10),
+        (0, 1, 0, 7, 3, 4, 6), (0, 1, 1, 1, 4, 7, 10), (2, 0), (0, 0, 1, 10, 3, 4, 2), (0, 0, 0, 10, 3, 4, 2),
+        (0, 1, 1, 10, 4, 2, 3), (0, 1, 0, 10, 4, 2, 3), (2, 1), (2, 2), (2, 3), (2, 4),
     ),
     (
         (0, 0, 1, 6, 5, 2, 7), (0, 0, 0, 6, 5, 2, 7), (0, 0, 0, 3, 7), (0, 0, 0, 4, 7, 5), (0, 0, 1, 4, 7, 5),
         (0, 0, 1, 3, 7), (0, 1, 1, 6, 5, 2, 7), (0, 1, 0, 6, 5, 2, 7), (3, 9), (1, 0, 0, 4, 9), (1, 0, 1, 4, 9),
-        (3, 8), (1, 0, 0, 3, 8), (1, 0, 1, 3, 8), (0, 0, 1, 10, 7, 5), (0, 0, 1, 11, 5, 4, 8), (0, 0, 0, 10, 7, 5),
-        (0, 1, 0, 3, 7, 8), (0, 1, 0, 4, 5, 7, 9), (0, 1, 1, 4, 5, 7, 9), (0, 0, 0, 11, 5, 4, 8), (0, 1, 1, 3, 7, 8),
-        (0, 1, 1, 10, 7, 5), (0, 1, 0, 10, 7, 5), (2, 0), (0, 0, 1, 8, 5, 4, 7), (0, 1, 1, 11, 8, 4, 5),
-        (0, 0, 0, 8, 5, 4, 7), (0, 1, 1, 8, 4, 5, 7), (0, 0, 1, 13, 9, 8, 7), (0, 1, 0, 8, 4, 5, 7), (2, 1),
-        (0, 1, 0, 11, 8, 4, 5), (0, 0, 0, 13, 9, 8, 7), (0, 1, 1, 13, 9, 8, 7), (2, 2), (0, 1, 0, 13, 9, 8, 7),
-        (2, 3), (2, 4),
-    ),
-    (
-        (0, 0, 1, 7, 5, 2), (0, 0, 0, 7, 5, 2), (0, 0, 1, 6, 3), (0, 0, 0, 6, 3), (3, 9), (1, 0, 1, 6, 9),
-        (1, 0, 0, 6, 9), (0, 1, 1, 7, 5, 2), (3, 8), (1, 0, 1, 7, 8), (1, 0, 0, 7, 8), (1, 0, 1, 6, 8),
-        (1, 0, 0, 6, 8), (1, 1, 1, 7, 8), (3, 10), (1, 0, 1, 7, 10), (1, 0, 0, 7, 10), (1, 1, 1, 7, 10),
-        (0, 1, 0, 7, 8, 5, 10, 2), (0, 1, 1, 6, 8, 3, 9), (0, 1, 0, 6, 8, 3, 9), (2, 0), (2, 1),
-        (0, 0, 1, 15, 9, 10, 8, 6), (0, 0, 0, 15, 9, 10, 8, 6), (0, 1, 1, 15, 9, 6, 10, 8), (2, 2),
-        (0, 1, 0, 15, 9, 6, 10, 8), (2, 3), (2, 4),
-    ),
-    (
-        (0, 0, 1, 8, 9, 12, 10, 3, 11), (0, 0, 0, 8, 9, 12, 10, 3, 11), (0, 1, 1, 8, 9, 11, 3, 12, 10),
-        (0, 1, 0, 8, 9, 11, 3, 12, 10), (0, 0, 0, 3, 10, 13, 5, 9), (0, 0, 1, 3, 10, 13, 5, 9), (2, 0),
-        (0, 0, 0, 5, 11, 4, 9, 7), (0, 0, 1, 5, 11, 4, 9, 7), (0, 1, 0, 5, 7, 11, 9, 4), (0, 1, 1, 5, 7, 11, 9, 4),
-        (0, 1, 0, 3, 13, 9, 5, 10), (0, 1, 1, 3, 13, 9, 5, 10), (2, 1), (0, 0, 0, 0, 6, 7, 9), (0, 0, 1, 0, 6, 7, 9),
-        (0, 1, 0, 0, 9, 7, 6), (0, 1, 1, 0, 9, 7, 6), (2, 2), (2, 3), (2, 4),
+        (3, 8), (1, 0, 0, 3, 8), (1, 0, 1, 3, 8), (0, 1, 0, 3, 7, 8), (0, 1, 0, 4, 5, 7, 9), (0, 1, 1, 4, 5, 7, 9),
+        (0, 0, 1, 10, 7, 5), (0, 0, 0, 10, 7, 5), (0, 1, 1, 3, 7, 8), (0, 0, 1, 11, 5, 4, 8), (0, 0, 0, 11, 5, 4, 8),
+        (0, 1, 1, 10, 7, 5), (0, 1, 0, 10, 7, 5), (2, 0), (0, 1, 1, 11, 8, 4, 5), (0, 0, 0, 8, 5, 4, 7),
+        (0, 0, 1, 8, 5, 4, 7), (0, 1, 0, 11, 8, 4, 5), (2, 1), (0, 1, 0, 8, 4, 5, 7), (0, 0, 1, 13, 9, 8, 7),
+        (0, 0, 0, 13, 9, 8, 7), (0, 1, 1, 8, 4, 5, 7), (0, 1, 1, 13, 9, 8, 7), (2, 2), (0, 1, 0, 13, 9, 8, 7), (2, 3),
+        (2, 4),
+    ),
+    (
+        (0, 0, 1, 7, 5, 2), (0, 0, 0, 7, 5, 2), (0, 0, 1, 6, 3), (0, 0, 0, 6, 3), (0, 1, 1, 7, 5, 2), (3, 9),
+        (1, 0, 1, 6, 9), (1, 0, 0, 6, 9), (0, 1, 0, 7, 5, 2), (3, 8), (1, 0, 1, 7, 8), (1, 0, 0, 7, 8),
+        (1, 0, 1, 6, 8), (1, 0, 0, 6, 8), (1, 1, 1, 7, 8), (1, 1, 0, 7, 8), (3, 10), (1, 0, 1, 7, 10),
+        (1, 0, 0, 7, 10), (1, 1, 1, 7, 10), (1, 1, 0, 7, 10), (0, 1, 1, 6, 8, 3, 9), (0, 1, 0, 6, 8, 3, 9), (2, 0),
+        (0, 0, 1, 15, 9, 10, 8, 6), (0, 0, 0, 15, 9, 10, 8, 6), (2, 1), (0, 1, 1, 15, 9, 6, 10, 8),
+        (0, 1, 0, 15, 9, 6, 10, 8), (2, 2), (2, 3), (2, 4),
+    ),
+    (
+        (0, 0, 0, 8, 9, 12, 10, 3, 11), (0, 0, 1, 8, 9, 12, 10, 3, 11), (0, 1, 0, 8, 9, 11, 3, 12, 10),
+        (0, 1, 1, 8, 9, 11, 3, 12, 10), (0, 0, 0, 3, 10, 13, 5, 9), (0, 0, 1, 3, 10, 13, 5, 9),
+        (0, 0, 0, 5, 11, 4, 9, 7), (2, 0), (0, 0, 1, 5, 11, 4, 9, 7), (0, 1, 0, 5, 7, 11, 9, 4),
+        (0, 1, 0, 3, 13, 9, 5, 10), (0, 1, 1, 5, 7, 11, 9, 4), (0, 1, 1, 3, 13, 9, 5, 10), (2, 1),
+        (0, 0, 0, 0, 6, 7, 9), (0, 0, 1, 0, 6, 7, 9), (0, 1, 0, 0, 9, 7, 6), (0, 1, 1, 0, 9, 7, 6), (2, 2), (2, 3),
+        (2, 4),
     ),
     (
         (0, 0, 1, 9, 7, 8, 10, 4, 12), (0, 0, 0, 9, 7, 8, 10, 4, 12), (0, 1, 1, 9, 4, 7, 8, 12, 10),
         (0, 1, 0, 9, 4, 7, 8, 12, 10), (0, 0, 1, 12, 7, 6, 5, 8), (0, 0, 0, 12, 7, 6, 5, 8), (0, 0, 0, 4, 8, 10, 12),
         (0, 0, 1, 4, 8, 10, 12), (2, 0), (0, 1, 1, 12, 5, 8, 6, 7), (0, 1, 0, 12, 5, 8, 6, 7),
-        (0, 1, 0, 4, 12, 10, 8), (2, 1), (0, 1, 1, 4, 12, 10, 8), (0, 0, 0, 2, 11, 10, 8, 12),
-        (0, 0, 1, 2, 11, 10, 8, 12), (0, 1, 0, 2, 11, 8, 12, 10), (0, 1, 1, 2, 11, 8, 12, 10), (2, 2), (2, 3), (2, 4),
+        (0, 1, 0, 4, 12, 10, 8), (0, 1, 1, 4, 12, 10, 8), (0, 0, 0, 2, 11, 10, 8, 12), (0, 0, 1, 2, 11, 10, 8, 12),
+        (2, 1), (0, 1, 0, 2, 11, 8, 12, 10), (0, 1, 1, 2, 11, 8, 12, 10), (2, 2), (2, 3), (2, 4),
     ),
     (
         (0, 0, 1, 10, 12, 9, 6, 0, 11, 8), (0, 0, 0, 10, 12, 9, 6, 0, 11, 8), (0, 1, 1, 10, 6, 11, 8, 0, 12, 9),
         (0, 1, 0, 10, 6, 11, 8, 0, 12, 9), (0, 0, 1, 7, 13, 9), (0, 0, 1, 14, 9, 12, 11, 5), (0, 0, 0, 7, 13, 9),
-        (0, 1, 1, 7, 13, 9), (2, 0), (0, 1, 0, 7, 13, 9), (0, 0, 0, 14, 9, 12, 11, 5), (0, 1, 1, 14, 9, 12, 11, 5),
-        (0, 1, 0, 14, 9, 12, 11, 5), (0, 0, 0, 1, 12, 8, 9, 11), (2, 1), (0, 0, 1, 1, 12, 8, 9, 11),
+        (0, 1, 1, 7, 13, 9), (0, 0, 0, 14, 9, 12, 11, 5), (0, 1, 0, 7, 13, 9), (2, 0), (0, 1, 1, 14, 9, 12, 11, 5),
+        (0, 1, 0, 14, 9, 12, 11, 5), (2, 1), (0, 0, 0, 1, 12, 8, 9, 11), (0, 0, 1, 1, 12, 8, 9, 11),
         (0, 1, 0, 1, 9, 12, 8, 11), (0, 1, 1, 1, 9, 12, 8, 11), (2, 2), (2, 3), (2, 4),
     ),
     (
@@ -155,34 +155,53 @@
     ),
     (
         (0, 0, 1, 12, 10, 0, 11, 9), (0, 0, 0, 12, 10, 0, 11, 9), (0, 1, 1, 12, 10, 9, 0, 11), (0, 0, 1, 9, 11, 15),
-        (0, 1, 0, 12, 10, 9, 0, 11), (0, 0, 0, 9, 11, 15), (0, 0, 1, 8, 14, 0, 13), (0, 0, 0, 8, 14, 0, 13),
-        (0, 1, 1, 9, 11, 15), (2, 0), (0, 1, 0, 9, 11, 15), (0, 1, 1, 8, 0, 14, 13), (0, 0, 0, 0, 14, 10, 15, 11),
-        (0, 1, 0, 8, 0, 14, 13), (0, 0, 1, 0, 14, 10, 15, 11), (0, 1, 0, 0, 11, 15, 10, 14),
-        (0, 1, 1, 0, 11, 15, 10, 14), (0, 0, 0, 4, 13, 11, 15, 14), (0, 0, 1, 4, 13, 11, 15, 14), (2, 1),
+        (0, 1, 0, 12, 10, 9, 0, 11), (0, 0, 0, 9, 11, 15), (0, 0, 0, 8, 14, 0, 13), (0, 0, 1, 8, 14, 0, 13),
+        (0, 1, 1, 9, 11, 15), (0, 1, 0, 9, 11, 15), (0, 1, 0, 8, 0, 14, 13), (2, 0), (0, 1, 1, 8, 0, 14, 13),
+        (0, 0, 0, 0, 14, 10, 15, 11), (0, 0, 1, 0, 14, 10, 15, 11), (0, 0, 0, 4, 13, 11, 15, 14),
+        (0, 0, 1, 4, 13, 11, 15, 14), (0, 1, 0, 0, 11, 15, 10, 14), (0, 1, 1, 0, 11, 15, 10, 14), (2, 1),
         (0, 1, 0, 4, 11, 14, 13, 15), (0, 1, 1, 4, 11, 14, 13, 15), (2, 2), (2, 3), (2, 4),
     ),
     (
         (0, 0, 1, 13, 11, 12, 0, 14, 10), (0, 0, 0, 13, 11, 12, 0, 14, 10), (0, 1, 1, 13, 0, 12, 11, 14, 10),
-        (0, 1, 0, 13, 0, 12, 11, 14, 10), (0, 0, 0, 0, 12, 8), (0, 0, 1, 0, 12, 8), (0, 1, 0, 0, 12, 8),
-        (0, 1, 1, 0, 12, 8), (0, 0, 1, 7, 12, 14, 15, 11), (2, 0), (0, 0, 0, 7, 12, 14, 15, 11),
-        (0, 1, 1, 7, 11, 12, 15, 14), (0, 0, 1, 6, 12), (0, 0, 0, 3, 11, 14, 12, 15), (0, 1, 0, 7, 11, 12, 15, 14),
-        (2, 1), (0, 0, 0, 6, 12), (0, 0, 1, 3, 11, 14, 12, 15), (0, 1, 1, 6, 12), (0, 1, 0, 3, 15, 14, 11, 12),
-        (0, 1, 0, 6, 12), (0, 1, 1, 3, 15, 14, 11, 12), (2, 2), (2, 3), (2, 4),
+        (0, 1, 0, 13, 0, 12, 11, 14, 10), (0, 0, 0, 0, 12, 8), (0, 0, 1, 7, 12, 14, 15, 11), (0, 0, 1, 0, 12, 8),
+        (0, 1, 0, 0, 12, 8), (0, 1, 1, 0, 12, 8), (0, 0, 0, 7, 12, 14, 15, 11), (0, 1, 1, 7, 11, 12, 15, 14), (2, 0),
+        (0, 1, 0, 7, 11, 12, 15, 14), (0, 0, 0, 3, 11, 14, 12, 15), (0, 0, 1, 3, 11, 14, 12, 15), (0, 0, 1, 6, 12),
+        (2, 1), (0, 0, 0, 6, 12), (0, 1, 1, 6, 12), (0, 1, 0, 6, 12), (0, 1, 0, 3, 15, 14, 11, 12), (2, 2),
+        (0, 1, 1, 3, 15, 14, 11, 12), (2, 3), (2, 4),
     ),
     (
         (0, 0, 1, 14, 8, 10, 15, 13, 2), (0, 0, 0, 14, 8, 10, 15, 13, 2), (0, 1, 1, 14, 10, 8, 15, 2, 13),
         (0, 1, 0, 14, 10, 8, 15, 2, 13), (0, 0, 0, 2, 9, 13, 15), (0, 0, 1, 2, 9, 13, 15), (0, 0, 0, 1, 15),
-        (0, 0, 1, 1, 15), (0, 1, 0, 2, 15, 9, 13), (0, 1, 1, 2, 15, 9, 13), (2, 0), (0, 0, 1, 6, 13, 10, 15, 11),
-        (0, 1, 0, 1, 15), (0, 1, 1, 1, 15), (0, 0, 0, 6, 13, 10, 15, 11), (0, 1, 1, 6, 10, 13, 11, 15),
+        (0, 0, 1, 1, 15), (0, 1, 0, 2, 15, 9, 13), (0, 1, 1, 2, 15, 9, 13), (0, 0, 1, 6, 13, 10, 15, 11),
+        (0, 1, 0, 1, 15), (2, 0), (0, 0, 0, 6, 13, 10, 15, 11), (0, 1, 1, 1, 15), (0, 1, 1, 6, 10, 13, 11, 15),
         (0, 1, 0, 6, 10, 13, 11, 15), (2, 1), (2, 2), (2, 3), (2, 4),
     ),
     (
         (0, 0, 1, 15, 12, 11, 14, 2, 13), (0, 0, 0, 15, 12, 11, 14, 2, 13), (0, 1, 1, 15, 2, 14, 11, 13, 12),
         (0, 1, 0, 15, 2, 14, 11, 13, 12), (0, 0, 1, 9, 14, 0, 13, 1), (0, 0, 0, 9, 14, 0, 13, 1),
-        (0, 0, 1, 11, 14, 13), (0, 0, 1, 10, 14, 13), (0, 0, 0, 11, 14, 13), (0, 0, 0, 10, 14, 13),
-        (0, 1, 1, 9, 1, 0, 14, 13), (0, 1, 1, 11, 13, 14), (0, 1, 0, 9, 1, 0, 14, 13), (2, 0), (0, 1, 1, 10, 13, 14),
-        (0, 1, 0, 11, 13, 14), (2, 1), (0, 1, 0, 10, 13, 14), (2, 2), (2, 3), (2, 4),
-    ),
+        (0, 0, 1, 11, 14, 13), (0, 0, 0, 11, 14, 13), (0, 0, 1, 10, 14, 13), (0, 0, 0, 10, 14, 13),
+        (0, 1, 1, 9, 1, 0, 14, 13), (0, 1, 0, 9, 1, 0, 14, 13), (2, 0), (0, 1, 1, 11, 13, 14), (0, 1, 0, 11, 13, 14),
+        (0, 1, 1, 10, 13, 14), (0, 1, 0, 10, 13, 14), (2, 1), (2, 2), (2, 3), (2, 4),
+    ),
+)
+
+ASIDE = (
+    (),
+    (),
+    (),
+    (),
+    (),
+    (),
+    (),
+    (),
+    (),
+    (),
+    (),
+    (),
+    (),
+    (),
+    (),
+    (),
 )
 
 SLOT = [{source: i for i, source in enumerate(order)} for order in ORDER]
@@ -233,11 +252,11 @@
 PLAN_Q = (
     ("ring",),
     ("attend", 2), ("attend", 1), ("attend", 3),
-    ("w_passed", 0), ("piece", 0, 1), ("w_passed", 1), ("piece", 1, 1),
-    ("q_last",), ("k_last",), ("attend", 0),
-    ("piece", 0, 0), ("piece", 1, 0),
-    ("reduced", 0, 2), ("reduced", 0, 1), ("reduced", 0, 3), ("reduced", 1, 2), ("reduced", 1, 1), ("reduced", 1, 3),
-    ("reduced", 0, 0), ("reduced", 1, 0),
+    ("w_passed", 0), ("piece", 0, 1),
+    ("q_last",), ("k_last",), ("attend", 0), ("piece", 0, 0),
+    ("w_passed", 1), ("piece", 1, 2),
+    ("reduced", 0, 2), ("reduced", 0, 1), ("reduced", 0, 3), ("reduced", 0, 0),
+    ("reduced", 1, 2), ("reduced", 1, 1), ("reduced", 1, 3), ("reduced", 1, 0),
 )
 
 PLAN_W = (
@@ -326,6 +345,9 @@
             for other in range(16):
                 if place in FIRST[other]:
                     pl.semaphore_signal(barrier, inc=1, device_id=dev(to_z=other, role=WC), device_id_type=MESH)
+                if place in ASIDE[other]:
+                    to = dev(dy=4, to_z=other, role=WC)
+                    pl.semaphore_signal(barrier, inc=1, device_id=to, device_id_type=MESH)
 
         by_place(z, greet)
 
@@ -354,7 +376,10 @@
             to = dev(to_z=t, role=WC)
             send(unit(here, wave, core), unit(there, wave, core), w_sem(t, wave, core, source), to)
 
-    def w_cross(core):
+    def w_cross(place, core):
+        for t in ASIDE[place]:
+            there = wall.at[SLOT[t][place], :, lanes_of(yh, core)]
+            send(wcross.at[core], there, w_sem(t, 1, core, place), dev(dy=4, to_z=t, role=WC))
         send(wcross.at[core], wall.at[0, :, lanes_of(yh, core)], rsem.at[2 + core], dev(dy=4, role=WC))
 
     waited = []
@@ -381,7 +406,7 @@
                 if (core == QC or place == 0) and place not in waited:
                     received(sized(65536), rsem.at[4])
                     waited.append(place)
-                w_cross(core)
+                w_cross(place, core)
         w_sends(place, wave, core, source, targets)
 
     def w_route(part):
@@ -527,7 +552,7 @@
         once(~origin, None, meet)
 
         def greeted(place):
-            pl.semaphore_wait(barrier, 2 + len(FIRST[place]) - one_more)
+            pl.semaphore_wait(barrier, 2 + len(FIRST[place]) + len(ASIDE[place]) - one_more)
             for other in range(8):
                 if (3, place) in ROUTES[other]:
                     to = dev(to_z=other, role=WC)
@@ -568,13 +593,13 @@
             dst = xr.at[p % 2, gs, d - 1, :, :, lanes]
             send(src, dst, xsem.at[p % 2, gs], dev(dx=d, role=QC if p < 2 else WC))
 
-    def piece(p, most):
-        groups = slice(1, 4) if most else slice(0, 1)
-        n = 3 if most else 1
+    def piece(p, which):
+        groups = (slice(0, 1), slice(1, 4), slice(0, 4))[which]
+        n = groups.stop - groups.start
         rows = wall[4 * p : 4 * p + 4].reshape(256, 1024)
         total = lax.dot_general(att[groups].reshape(n * 256, 1024), rows, NT, preferred_element_type=F32)
         psend[p, groups] = total.astype(BF16).reshape(n, 2, 4, 32, 256)
-        for gs in (2, 1, 3) if most else (0,):
+        for gs in ((0,), (2, 1, 3), (2, 1, 3, 0))[which]:
             spread(p, gs, pl.ds(0, 256))
 
     def w_piece(p, slot, n):

time: 59.5 us -> 58.8 us (0.988)
  the two profiles are of different devices: /device:TPU:3 before, /device:TPU:1 now
where the time goes in v4:
time: 58.8 us; the launch traced here: 58.6 us
  Pallas kernels  57.8 us (98%)
  between operations  0.82 us (1%)
    pallas_call x1, Pallas kernels, local(): pl.pallas_call(kernel, out_shape=jax.ShapeDtypeStruct((PIECES, 8, 16, 256...  55.6 us
    pallas_call x1, Pallas kernels, local(): pl.pallas_call(last_kernel, out_shape=(jax.ShapeDtypeStruct((16, 8192), B...  2.25 us

profile of v4, /device:TPU:1, one launch (start us, length us, event | category | flops | bytes accessed | tf_op | source)
XLA Modules:
  0.0 58.6 jit_solution(1151646672200768960)
XLA Ops:
  0.6 55.6 %layer.1.sums = bf16[4,8,16,256]{3,2,1,0:T(8,128)(2,1)} custom-call(bf16[256,256]{1,0:T(8,128)(2,1)} %q.1, bf16[16,512]{1,0:T(8,128)(2,1)} %k.1, bf16[16,512]{1,0:T(8,128)(2,1)} %v.1, bf16[256,128]{1,0:T(8,128)(2,1)} %w.1), custom_call_target="tpu_custom_call" | custom-call | tf_op jit(solution)/shard_map/layer/pallas_call | solution.py:738
  56.2 2.3 %final.1 = (bf16[16,8192]{1,0:T(8,128)(2,1)}, bf16[16,8192]{1,0:T(8,128)(2,1)}) custom-call(bf16[4,8,16,256]{3,2,1,0:T(8,128)(2,1)} %layer.1.sums, bf16[16,8192]{1,0:T(8,128)(2,1)} %res.1, f32[64,128]{1,0:T(8,128)} %bitcast.1), custom_call_target="tpu_custom_call" | custom-call | tf_op jit(solution)/shard_map/final/pallas_call | solution.py:771

commit v5 on v4

--- a/solution.py
+++ b/solution.py
@@ -62,41 +62,42 @@
         (1, 0, 1, 1, 14), (1, 1, 0, 2, 14), (3, 13), (1, 0, 0, 0, 13), (1, 0, 1, 0, 13), (1, 1, 0, 0, 13),
         (1, 1, 1, 0, 13), (1, 0, 0, 1, 13), (1, 0, 1, 1, 13), (0, 1, 1, 2, 1, 14), (0, 1, 0, 3, 1), (0, 1, 1, 3, 1),
         (0, 0, 1, 13, 15, 1), (0, 1, 0, 1, 14, 13), (0, 0, 1, 12, 15, 3, 1), (0, 0, 0, 13, 15, 1),
-        (0, 1, 1, 1, 14, 13), (0, 0, 0, 12, 15, 3, 1), (0, 0, 1, 11, 15, 1), (0, 0, 0, 11, 15, 1), (2, 0),
+        (0, 1, 1, 1, 14, 13), (0, 0, 0, 12, 15, 3, 1), (2, 0), (0, 0, 1, 11, 15, 1), (0, 0, 0, 11, 15, 1),
         (0, 0, 1, 10, 1, 15), (0, 0, 0, 10, 1, 15), (0, 1, 1, 13, 1, 15), (0, 1, 1, 12, 15, 3, 1),
-        (0, 1, 0, 13, 1, 15), (0, 1, 0, 12, 15, 3, 1), (0, 1, 1, 11, 15, 1), (2, 1), (0, 1, 0, 11, 15, 1),
-        (0, 0, 0, 8, 15, 1), (0, 1, 1, 10, 1, 15), (0, 0, 1, 8, 15, 1), (0, 1, 0, 10, 1, 15), (2, 2),
+        (0, 1, 0, 13, 1, 15), (0, 1, 0, 12, 15, 3, 1), (2, 1), (0, 1, 1, 11, 15, 1), (0, 1, 0, 11, 15, 1),
+        (0, 0, 0, 8, 15, 1), (0, 1, 1, 10, 1, 15), (0, 0, 1, 8, 15, 1), (2, 2), (0, 1, 0, 10, 1, 15),
         (0, 1, 0, 8, 1, 15), (2, 3), (0, 1, 1, 8, 1, 15), (2, 4),
     ),
     (
         (0, 0, 0, 1, 5, 2), (0, 0, 1, 1, 5, 2), (0, 1, 0, 1, 5, 2), (0, 1, 1, 1, 5, 2), (0, 0, 0, 4, 0, 2, 3),
         (0, 0, 1, 4, 0, 2, 3), (0, 0, 0, 5, 0), (0, 0, 1, 5, 0), (3, 14), (0, 0, 1, 6, 0, 14), (0, 0, 0, 6, 0, 14),
-        (0, 1, 0, 4, 2, 0, 3), (0, 1, 1, 4, 2, 0, 3), (0, 1, 0, 5, 0), (2, 0), (0, 0, 1, 13, 4, 2), (0, 1, 1, 5, 0),
+        (0, 1, 0, 4, 2, 0, 3), (0, 1, 1, 4, 2, 0, 3), (2, 0), (0, 1, 0, 5, 0), (0, 0, 1, 13, 4, 2), (0, 1, 1, 5, 0),
         (0, 0, 0, 13, 4, 2), (0, 1, 1, 6, 0, 14), (0, 0, 1, 11, 2, 3), (0, 1, 0, 6, 0, 14), (0, 0, 0, 11, 2, 3),
-        (0, 1, 1, 13, 4, 2), (2, 1), (0, 1, 0, 13, 4, 2), (0, 1, 1, 11, 3, 2), (0, 1, 0, 11, 3, 2), (2, 2), (2, 3),
+        (2, 1), (0, 1, 1, 13, 4, 2), (0, 1, 0, 13, 4, 2), (0, 1, 1, 11, 3, 2), (2, 2), (0, 1, 0, 11, 3, 2), (2, 3),
         (2, 4),
     ),
     (
         (0, 0, 0, 2, 0, 4), (0, 0, 1, 2, 0, 4), (0, 0, 0, 1, 6, 3, 0), (0, 0, 1, 1, 6, 3, 0), (0, 1, 0, 2, 4, 0),
         (0, 1, 1, 2, 4, 0), (0, 0, 0, 5, 3, 1), (0, 0, 1, 5, 3, 1), (0, 0, 1, 6, 1, 4), (0, 0, 0, 6, 1, 4),
         (0, 1, 0, 1, 6, 0, 3), (0, 1, 1, 1, 6, 0, 3), (0, 0, 1, 7, 0, 1), (0, 0, 0, 7, 0, 1), (0, 1, 0, 5, 3, 1),
-        (0, 1, 1, 5, 3, 1), (0, 0, 1, 15, 1, 3, 0, 4), (2, 0), (0, 0, 0, 15, 1, 3, 0, 4), (0, 0, 1, 14, 4, 0, 1),
+        (0, 1, 1, 5, 3, 1), (2, 0), (0, 0, 1, 15, 1, 3, 0, 4), (0, 0, 0, 15, 1, 3, 0, 4), (0, 0, 1, 14, 4, 0, 1),
         (0, 1, 1, 6, 4, 1), (0, 1, 0, 6, 4, 1), (0, 0, 0, 14, 4, 0, 1), (0, 1, 1, 7, 1, 0), (0, 1, 0, 7, 1, 0),
-        (0, 1, 1, 15, 0, 4, 3, 1), (2, 1), (0, 1, 0, 15, 0, 4, 3, 1), (0, 1, 1, 14, 1, 0, 4), (0, 1, 0, 14, 1, 0, 4),
+        (2, 1), (0, 1, 1, 15, 0, 4, 3, 1), (0, 1, 0, 15, 0, 4, 3, 1), (0, 1, 1, 14, 1, 0, 4), (0, 1, 0, 14, 1, 0, 4),
         (2, 2), (2, 3), (2, 4),
     ),
     (
         (0, 0, 0, 3, 4, 6, 2, 0), (0, 0, 1, 3, 4, 6, 2, 0), (0, 1, 0, 3, 4, 2, 0, 6), (0, 1, 1, 3, 4, 2, 0, 6),
         (0, 0, 0, 0, 4), (0, 0, 1, 0, 4), (0, 1, 0, 0, 4), (3, 14), (3, 13), (0, 0, 0, 8, 6, 2), (0, 1, 1, 0, 4),
-        (0, 0, 1, 8, 6, 2), (2, 0), (0, 0, 1, 12, 2, 14, 13, 4), (0, 1, 0, 8, 2, 6), (0, 0, 0, 12, 2, 14, 13, 4),
-        (0, 1, 1, 8, 2, 6), (2, 1), (0, 1, 1, 12, 2, 14, 13, 4), (0, 1, 0, 12, 2, 14, 13, 4), (2, 2), (2, 3), (2, 4),
+        (2, 0), (0, 0, 1, 8, 6, 2), (0, 0, 1, 12, 2, 14, 13, 4), (2, 1), (0, 1, 0, 8, 2, 6),
+        (0, 0, 0, 12, 2, 14, 13, 4), (0, 1, 1, 8, 2, 6), (0, 1, 1, 12, 2, 14, 13, 4), (0, 1, 0, 12, 2, 14, 13, 4),
+        (2, 2), (2, 3), (2, 4),
     ),
     (
         (0, 0, 0, 4, 6, 1), (0, 0, 1, 4, 6, 1), (0, 0, 0, 2, 7, 6, 5, 3), (0, 0, 1, 2, 7, 6, 5, 3),
         (0, 1, 0, 4, 1, 6), (0, 1, 1, 4, 1, 6), (0, 1, 0, 2, 5, 3, 6, 7), (0, 1, 1, 2, 5, 3, 6, 7), (3, 15), (3, 14),
-        (0, 0, 1, 9, 3, 5, 2, 6), (0, 0, 0, 9, 3, 5, 2, 6), (0, 0, 1, 15, 5, 7), (0, 0, 0, 15, 5, 7),
-        (0, 1, 1, 9, 5, 6, 2, 3), (2, 0), (0, 0, 1, 14, 7, 6, 3), (0, 1, 0, 9, 5, 6, 2, 3), (0, 0, 0, 14, 7, 6, 3),
-        (2, 1), (0, 0, 1, 13, 6, 3, 5), (0, 0, 0, 13, 6, 3, 5), (0, 1, 1, 15, 7, 5), (0, 1, 0, 15, 7, 5),
+        (0, 0, 1, 9, 3, 5, 2, 6), (0, 0, 0, 9, 3, 5, 2, 6), (0, 0, 1, 15, 5, 7), (2, 0), (0, 0, 0, 15, 5, 7),
+        (0, 1, 1, 9, 5, 6, 2, 3), (0, 0, 1, 14, 7, 6, 3), (0, 1, 0, 9, 5, 6, 2, 3), (2, 1), (0, 0, 0, 14, 7, 6, 3),
+        (0, 0, 1, 13, 6, 3, 5), (0, 0, 0, 13, 6, 3, 5), (0, 1, 1, 15, 7, 5), (0, 1, 0, 15, 7, 5),
         (0, 1, 1, 14, 6, 7, 3), (0, 0, 0, 5, 15, 14, 6), (0, 1, 0, 14, 6, 7, 3), (0, 1, 1, 13, 3, 5, 6),
         (0, 1, 0, 13, 3, 5, 6), (0, 0, 1, 5, 15, 14, 6), (2, 2), (0, 1, 0, 5, 15, 14, 6), (2, 3),
         (0, 1, 1, 5, 15, 14, 6), (2, 4),
@@ -115,7 +116,7 @@
         (0, 0, 1, 10, 7, 5), (0, 0, 0, 10, 7, 5), (0, 1, 1, 3, 7, 8), (0, 0, 1, 11, 5, 4, 8), (0, 0, 0, 11, 5, 4, 8),
         (0, 1, 1, 10, 7, 5), (0, 1, 0, 10, 7, 5), (2, 0), (0, 1, 1, 11, 8, 4, 5), (0, 0, 0, 8, 5, 4, 7),
         (0, 0, 1, 8, 5, 4, 7), (0, 1, 0, 11, 8, 4, 5), (2, 1), (0, 1, 0, 8, 4, 5, 7), (0, 0, 1, 13, 9, 8, 7),
-        (0, 0, 0, 13, 9, 8, 7), (0, 1, 1, 8, 4, 5, 7), (0, 1, 1, 13, 9, 8, 7), (2, 2), (0, 1, 0, 13, 9, 8, 7), (2, 3),
+        (0, 0, 0, 13, 9, 8, 7), (0, 1, 1, 8, 4, 5, 7), (2, 2), (0, 1, 1, 13, 9, 8, 7), (0, 1, 0, 13, 9, 8, 7), (2, 3),
         (2, 4),
     ),
     (
@@ -123,40 +124,39 @@
         (1, 0, 1, 6, 9), (1, 0, 0, 6, 9), (0, 1, 0, 7, 5, 2), (3, 8), (1, 0, 1, 7, 8), (1, 0, 0, 7, 8),
         (1, 0, 1, 6, 8), (1, 0, 0, 6, 8), (1, 1, 1, 7, 8), (1, 1, 0, 7, 8), (3, 10), (1, 0, 1, 7, 10),
         (1, 0, 0, 7, 10), (1, 1, 1, 7, 10), (1, 1, 0, 7, 10), (0, 1, 1, 6, 8, 3, 9), (0, 1, 0, 6, 8, 3, 9), (2, 0),
-        (0, 0, 1, 15, 9, 10, 8, 6), (0, 0, 0, 15, 9, 10, 8, 6), (2, 1), (0, 1, 1, 15, 9, 6, 10, 8),
+        (2, 1), (0, 0, 1, 15, 9, 10, 8, 6), (0, 0, 0, 15, 9, 10, 8, 6), (0, 1, 1, 15, 9, 6, 10, 8),
         (0, 1, 0, 15, 9, 6, 10, 8), (2, 2), (2, 3), (2, 4),
     ),
     (
         (0, 0, 0, 8, 9, 12, 10, 3, 11), (0, 0, 1, 8, 9, 12, 10, 3, 11), (0, 1, 0, 8, 9, 11, 3, 12, 10),
-        (0, 1, 1, 8, 9, 11, 3, 12, 10), (0, 0, 0, 3, 10, 13, 5, 9), (0, 0, 1, 3, 10, 13, 5, 9),
-        (0, 0, 0, 5, 11, 4, 9, 7), (2, 0), (0, 0, 1, 5, 11, 4, 9, 7), (0, 1, 0, 5, 7, 11, 9, 4),
-        (0, 1, 0, 3, 13, 9, 5, 10), (0, 1, 1, 5, 7, 11, 9, 4), (0, 1, 1, 3, 13, 9, 5, 10), (2, 1),
-        (0, 0, 0, 0, 6, 7, 9), (0, 0, 1, 0, 6, 7, 9), (0, 1, 0, 0, 9, 7, 6), (0, 1, 1, 0, 9, 7, 6), (2, 2), (2, 3),
-        (2, 4),
+        (0, 1, 1, 8, 9, 11, 3, 12, 10), (0, 0, 0, 3, 10, 13, 5, 9), (2, 0), (0, 0, 1, 3, 10, 13, 5, 9),
+        (0, 0, 0, 5, 11, 4, 9, 7), (0, 0, 1, 5, 11, 4, 9, 7), (0, 1, 0, 5, 7, 11, 9, 4), (0, 1, 0, 3, 13, 9, 5, 10),
+        (0, 1, 1, 5, 7, 11, 9, 4), (0, 1, 1, 3, 13, 9, 5, 10), (2, 1), (0, 0, 0, 0, 6, 7, 9), (0, 0, 1, 0, 6, 7, 9),
+        (0, 1, 0, 0, 9, 7, 6), (0, 1, 1, 0, 9, 7, 6), (2, 2), (2, 3), (2, 4),
     ),
     (
         (0, 0, 1, 9, 7, 8, 10, 4, 12), (0, 0, 0, 9, 7, 8, 10, 4, 12), (0, 1, 1, 9, 4, 7, 8, 12, 10),
         (0, 1, 0, 9, 4, 7, 8, 12, 10), (0, 0, 1, 12, 7, 6, 5, 8), (0, 0, 0, 12, 7, 6, 5, 8), (0, 0, 0, 4, 8, 10, 12),
-        (0, 0, 1, 4, 8, 10, 12), (2, 0), (0, 1, 1, 12, 5, 8, 6, 7), (0, 1, 0, 12, 5, 8, 6, 7),
-        (0, 1, 0, 4, 12, 10, 8), (0, 1, 1, 4, 12, 10, 8), (0, 0, 0, 2, 11, 10, 8, 12), (0, 0, 1, 2, 11, 10, 8, 12),
-        (2, 1), (0, 1, 0, 2, 11, 8, 12, 10), (0, 1, 1, 2, 11, 8, 12, 10), (2, 2), (2, 3), (2, 4),
+        (2, 0), (0, 0, 1, 4, 8, 10, 12), (0, 1, 1, 12, 5, 8, 6, 7), (0, 1, 0, 12, 5, 8, 6, 7),
+        (0, 1, 0, 4, 12, 10, 8), (0, 1, 1, 4, 12, 10, 8), (2, 1), (0, 0, 0, 2, 11, 10, 8, 12),
+        (0, 0, 1, 2, 11, 10, 8, 12), (0, 1, 0, 2, 11, 8, 12, 10), (0, 1, 1, 2, 11, 8, 12, 10), (2, 2), (2, 3), (2, 4),
     ),
     (
         (0, 0, 1, 10, 12, 9, 6, 0, 11, 8), (0, 0, 0, 10, 12, 9, 6, 0, 11, 8), (0, 1, 1, 10, 6, 11, 8, 0, 12, 9),
-        (0, 1, 0, 10, 6, 11, 8, 0, 12, 9), (0, 0, 1, 7, 13, 9), (0, 0, 1, 14, 9, 12, 11, 5), (0, 0, 0, 7, 13, 9),
-        (0, 1, 1, 7, 13, 9), (0, 0, 0, 14, 9, 12, 11, 5), (0, 1, 0, 7, 13, 9), (2, 0), (0, 1, 1, 14, 9, 12, 11, 5),
-        (0, 1, 0, 14, 9, 12, 11, 5), (2, 1), (0, 0, 0, 1, 12, 8, 9, 11), (0, 0, 1, 1, 12, 8, 9, 11),
-        (0, 1, 0, 1, 9, 12, 8, 11), (0, 1, 1, 1, 9, 12, 8, 11), (2, 2), (2, 3), (2, 4),
+        (0, 1, 0, 10, 6, 11, 8, 0, 12, 9), (0, 0, 1, 7, 13, 9), (0, 0, 1, 14, 9, 12, 11, 5), (2, 0),
+        (0, 0, 0, 7, 13, 9), (0, 1, 1, 7, 13, 9), (0, 0, 0, 14, 9, 12, 11, 5), (0, 1, 0, 7, 13, 9),
+        (0, 1, 1, 14, 9, 12, 11, 5), (0, 1, 0, 14, 9, 12, 11, 5), (2, 1), (0, 0, 0, 1, 12, 8, 9, 11),
+        (0, 0, 1, 1, 12, 8, 9, 11), (0, 1, 0, 1, 9, 12, 8, 11), (0, 1, 1, 1, 9, 12, 8, 11), (2, 2), (2, 3), (2, 4),
     ),
     (
         (0, 0, 1, 11, 6, 9, 0, 10, 12, 7), (0, 0, 0, 11, 6, 9, 0, 10, 12, 7), (0, 1, 1, 11, 6, 12, 9, 10, 7, 0),
-        (0, 1, 0, 11, 6, 12, 9, 10, 7, 0), (2, 0), (0, 0, 0, 5, 13, 12, 10), (0, 0, 1, 5, 13, 12, 10),
-        (0, 1, 0, 5, 13, 10, 12), (2, 1), (0, 1, 1, 5, 13, 10, 12), (2, 2), (2, 3), (2, 4),
+        (0, 1, 0, 11, 6, 12, 9, 10, 7, 0), (2, 0), (0, 0, 0, 5, 13, 12, 10), (2, 1), (0, 0, 1, 5, 13, 12, 10),
+        (0, 1, 0, 5, 13, 10, 12), (0, 1, 1, 5, 13, 10, 12), (2, 2), (2, 3), (2, 4),
     ),
     (
         (0, 0, 1, 12, 10, 0, 11, 9), (0, 0, 0, 12, 10, 0, 11, 9), (0, 1, 1, 12, 10, 9, 0, 11), (0, 0, 1, 9, 11, 15),
         (0, 1, 0, 12, 10, 9, 0, 11), (0, 0, 0, 9, 11, 15), (0, 0, 0, 8, 14, 0, 13), (0, 0, 1, 8, 14, 0, 13),
-        (0, 1, 1, 9, 11, 15), (0, 1, 0, 9, 11, 15), (0, 1, 0, 8, 0, 14, 13), (2, 0), (0, 1, 1, 8, 0, 14, 13),
+        (0, 1, 1, 9, 11, 15), (2, 0), (0, 1, 0, 9, 11, 15), (0, 1, 0, 8, 0, 14, 13), (0, 1, 1, 8, 0, 14, 13),
         (0, 0, 0, 0, 14, 10, 15, 11), (0, 0, 1, 0, 14, 10, 15, 11), (0, 0, 0, 4, 13, 11, 15, 14),
         (0, 0, 1, 4, 13, 11, 15, 14), (0, 1, 0, 0, 11, 15, 10, 14), (0, 1, 1, 0, 11, 15, 10, 14), (2, 1),
         (0, 1, 0, 4, 11, 14, 13, 15), (0, 1, 1, 4, 11, 14, 13, 15), (2, 2), (2, 3), (2, 4),
@@ -164,16 +164,16 @@
     (
         (0, 0, 1, 13, 11, 12, 0, 14, 10), (0, 0, 0, 13, 11, 12, 0, 14, 10), (0, 1, 1, 13, 0, 12, 11, 14, 10),
         (0, 1, 0, 13, 0, 12, 11, 14, 10), (0, 0, 0, 0, 12, 8), (0, 0, 1, 7, 12, 14, 15, 11), (0, 0, 1, 0, 12, 8),
-        (0, 1, 0, 0, 12, 8), (0, 1, 1, 0, 12, 8), (0, 0, 0, 7, 12, 14, 15, 11), (0, 1, 1, 7, 11, 12, 15, 14), (2, 0),
-        (0, 1, 0, 7, 11, 12, 15, 14), (0, 0, 0, 3, 11, 14, 12, 15), (0, 0, 1, 3, 11, 14, 12, 15), (0, 0, 1, 6, 12),
-        (2, 1), (0, 0, 0, 6, 12), (0, 1, 1, 6, 12), (0, 1, 0, 6, 12), (0, 1, 0, 3, 15, 14, 11, 12), (2, 2),
+        (0, 1, 0, 0, 12, 8), (0, 1, 1, 0, 12, 8), (2, 0), (0, 0, 0, 7, 12, 14, 15, 11), (0, 1, 1, 7, 11, 12, 15, 14),
+        (0, 1, 0, 7, 11, 12, 15, 14), (0, 0, 0, 3, 11, 14, 12, 15), (2, 1), (0, 0, 1, 3, 11, 14, 12, 15),
+        (0, 0, 1, 6, 12), (0, 0, 0, 6, 12), (0, 1, 1, 6, 12), (0, 1, 0, 6, 12), (2, 2), (0, 1, 0, 3, 15, 14, 11, 12),
         (0, 1, 1, 3, 15, 14, 11, 12), (2, 3), (2, 4),
     ),
     (
         (0, 0, 1, 14, 8, 10, 15, 13, 2), (0, 0, 0, 14, 8, 10, 15, 13, 2), (0, 1, 1, 14, 10, 8, 15, 2, 13),
         (0, 1, 0, 14, 10, 8, 15, 2, 13), (0, 0, 0, 2, 9, 13, 15), (0, 0, 1, 2, 9, 13, 15), (0, 0, 0, 1, 15),
-        (0, 0, 1, 1, 15), (0, 1, 0, 2, 15, 9, 13), (0, 1, 1, 2, 15, 9, 13), (0, 0, 1, 6, 13, 10, 15, 11),
-        (0, 1, 0, 1, 15), (2, 0), (0, 0, 0, 6, 13, 10, 15, 11), (0, 1, 1, 1, 15), (0, 1, 1, 6, 10, 13, 11, 15),
+        (0, 0, 1, 1, 15), (0, 1, 0, 2, 15, 9, 13), (0, 1, 1, 2, 15, 9, 13), (2, 0), (0, 0, 1, 6, 13, 10, 15, 11),
+        (0, 1, 0, 1, 15), (0, 0, 0, 6, 13, 10, 15, 11), (0, 1, 1, 1, 15), (0, 1, 1, 6, 10, 13, 11, 15),
         (0, 1, 0, 6, 10, 13, 11, 15), (2, 1), (2, 2), (2, 3), (2, 4),
     ),
     (
@@ -181,7 +181,7 @@
         (0, 1, 0, 15, 2, 14, 11, 13, 12), (0, 0, 1, 9, 14, 0, 13, 1), (0, 0, 0, 9, 14, 0, 13, 1),
         (0, 0, 1, 11, 14, 13), (0, 0, 0, 11, 14, 13), (0, 0, 1, 10, 14, 13), (0, 0, 0, 10, 14, 13),
         (0, 1, 1, 9, 1, 0, 14, 13), (0, 1, 0, 9, 1, 0, 14, 13), (2, 0), (0, 1, 1, 11, 13, 14), (0, 1, 0, 11, 13, 14),
-        (0, 1, 1, 10, 13, 14), (0, 1, 0, 10, 13, 14), (2, 1), (2, 2), (2, 3), (2, 4),
+        (0, 1, 1, 10, 13, 14), (2, 1), (0, 1, 0, 10, 13, 14), (2, 2), (2, 3), (2, 4),
     ),
 )
 
@@ -261,8 +261,7 @@
 
 PLAN_W = (
     ("w_begin",), ("w_route", 0),
-    ("a_got", 2), ("a_got", 1), ("a_got", 3), ("a_got", 0),
-    ("w_piece", 2, 0, 4), ("w_route", 1), ("w_piece", 3, 0, 2), ("w_route", 2), ("w_piece", 3, 2, 2),
+    ("w_rest",), ("w_route", 1), ("w_piece", 3, 0, 2), ("w_route", 2), ("w_piece", 3, 2, 2),
     ("reduced", 2, 0), ("reduced", 2, 1), ("reduced", 2, 3), ("reduced", 2, 2),
     ("reduced", 3, 0), ("reduced", 3, 1), ("reduced", 3, 3), ("reduced", 3, 2),
 )
@@ -409,6 +408,16 @@
                 w_cross(place, core)
         w_sends(place, wave, core, source, targets)
 
+    def w_rows():
+        for gs in (2, 1, 3, 0):
+            a_got(gs)
+        w_piece(2, 0, 4)
+
+    def w_rest():
+        before = sent[0]
+        pl.when(z > 0)(w_rows)
+        sent[0] = before
+
     def w_route(part):
         totals = []
 
@@ -420,13 +429,18 @@
             for step in route[cuts[part] : cuts[part + 1]]:
                 with jax.named_scope("_".join(map(str, ("at", place, *step)))):
                     w_step(place, *step)
+                if place == 0 and step == (2, 2):
+                    extra = sent[0]
+                    w_rows()
+                    w_extra.append(sent[0] - extra)
+                    sent[0] = extra
             totals.append(sent[0] - start)
             sent[0] = start
 
         by_place(z, go_on)
         w_totals.append(totals)
 
-    w_totals = []
+    w_totals, w_extra = [], []
 
     def w_passed(p):
         received(wall.at[pl.ds(4 * p, 4)], wpsem.at[p])
@@ -553,7 +567,7 @@
 
         def greeted(place):
             pl.semaphore_wait(barrier, 2 + len(FIRST[place]) + len(ASIDE[place]) - one_more)
-            for other in range(8):
+            for other in range(16):
                 if (3, place) in ROUTES[other]:
                     to = dev(to_z=other, role=WC)
                     pl.semaphore_signal(late.at[place - 8], inc=1, device_id=to, device_id_type=MESH)
@@ -632,7 +646,7 @@
 
     steps = dict(
         q_begin=q_begin, w_begin=w_begin, q_own=q_own, q_relay=q_relay, q_last=q_last, k_own=k_own, k_relay=k_relay,
-        k_last=k_last, attend=attend, w_route=w_route, w_passed=w_passed, a_got=a_got, piece=piece, w_piece=w_piece, reduced=reduced,
+        k_last=k_last, attend=attend, w_route=w_route, w_passed=w_passed, a_got=a_got, piece=piece, w_piece=w_piece, w_rest=w_rest, reduced=reduced,
         ring=ring, q_own_first=q_own_first, q_own_last=q_own_last,
     )
 
@@ -659,7 +673,7 @@
                 outs.append(pltpu.make_async_copy(rbuf.at[p], sums.at[p], lsem.at[3 + p]))
                 outs[-1].start()
             if mine:
-                by_place(z, lambda place: drain(sent[0] + sum(totals[place] for totals in w_totals)))
+                by_place(z, lambda place: drain(sent[0] + w_extra[0] + sum(totals[place] for totals in w_totals)))
             else:
                 drain(sent[0])
             for copy in outs:

time: 58.8 us -> 57.3 us (0.974)
  Pallas kernels: 57.8 us -> 55.9 us
    pallas_call x1, Pallas kernels: 55.6 us -> 53.6 us  [local(): pl.pallas_call(kernel, out_shape=jax.ShapeDtypeStruct((PIECES, 8, 16, 256...]
where the time goes in v5:
time: 57.3 us; the launch traced here: 56.7 us
  Pallas kernels  55.9 us (98%)
  between operations  0.82 us (1%)
    pallas_call x1, Pallas kernels, local(): pl.pallas_call(kernel, out_shape=jax.ShapeDtypeStruct((PIECES, 8, 16, 256...  53.6 us
    pallas_call x1, Pallas kernels, local(): pl.pallas_call(last_kernel, out_shape=(jax.ShapeDtypeStruct((16, 8192), B...  2.25 us

profile of v5, /device:TPU:1, one launch (start us, length us, event | category | flops | bytes accessed | tf_op | source)
XLA Modules:
  0.0 56.7 jit_solution(485525384156693834)
XLA Ops:
  0.6 53.6 %layer.1.sums = bf16[4,8,16,256]{3,2,1,0:T(8,128)(2,1)} custom-call(bf16[256,256]{1,0:T(8,128)(2,1)} %q.1, bf16[16,512]{1,0:T(8,128)(2,1)} %k.1, bf16[16,512]{1,0:T(8,128)(2,1)} %v.1, bf16[256,128]{1,0:T(8,128)(2,1)} %w.1), custom_call_target="tpu_custom_call" | custom-call | tf_op jit(solution)/shard_map/layer/pallas_call | solution.py:752
  54.2 2.3 %final.1 = (bf16[16,8192]{1,0:T(8,128)(2,1)}, bf16[16,8192]{1,0:T(8,128)(2,1)}) custom-call(bf16[4,8,16,256]{3,2,1,0:T(8,128)(2,1)} %layer.1.sums, bf16[16,8192]{1,0:T(8,128)(2,1)} %res.1, f32[64,128]{1,0:T(8,128)} %bitcast.1), custom_call_target="tpu_custom_call" | custom-call | tf_op jit(solution)/shard_map/final/pallas_call | solution.py:785

commit v6 on v5

--- a/solution.py
+++ b/solution.py
@@ -64,124 +64,124 @@
         (0, 0, 1, 13, 15, 1), (0, 1, 0, 1, 14, 13), (0, 0, 1, 12, 15, 3, 1), (0, 0, 0, 13, 15, 1),
         (0, 1, 1, 1, 14, 13), (0, 0, 0, 12, 15, 3, 1), (2, 0), (0, 0, 1, 11, 15, 1), (0, 0, 0, 11, 15, 1),
         (0, 0, 1, 10, 1, 15), (0, 0, 0, 10, 1, 15), (0, 1, 1, 13, 1, 15), (0, 1, 1, 12, 15, 3, 1),
-        (0, 1, 0, 13, 1, 15), (0, 1, 0, 12, 15, 3, 1), (2, 1), (0, 1, 1, 11, 15, 1), (0, 1, 0, 11, 15, 1),
-        (0, 0, 0, 8, 15, 1), (0, 1, 1, 10, 1, 15), (0, 0, 1, 8, 15, 1), (2, 2), (0, 1, 0, 10, 1, 15),
-        (0, 1, 0, 8, 1, 15), (2, 3), (0, 1, 1, 8, 1, 15), (2, 4),
+        (0, 1, 0, 13, 1, 15), (2, 1), (0, 1, 0, 12, 15, 3, 1), (2, 2), (0, 1, 1, 11, 15, 1), (0, 1, 0, 11, 15, 1),
+        (0, 0, 0, 8, 15, 1), (0, 1, 1, 10, 1, 15), (0, 0, 1, 8, 15, 1), (2, 3), (0, 1, 0, 10, 1, 15),
+        (0, 1, 0, 8, 1, 15), (2, 4), (0, 1, 1, 8, 1, 15), (2, 5),
     ),
     (
         (0, 0, 0, 1, 5, 2), (0, 0, 1, 1, 5, 2), (0, 1, 0, 1, 5, 2), (0, 1, 1, 1, 5, 2), (0, 0, 0, 4, 0, 2, 3),
         (0, 0, 1, 4, 0, 2, 3), (0, 0, 0, 5, 0), (0, 0, 1, 5, 0), (3, 14), (0, 0, 1, 6, 0, 14), (0, 0, 0, 6, 0, 14),
         (0, 1, 0, 4, 2, 0, 3), (0, 1, 1, 4, 2, 0, 3), (2, 0), (0, 1, 0, 5, 0), (0, 0, 1, 13, 4, 2), (0, 1, 1, 5, 0),
-        (0, 0, 0, 13, 4, 2), (0, 1, 1, 6, 0, 14), (0, 0, 1, 11, 2, 3), (0, 1, 0, 6, 0, 14), (0, 0, 0, 11, 2, 3),
-        (2, 1), (0, 1, 1, 13, 4, 2), (0, 1, 0, 13, 4, 2), (0, 1, 1, 11, 3, 2), (2, 2), (0, 1, 0, 11, 3, 2), (2, 3),
-        (2, 4),
+        (2, 1), (0, 0, 0, 13, 4, 2), (0, 1, 1, 6, 0, 14), (0, 0, 1, 11, 2, 3), (0, 1, 0, 6, 0, 14),
+        (0, 0, 0, 11, 2, 3), (2, 2), (0, 1, 1, 13, 4, 2), (0, 1, 0, 13, 4, 2), (0, 1, 1, 11, 3, 2), (2, 3),
+        (0, 1, 0, 11, 3, 2), (2, 4), (2, 5),
     ),
     (
         (0, 0, 0, 2, 0, 4), (0, 0, 1, 2, 0, 4), (0, 0, 0, 1, 6, 3, 0), (0, 0, 1, 1, 6, 3, 0), (0, 1, 0, 2, 4, 0),
         (0, 1, 1, 2, 4, 0), (0, 0, 0, 5, 3, 1), (0, 0, 1, 5, 3, 1), (0, 0, 1, 6, 1, 4), (0, 0, 0, 6, 1, 4),
         (0, 1, 0, 1, 6, 0, 3), (0, 1, 1, 1, 6, 0, 3), (0, 0, 1, 7, 0, 1), (0, 0, 0, 7, 0, 1), (0, 1, 0, 5, 3, 1),
         (0, 1, 1, 5, 3, 1), (2, 0), (0, 0, 1, 15, 1, 3, 0, 4), (0, 0, 0, 15, 1, 3, 0, 4), (0, 0, 1, 14, 4, 0, 1),
-        (0, 1, 1, 6, 4, 1), (0, 1, 0, 6, 4, 1), (0, 0, 0, 14, 4, 0, 1), (0, 1, 1, 7, 1, 0), (0, 1, 0, 7, 1, 0),
-        (2, 1), (0, 1, 1, 15, 0, 4, 3, 1), (0, 1, 0, 15, 0, 4, 3, 1), (0, 1, 1, 14, 1, 0, 4), (0, 1, 0, 14, 1, 0, 4),
-        (2, 2), (2, 3), (2, 4),
+        (0, 1, 1, 6, 4, 1), (0, 1, 0, 6, 4, 1), (2, 1), (0, 0, 0, 14, 4, 0, 1), (0, 1, 1, 7, 1, 0),
+        (0, 1, 0, 7, 1, 0), (2, 2), (0, 1, 1, 15, 0, 4, 3, 1), (0, 1, 0, 15, 0, 4, 3, 1), (0, 1, 1, 14, 1, 0, 4),
+        (0, 1, 0, 14, 1, 0, 4), (2, 3), (2, 4), (2, 5),
     ),
     (
         (0, 0, 0, 3, 4, 6, 2, 0), (0, 0, 1, 3, 4, 6, 2, 0), (0, 1, 0, 3, 4, 2, 0, 6), (0, 1, 1, 3, 4, 2, 0, 6),
         (0, 0, 0, 0, 4), (0, 0, 1, 0, 4), (0, 1, 0, 0, 4), (3, 14), (3, 13), (0, 0, 0, 8, 6, 2), (0, 1, 1, 0, 4),
-        (2, 0), (0, 0, 1, 8, 6, 2), (0, 0, 1, 12, 2, 14, 13, 4), (2, 1), (0, 1, 0, 8, 2, 6),
+        (2, 0), (0, 0, 1, 8, 6, 2), (2, 1), (0, 0, 1, 12, 2, 14, 13, 4), (2, 2), (0, 1, 0, 8, 2, 6),
         (0, 0, 0, 12, 2, 14, 13, 4), (0, 1, 1, 8, 2, 6), (0, 1, 1, 12, 2, 14, 13, 4), (0, 1, 0, 12, 2, 14, 13, 4),
-        (2, 2), (2, 3), (2, 4),
+        (2, 3), (2, 4), (2, 5),
     ),
     (
         (0, 0, 0, 4, 6, 1), (0, 0, 1, 4, 6, 1), (0, 0, 0, 2, 7, 6, 5, 3), (0, 0, 1, 2, 7, 6, 5, 3),
         (0, 1, 0, 4, 1, 6), (0, 1, 1, 4, 1, 6), (0, 1, 0, 2, 5, 3, 6, 7), (0, 1, 1, 2, 5, 3, 6, 7), (3, 15), (3, 14),
-        (0, 0, 1, 9, 3, 5, 2, 6), (0, 0, 0, 9, 3, 5, 2, 6), (0, 0, 1, 15, 5, 7), (2, 0), (0, 0, 0, 15, 5, 7),
-        (0, 1, 1, 9, 5, 6, 2, 3), (0, 0, 1, 14, 7, 6, 3), (0, 1, 0, 9, 5, 6, 2, 3), (2, 1), (0, 0, 0, 14, 7, 6, 3),
+        (0, 0, 1, 9, 3, 5, 2, 6), (0, 0, 0, 9, 3, 5, 2, 6), (0, 0, 1, 15, 5, 7), (2, 0), (0, 0, 0, 15, 5, 7), (2, 1),
+        (0, 1, 1, 9, 5, 6, 2, 3), (0, 0, 1, 14, 7, 6, 3), (0, 1, 0, 9, 5, 6, 2, 3), (2, 2), (0, 0, 0, 14, 7, 6, 3),
         (0, 0, 1, 13, 6, 3, 5), (0, 0, 0, 13, 6, 3, 5), (0, 1, 1, 15, 7, 5), (0, 1, 0, 15, 7, 5),
         (0, 1, 1, 14, 6, 7, 3), (0, 0, 0, 5, 15, 14, 6), (0, 1, 0, 14, 6, 7, 3), (0, 1, 1, 13, 3, 5, 6),
-        (0, 1, 0, 13, 3, 5, 6), (0, 0, 1, 5, 15, 14, 6), (2, 2), (0, 1, 0, 5, 15, 14, 6), (2, 3),
-        (0, 1, 1, 5, 15, 14, 6), (2, 4),
+        (0, 1, 0, 13, 3, 5, 6), (0, 0, 1, 5, 15, 14, 6), (2, 3), (0, 1, 0, 5, 15, 14, 6), (2, 4),
+        (0, 1, 1, 5, 15, 14, 6), (2, 5),
     ),
     (
         (0, 0, 0, 5, 2), (0, 0, 1, 5, 2), (0, 0, 0, 1, 4, 7), (0, 1, 0, 5, 2), (0, 1, 1, 5, 2), (0, 0, 1, 7, 4, 3, 6),
         (0, 0, 1, 1, 4, 7), (0, 0, 0, 7, 4, 3, 6), (3, 8), (1, 0, 0, 5, 8), (1, 0, 1, 5, 8), (1, 1, 0, 5, 8),
         (1, 1, 1, 5, 8), (3, 10), (1, 0, 0, 1, 10), (1, 0, 1, 1, 10), (0, 1, 1, 7, 3, 4, 6), (0, 1, 0, 1, 4, 7, 10),
-        (0, 1, 0, 7, 3, 4, 6), (0, 1, 1, 1, 4, 7, 10), (2, 0), (0, 0, 1, 10, 3, 4, 2), (0, 0, 0, 10, 3, 4, 2),
-        (0, 1, 1, 10, 4, 2, 3), (0, 1, 0, 10, 4, 2, 3), (2, 1), (2, 2), (2, 3), (2, 4),
+        (0, 1, 0, 7, 3, 4, 6), (0, 1, 1, 1, 4, 7, 10), (2, 0), (2, 1), (0, 0, 1, 10, 3, 4, 2), (0, 0, 0, 10, 3, 4, 2),
+        (0, 1, 1, 10, 4, 2, 3), (0, 1, 0, 10, 4, 2, 3), (2, 2), (2, 3), (2, 4), (2, 5),
     ),
     (
         (0, 0, 1, 6, 5, 2, 7), (0, 0, 0, 6, 5, 2, 7), (0, 0, 0, 3, 7), (0, 0, 0, 4, 7, 5), (0, 0, 1, 4, 7, 5),
         (0, 0, 1, 3, 7), (0, 1, 1, 6, 5, 2, 7), (0, 1, 0, 6, 5, 2, 7), (3, 9), (1, 0, 0, 4, 9), (1, 0, 1, 4, 9),
         (3, 8), (1, 0, 0, 3, 8), (1, 0, 1, 3, 8), (0, 1, 0, 3, 7, 8), (0, 1, 0, 4, 5, 7, 9), (0, 1, 1, 4, 5, 7, 9),
         (0, 0, 1, 10, 7, 5), (0, 0, 0, 10, 7, 5), (0, 1, 1, 3, 7, 8), (0, 0, 1, 11, 5, 4, 8), (0, 0, 0, 11, 5, 4, 8),
-        (0, 1, 1, 10, 7, 5), (0, 1, 0, 10, 7, 5), (2, 0), (0, 1, 1, 11, 8, 4, 5), (0, 0, 0, 8, 5, 4, 7),
-        (0, 0, 1, 8, 5, 4, 7), (0, 1, 0, 11, 8, 4, 5), (2, 1), (0, 1, 0, 8, 4, 5, 7), (0, 0, 1, 13, 9, 8, 7),
-        (0, 0, 0, 13, 9, 8, 7), (0, 1, 1, 8, 4, 5, 7), (2, 2), (0, 1, 1, 13, 9, 8, 7), (0, 1, 0, 13, 9, 8, 7), (2, 3),
-        (2, 4),
+        (0, 1, 1, 10, 7, 5), (0, 1, 0, 10, 7, 5), (2, 0), (2, 1), (0, 1, 1, 11, 8, 4, 5), (0, 0, 0, 8, 5, 4, 7),
+        (0, 0, 1, 8, 5, 4, 7), (0, 1, 0, 11, 8, 4, 5), (2, 2), (0, 1, 0, 8, 4, 5, 7), (0, 0, 1, 13, 9, 8, 7),
+        (0, 0, 0, 13, 9, 8, 7), (0, 1, 1, 8, 4, 5, 7), (2, 3), (0, 1, 1, 13, 9, 8, 7), (0, 1, 0, 13, 9, 8, 7), (2, 4),
+        (2, 5),
     ),
     (
         (0, 0, 1, 7, 5, 2), (0, 0, 0, 7, 5, 2), (0, 0, 1, 6, 3), (0, 0, 0, 6, 3), (0, 1, 1, 7, 5, 2), (3, 9),
         (1, 0, 1, 6, 9), (1, 0, 0, 6, 9), (0, 1, 0, 7, 5, 2), (3, 8), (1, 0, 1, 7, 8), (1, 0, 0, 7, 8),
         (1, 0, 1, 6, 8), (1, 0, 0, 6, 8), (1, 1, 1, 7, 8), (1, 1, 0, 7, 8), (3, 10), (1, 0, 1, 7, 10),
         (1, 0, 0, 7, 10), (1, 1, 1, 7, 10), (1, 1, 0, 7, 10), (0, 1, 1, 6, 8, 3, 9), (0, 1, 0, 6, 8, 3, 9), (2, 0),
-        (2, 1), (0, 0, 1, 15, 9, 10, 8, 6), (0, 0, 0, 15, 9, 10, 8, 6), (0, 1, 1, 15, 9, 6, 10, 8),
-        (0, 1, 0, 15, 9, 6, 10, 8), (2, 2), (2, 3), (2, 4),
+        (2, 1), (2, 2), (0, 0, 1, 15, 9, 10, 8, 6), (0, 0, 0, 15, 9, 10, 8, 6), (0, 1, 1, 15, 9, 6, 10, 8),
+        (0, 1, 0, 15, 9, 6, 10, 8), (2, 3), (2, 4), (2, 5),
     ),
     (
         (0, 0, 0, 8, 9, 12, 10, 3, 11), (0, 0, 1, 8, 9, 12, 10, 3, 11), (0, 1, 0, 8, 9, 11, 3, 12, 10),
         (0, 1, 1, 8, 9, 11, 3, 12, 10), (0, 0, 0, 3, 10, 13, 5, 9), (2, 0), (0, 0, 1, 3, 10, 13, 5, 9),
         (0, 0, 0, 5, 11, 4, 9, 7), (0, 0, 1, 5, 11, 4, 9, 7), (0, 1, 0, 5, 7, 11, 9, 4), (0, 1, 0, 3, 13, 9, 5, 10),
-        (0, 1, 1, 5, 7, 11, 9, 4), (0, 1, 1, 3, 13, 9, 5, 10), (2, 1), (0, 0, 0, 0, 6, 7, 9), (0, 0, 1, 0, 6, 7, 9),
-        (0, 1, 0, 0, 9, 7, 6), (0, 1, 1, 0, 9, 7, 6), (2, 2), (2, 3), (2, 4),
+        (0, 1, 1, 5, 7, 11, 9, 4), (2, 1), (0, 1, 1, 3, 13, 9, 5, 10), (2, 2), (0, 0, 0, 0, 6, 7, 9),
+        (0, 0, 1, 0, 6, 7, 9), (0, 1, 0, 0, 9, 7, 6), (0, 1, 1, 0, 9, 7, 6), (2, 3), (2, 4), (2, 5),
     ),
     (
         (0, 0, 1, 9, 7, 8, 10, 4, 12), (0, 0, 0, 9, 7, 8, 10, 4, 12), (0, 1, 1, 9, 4, 7, 8, 12, 10),
         (0, 1, 0, 9, 4, 7, 8, 12, 10), (0, 0, 1, 12, 7, 6, 5, 8), (0, 0, 0, 12, 7, 6, 5, 8), (0, 0, 0, 4, 8, 10, 12),
-        (2, 0), (0, 0, 1, 4, 8, 10, 12), (0, 1, 1, 12, 5, 8, 6, 7), (0, 1, 0, 12, 5, 8, 6, 7),
-        (0, 1, 0, 4, 12, 10, 8), (0, 1, 1, 4, 12, 10, 8), (2, 1), (0, 0, 0, 2, 11, 10, 8, 12),
-        (0, 0, 1, 2, 11, 10, 8, 12), (0, 1, 0, 2, 11, 8, 12, 10), (0, 1, 1, 2, 11, 8, 12, 10), (2, 2), (2, 3), (2, 4),
+        (2, 0), (0, 0, 1, 4, 8, 10, 12), (0, 1, 1, 12, 5, 8, 6, 7), (0, 1, 0, 12, 5, 8, 6, 7), (2, 1),
+        (0, 1, 0, 4, 12, 10, 8), (0, 1, 1, 4, 12, 10, 8), (2, 2), (0, 0, 0, 2, 11, 10, 8, 12),
+        (0, 0, 1, 2, 11, 10, 8, 12), (0, 1, 0, 2, 11, 8, 12, 10), (0, 1, 1, 2, 11, 8, 12, 10), (2, 3), (2, 4), (2, 5),
     ),
     (
         (0, 0, 1, 10, 12, 9, 6, 0, 11, 8), (0, 0, 0, 10, 12, 9, 6, 0, 11, 8), (0, 1, 1, 10, 6, 11, 8, 0, 12, 9),
         (0, 1, 0, 10, 6, 11, 8, 0, 12, 9), (0, 0, 1, 7, 13, 9), (0, 0, 1, 14, 9, 12, 11, 5), (2, 0),
-        (0, 0, 0, 7, 13, 9), (0, 1, 1, 7, 13, 9), (0, 0, 0, 14, 9, 12, 11, 5), (0, 1, 0, 7, 13, 9),
-        (0, 1, 1, 14, 9, 12, 11, 5), (0, 1, 0, 14, 9, 12, 11, 5), (2, 1), (0, 0, 0, 1, 12, 8, 9, 11),
-        (0, 0, 1, 1, 12, 8, 9, 11), (0, 1, 0, 1, 9, 12, 8, 11), (0, 1, 1, 1, 9, 12, 8, 11), (2, 2), (2, 3), (2, 4),
+        (0, 0, 0, 7, 13, 9), (0, 1, 1, 7, 13, 9), (0, 0, 0, 14, 9, 12, 11, 5), (0, 1, 0, 7, 13, 9), (2, 1),
+        (0, 1, 1, 14, 9, 12, 11, 5), (0, 1, 0, 14, 9, 12, 11, 5), (2, 2), (0, 0, 0, 1, 12, 8, 9, 11),
+        (0, 0, 1, 1, 12, 8, 9, 11), (0, 1, 0, 1, 9, 12, 8, 11), (0, 1, 1, 1, 9, 12, 8, 11), (2, 3), (2, 4), (2, 5),
     ),
     (
         (0, 0, 1, 11, 6, 9, 0, 10, 12, 7), (0, 0, 0, 11, 6, 9, 0, 10, 12, 7), (0, 1, 1, 11, 6, 12, 9, 10, 7, 0),
-        (0, 1, 0, 11, 6, 12, 9, 10, 7, 0), (2, 0), (0, 0, 0, 5, 13, 12, 10), (2, 1), (0, 0, 1, 5, 13, 12, 10),
-        (0, 1, 0, 5, 13, 10, 12), (0, 1, 1, 5, 13, 10, 12), (2, 2), (2, 3), (2, 4),
+        (0, 1, 0, 11, 6, 12, 9, 10, 7, 0), (2, 0), (2, 1), (0, 0, 0, 5, 13, 12, 10), (2, 2), (0, 0, 1, 5, 13, 12, 10),
+        (0, 1, 0, 5, 13, 10, 12), (0, 1, 1, 5, 13, 10, 12), (2, 3), (2, 4), (2, 5),
     ),
     (
         (0, 0, 1, 12, 10, 0, 11, 9), (0, 0, 0, 12, 10, 0, 11, 9), (0, 1, 1, 12, 10, 9, 0, 11), (0, 0, 1, 9, 11, 15),
         (0, 1, 0, 12, 10, 9, 0, 11), (0, 0, 0, 9, 11, 15), (0, 0, 0, 8, 14, 0, 13), (0, 0, 1, 8, 14, 0, 13),
-        (0, 1, 1, 9, 11, 15), (2, 0), (0, 1, 0, 9, 11, 15), (0, 1, 0, 8, 0, 14, 13), (0, 1, 1, 8, 0, 14, 13),
+        (0, 1, 1, 9, 11, 15), (2, 0), (0, 1, 0, 9, 11, 15), (0, 1, 0, 8, 0, 14, 13), (0, 1, 1, 8, 0, 14, 13), (2, 1),
         (0, 0, 0, 0, 14, 10, 15, 11), (0, 0, 1, 0, 14, 10, 15, 11), (0, 0, 0, 4, 13, 11, 15, 14),
-        (0, 0, 1, 4, 13, 11, 15, 14), (0, 1, 0, 0, 11, 15, 10, 14), (0, 1, 1, 0, 11, 15, 10, 14), (2, 1),
-        (0, 1, 0, 4, 11, 14, 13, 15), (0, 1, 1, 4, 11, 14, 13, 15), (2, 2), (2, 3), (2, 4),
+        (0, 0, 1, 4, 13, 11, 15, 14), (0, 1, 0, 0, 11, 15, 10, 14), (0, 1, 1, 0, 11, 15, 10, 14), (2, 2),
+        (0, 1, 0, 4, 11, 14, 13, 15), (0, 1, 1, 4, 11, 14, 13, 15), (2, 3), (2, 4), (2, 5),
     ),
     (
         (0, 0, 1, 13, 11, 12, 0, 14, 10), (0, 0, 0, 13, 11, 12, 0, 14, 10), (0, 1, 1, 13, 0, 12, 11, 14, 10),
         (0, 1, 0, 13, 0, 12, 11, 14, 10), (0, 0, 0, 0, 12, 8), (0, 0, 1, 7, 12, 14, 15, 11), (0, 0, 1, 0, 12, 8),
         (0, 1, 0, 0, 12, 8), (0, 1, 1, 0, 12, 8), (2, 0), (0, 0, 0, 7, 12, 14, 15, 11), (0, 1, 1, 7, 11, 12, 15, 14),
-        (0, 1, 0, 7, 11, 12, 15, 14), (0, 0, 0, 3, 11, 14, 12, 15), (2, 1), (0, 0, 1, 3, 11, 14, 12, 15),
-        (0, 0, 1, 6, 12), (0, 0, 0, 6, 12), (0, 1, 1, 6, 12), (0, 1, 0, 6, 12), (2, 2), (0, 1, 0, 3, 15, 14, 11, 12),
-        (0, 1, 1, 3, 15, 14, 11, 12), (2, 3), (2, 4),
+        (0, 1, 0, 7, 11, 12, 15, 14), (2, 1), (0, 0, 0, 3, 11, 14, 12, 15), (2, 2), (0, 0, 1, 3, 11, 14, 12, 15),
+        (0, 0, 1, 6, 12), (0, 0, 0, 6, 12), (0, 1, 1, 6, 12), (0, 1, 0, 6, 12), (2, 3), (0, 1, 0, 3, 15, 14, 11, 12),
+        (0, 1, 1, 3, 15, 14, 11, 12), (2, 4), (2, 5),
     ),
     (
         (0, 0, 1, 14, 8, 10, 15, 13, 2), (0, 0, 0, 14, 8, 10, 15, 13, 2), (0, 1, 1, 14, 10, 8, 15, 2, 13),
         (0, 1, 0, 14, 10, 8, 15, 2, 13), (0, 0, 0, 2, 9, 13, 15), (0, 0, 1, 2, 9, 13, 15), (0, 0, 0, 1, 15),
         (0, 0, 1, 1, 15), (0, 1, 0, 2, 15, 9, 13), (0, 1, 1, 2, 15, 9, 13), (2, 0), (0, 0, 1, 6, 13, 10, 15, 11),
-        (0, 1, 0, 1, 15), (0, 0, 0, 6, 13, 10, 15, 11), (0, 1, 1, 1, 15), (0, 1, 1, 6, 10, 13, 11, 15),
-        (0, 1, 0, 6, 10, 13, 11, 15), (2, 1), (2, 2), (2, 3), (2, 4),
+        (0, 1, 0, 1, 15), (0, 0, 0, 6, 13, 10, 15, 11), (0, 1, 1, 1, 15), (2, 1), (0, 1, 1, 6, 10, 13, 11, 15),
+        (0, 1, 0, 6, 10, 13, 11, 15), (2, 2), (2, 3), (2, 4), (2, 5),
     ),
     (
         (0, 0, 1, 15, 12, 11, 14, 2, 13), (0, 0, 0, 15, 12, 11, 14, 2, 13), (0, 1, 1, 15, 2, 14, 11, 13, 12),
         (0, 1, 0, 15, 2, 14, 11, 13, 12), (0, 0, 1, 9, 14, 0, 13, 1), (0, 0, 0, 9, 14, 0, 13, 1),
         (0, 0, 1, 11, 14, 13), (0, 0, 0, 11, 14, 13), (0, 0, 1, 10, 14, 13), (0, 0, 0, 10, 14, 13),
         (0, 1, 1, 9, 1, 0, 14, 13), (0, 1, 0, 9, 1, 0, 14, 13), (2, 0), (0, 1, 1, 11, 13, 14), (0, 1, 0, 11, 13, 14),
-        (0, 1, 1, 10, 13, 14), (2, 1), (0, 1, 0, 10, 13, 14), (2, 2), (2, 3), (2, 4),
+        (2, 1), (0, 1, 1, 10, 13, 14), (2, 2), (0, 1, 0, 10, 13, 14), (2, 3), (2, 4), (2, 5),
     ),
 )
 
@@ -206,9 +206,9 @@
 
 SLOT = [{source: i for i, source in enumerate(order)} for order in ORDER]
 RELAYS = [[tuple(step[1:4]) for step in route if step[0] == 0 and step[3] != z] for z, route in enumerate(ROUTES)]
-BOUNDS = (0, 4, 8, 12, 14, 16)
+BOUNDS = (0, 4, 6, 8, 12, 14, 16)
 PART = [sum(slot >= bound for bound in BOUNDS[1:]) for slot in range(16)]
-RSEMS = 10 + max(map(len, RELAYS))
+RSEMS = 11 + max(map(len, RELAYS))
 
 
 def leaves(z, p):
@@ -254,7 +254,7 @@
     ("attend", 2), ("attend", 1), ("attend", 3),
     ("w_passed", 0), ("piece", 0, 1),
     ("q_last",), ("k_last",), ("attend", 0), ("piece", 0, 0),
-    ("w_passed", 1), ("piece", 1, 2),
+    ("w_passed", 1), ("w_piece", 1, 0, 2), ("w_passed", 2), ("w_piece", 1, 2, 2),
     ("reduced", 0, 2), ("reduced", 0, 1), ("reduced", 0, 3), ("reduced", 0, 0),
     ("reduced", 1, 2), ("reduced", 1, 1), ("reduced", 1, 3), ("reduced", 1, 0),
 )
@@ -366,7 +366,7 @@
 
     def w_sem(place, wave, core, source):
         if (wave, core, source) in RELAYS[place]:
-            return rsem.at[10 + RELAYS[place].index((wave, core, source))]
+            return rsem.at[11 + RELAYS[place].index((wave, core, source))]
         return rsem.at[5 + PART[SLOT[place][source]]]
 
     def w_sends(place, wave, core, source, targets):
@@ -391,8 +391,8 @@
             p = step[0]
             if leaves(place, p):
                 received(sized(len(leaves(place, p)) * 32768), rsem.at[5 + p])
-            if p < 2:
-                rows = pl.ds(4 * p, 4)
+            if p < 3:
+                rows = pl.ds(BOUNDS[p], BOUNDS[p + 1] - BOUNDS[p])
                 send(wall.at[rows], wall.at[rows], wpsem.at[p], dev(role=QC))
             return
         wave, core, source, *targets = step
@@ -423,13 +423,13 @@
 
         def go_on(place):
             route = ROUTES[place]
-            first = 1 + max(i for i, step in enumerate(route) if step[0] != 2 or step[1] == 2)
-            cuts = (0, first, max(first, 1 + route.index((2, 3))), len(route))
+            first = 1 + max(i for i, step in enumerate(route) if step[0] != 2 or step[1] == 3)
+            cuts = (0, first, max(first, 1 + route.index((2, 4))), len(route))
             start = sent[0]
             for step in route[cuts[part] : cuts[part + 1]]:
                 with jax.named_scope("_".join(map(str, ("at", place, *step)))):
                     w_step(place, *step)
-                if place == 0 and step == (2, 2):
+                if place == 0 and step == (2, 3):
                     extra = sent[0]
                     w_rows()
                     w_extra.append(sent[0] - extra)
@@ -443,7 +443,7 @@
     w_totals, w_extra = [], []
 
     def w_passed(p):
-        received(wall.at[pl.ds(4 * p, 4)], wpsem.at[p])
+        received(wall.at[pl.ds(BOUNDS[p], BOUNDS[p + 1] - BOUNDS[p])], wpsem.at[p])
 
     def q_part(r, s, u):
         return qall.at[r % 4, half_of(r), s, pl.ds(128 * u, 128)]
@@ -621,7 +621,7 @@
         rows = wall[slots].reshape(64 * n, 1024)
         total = lax.dot_general(att[...].reshape(1024, 1024), rows, NT, preferred_element_type=F32)
         lanes = slice(64 * slot, 64 * (slot + n))
-        psend[p - 2, :, :, :, :, lanes] = total.astype(BF16).reshape(4, 2, 4, 32, 64 * n)
+        psend[p % 2, :, :, :, :, lanes] = total.astype(BF16).reshape(4, 2, 4, 32, 64 * n)
         for gs in (0, 1, 3, 2):
             spread(p, gs, pl.ds(64 * slot, 64 * n))
 
@@ -772,7 +772,7 @@
             dma((3 + PIECES,)),
             dma((1,)),
             dma((max(40, RSEMS),)),
-            dma((2,)),
+            dma((3,)),
             dma((4,)),
             dma((2, 4)),
             dma((6,)),

time: 57.3 us -> 57.1 us (level)
  no operation moved by 1% of the time
where the time goes in v6:
time: 57.1 us; the launch traced here: 56.9 us
  Pallas kernels  56 us (98%)
  between operations  0.82 us (1%)
    pallas_call x1, Pallas kernels, local(): pl.pallas_call(kernel, out_shape=jax.ShapeDtypeStruct((PIECES, 8, 16, 256...  53.8 us
    pallas_call x1, Pallas kernels, local(): pl.pallas_call(last_kernel, out_shape=(jax.ShapeDtypeStruct((16, 8192), B...  2.25 us

profile of v6, /device:TPU:1, one launch (start us, length us, event | category | flops | bytes accessed | tf_op | source)
XLA Modules:
  0.0 56.9 jit_solution(11743891866309949840)
XLA Ops:
  0.6 53.8 %layer.1.sums = bf16[4,8,16,256]{3,2,1,0:T(8,128)(2,1)} custom-call(bf16[256,256]{1,0:T(8,128)(2,1)} %q.1, bf16[16,512]{1,0:T(8,128)(2,1)} %k.1, bf16[16,512]{1,0:T(8,128)(2,1)} %v.1, bf16[256,128]{1,0:T(8,128)(2,1)} %w.1), custom_call_target="tpu_custom_call" | custom-call | tf_op jit(solution)/shard_map/layer/pallas_call | solution.py:752
  54.4 2.3 %final.1 = (bf16[16,8192]{1,0:T(8,128)(2,1)}, bf16[16,8192]{1,0:T(8,128)(2,1)}) custom-call(bf16[4,8,16,256]{3,2,1,0:T(8,128)(2,1)} %layer.1.sums, bf16[16,8192]{1,0:T(8,128)(2,1)} %res.1, f32[64,128]{1,0:T(8,128)} %bitcast.1), custom_call_target="tpu_custom_call" | custom-call | tf_op jit(solution)/shard_map/final/pallas_call | solution.py:785
